TPU v7x, 32 devices: a whole 2x2x4 slice. The times are simulated.
32 devices in a mesh: dp: 4 (over x, core), fsdp: 8 (over z, y).
Axes of the slice: x: 2, y: 2, z: 4, core: 2. Of those that a mesh axis runs over, the one named last changes fastest.
Arguments:
- tokens: bfloat16 [16384, 768], P(('dp', 'fsdp')), may hold values from -6 to 6
- lengths: int32 [32, 6], P(('dp', 'fsdp')), may hold values from 1 to 128, 256 in all within a row
- norm1_gain: bfloat16 [768], P('fsdp'), may hold values from 0.25 to 1.75
- norm1_bias: bfloat16 [768], P('fsdp'), may hold values from -1.75 to 1.75
- query_weight: bfloat16 [768, 768], P('fsdp'), may hold values from -0.21875 to 0.21875
- key_weight: bfloat16 [768, 768], P('fsdp'), may hold values from -0.21875 to 0.21875
- value_weight: bfloat16 [768, 768], P('fsdp'), may hold values from -0.21875 to 0.21875
- output_weight: bfloat16 [768, 768], P('fsdp'), may hold values from -0.625 to 0.625
- norm2_gain: bfloat16 [768], P('fsdp'), may hold values from 0.25 to 1.75
- norm2_bias: bfloat16 [768], P('fsdp'), may hold values from -1.75 to 1.75
- up_weight: bfloat16 [768, 3072], P('fsdp'), may hold values from -0.21875 to 0.21875
- up_bias: bfloat16 [3072], P('fsdp'), may hold values from -3 to 3
- down_weight: bfloat16 [3072, 768], P('fsdp'), may hold values from -0.109375 to 0.109375
- down_bias: bfloat16 [768], P('fsdp'), may hold values from -1.75 to 1.75
- cotangent: bfloat16 [16384, 768], P(('dp', 'fsdp')), may hold values from -6 to 6
Outputs:
- output: bfloat16 [16384, 768], P(('dp', 'fsdp'))
- input_grad: float32 [16384, 768], P(('dp', 'fsdp'))
- norm1_gain_grad: float32 [768], P('fsdp')
- norm1_bias_grad: float32 [768], P('fsdp')
- query_weight_grad: float32 [768, 768], P('fsdp')
- key_weight_grad: float32 [768, 768], P('fsdp')
- value_weight_grad: float32 [768, 768], P('fsdp')
- output_weight_grad: float32 [768, 768], P('fsdp')
- norm2_gain_grad: float32 [768], P('fsdp')
- norm2_bias_grad: float32 [768], P('fsdp')
- up_weight_grad: float32 [768, 3072], P('fsdp')
- up_bias_grad: float32 [3072], P('fsdp')
- down_weight_grad: float32 [3072, 768], P('fsdp')
- down_bias_grad: float32 [768], P('fsdp')
Inputs may be any that keep to these rules, and one draw needn't show every extreme that they name: Each row of lengths sums to 256, and its largest entry equals 128.
All inputs are finite; a program needn't handle non-finite values.
Results may differ from a plain program's by a relative error of at most 0.012.
Values may be sent and summed in bfloat16 or wider, within the bound.
No kernel may reach another device: no remote copies, remote signals or barrier semaphores. Data moves between devices by JAX's collectives and lax.ppermute only.
A program may use at most 192 MiB of HBM per device.

v0:
```python
from functools import partial
import math

import jax
import jax.numpy as jnp
from jax import lax
from jax.sharding import PartitionSpec as P

H = 12
HD = 64
BLOCK = 16


EPSILON = 1e-05
BASE = 10000.0
NEGATIVE = -1e30


def layer_norm(values, gain, shift):
    center = values - jnp.mean(values, axis=-1, keepdims=True)
    spread = jnp.mean(center * center, axis=-1, keepdims=True)
    return center * lax.rsqrt(spread + EPSILON) * gain + shift


def row_layout(length_row, row_count, slot_count):
    doubled = 2 * length_row
    ends_at = jnp.cumsum(doubled, dtype=jnp.int32)
    starts_at = ends_at - doubled
    row_index = jnp.arange(row_count, dtype=jnp.int32)
    member = (row_index[:, None] >= starts_at[None, :]) & (row_index[:, None] < ends_at[None, :])
    slot_ids = jnp.arange(slot_count, dtype=jnp.int32)
    slot_index = jnp.sum(jnp.where(member, slot_ids[None, :], 0), axis=1, dtype=jnp.int32)
    start_row = jnp.sum(jnp.where(member, starts_at[None, :], 0), axis=1, dtype=jnp.int32)
    seq_length = jnp.sum(jnp.where(member, length_row[None, :], 0), axis=1, dtype=jnp.int32)
    local_row = row_index - start_row
    clean_flag = (local_row >= seq_length).astype(jnp.int32)
    position = local_row - clean_flag * seq_length
    return (row_index, slot_index, clean_flag, position)


def allowed_pairs(query_side, key_side, block_size, slot_count):
    query_row, query_slot, query_clean, query_pos = query_side
    key_row, key_slot, key_clean, key_pos = key_side
    query_block = query_pos // block_size
    key_block = key_pos // block_size
    same_seq = query_slot[:, None] == key_slot[None, :]
    key_noisy = key_clean[None, :] == 0
    key_plain = key_clean[None, :] == 1
    noisy_rule = key_noisy & (key_block[None, :] == query_block[:, None]) | key_plain & (
        key_block[None, :] < query_block[:, None]
    )
    clean_rule = key_plain & (key_block[None, :] <= query_block[:, None])
    rule_held = jnp.where(query_clean[:, None] == 1, clean_rule, noisy_rule)
    padded = query_slot == slot_count - 1
    real_pairs = same_seq & rule_held & jnp.logical_not(padded)[:, None]
    self_pairs = padded[:, None] & (query_row[:, None] == key_row[None, :])
    return real_pairs | self_pairs


def rotary_tables(position, head_dim):
    half_dim = head_dim // 2
    freqs = jnp.exp(jnp.arange(half_dim, dtype=jnp.float32) * (-2.0 * math.log(BASE) / head_dim))
    angles = position.astype(jnp.float32)[:, None] * freqs[None, :]
    return (jnp.cos(angles)[:, None, :], jnp.sin(angles)[:, None, :])


def rotate(values, cosine, sine):
    half_dim = values.shape[-1] // 2
    first = values[..., :half_dim]
    second = values[..., half_dim:]
    return jnp.concatenate(
        [first * cosine - second * sine, second * cosine + first * sine], axis=-1
    )


def unrotate(grads_in, cosine, sine):
    half_dim = grads_in.shape[-1] // 2
    first = grads_in[..., :half_dim]
    second = grads_in[..., half_dim:]
    return jnp.concatenate(
        [first * cosine + second * sine, second * cosine - first * sine], axis=-1
    )


def in_blocks(source, count):
    return source.reshape((count, source.shape[0] // count) + source.shape[1:])


def matmul_low(left, right):
    return jnp.dot(left, right, preferred_element_type=jnp.float32)


def weight_grad(left, right):
    return jnp.einsum("ri,rj->ij", left, right, preferred_element_type=jnp.float32)


def back_through(grad_rows, weight):
    return jnp.einsum("rj,ij->ri", grad_rows, weight, preferred_element_type=jnp.float32)


def local(
    tokens,
    lengths,
    norm1_gain,
    norm1_bias,
    query_weight,
    key_weight,
    value_weight,
    output_weight,
    norm2_gain,
    norm2_bias,
    up_weight,
    up_bias,
    down_weight,
    down_bias,
    cotangent,
):
    row_count = tokens.shape[0]
    width = tokens.shape[1]
    slot_count = lengths.shape[1]
    heads_split = (row_count, H, HD)
    score_scale = HD ** (-0.5)
    query_rows = min(512, row_count)
    block_count = row_count // query_rows
    layout = row_layout(lengths[0], row_count, slot_count)
    cosine, sine = rotary_tables(layout[3], HD)
    block_layout = tuple((in_blocks(part_item, block_count) for part_item in layout))
    gathered = (
        lax.all_gather(norm1_gain, "fsdp", axis=0, tiled=True),
        lax.all_gather(norm1_bias, "fsdp", axis=0, tiled=True),
        lax.all_gather(query_weight, "fsdp", axis=0, tiled=True),
        lax.all_gather(key_weight, "fsdp", axis=0, tiled=True),
        lax.all_gather(value_weight, "fsdp", axis=0, tiled=True),
        lax.all_gather(output_weight, "fsdp", axis=0, tiled=True),
        lax.all_gather(norm2_gain, "fsdp", axis=0, tiled=True),
        lax.all_gather(norm2_bias, "fsdp", axis=0, tiled=True),
        lax.all_gather(up_weight, "fsdp", axis=0, tiled=True),
        lax.all_gather(up_bias, "fsdp", axis=0, tiled=True),
        lax.all_gather(down_weight, "fsdp", axis=0, tiled=True),
        lax.all_gather(down_bias, "fsdp", axis=0, tiled=True),
    )
    (
        first_gain,
        first_shift,
        query_full,
        key_full,
        value_full,
        output_full,
        second_gain,
        second_shift,
        up_full,
        up_shift,
        down_full,
        down_shift,
    ) = gathered
    inputs = tokens.astype(jnp.float32)
    normed_f, first_pull = jax.vjp(
        layer_norm, inputs, first_gain.astype(jnp.float32), first_shift.astype(jnp.float32)
    )
    normed = normed_f.astype(jnp.bfloat16)
    queries = rotate(matmul_low(normed, query_full).reshape(heads_split), cosine, sine).astype(
        jnp.bfloat16
    )
    key_rows = rotate(matmul_low(normed, key_full).reshape(heads_split), cosine, sine).astype(
        jnp.bfloat16
    )
    value_rows = matmul_low(normed, value_full).astype(jnp.bfloat16).reshape(heads_split)

    def attend(block_item):
        query_block = block_item[0]
        allowed = allowed_pairs(block_item[1:], layout, BLOCK, slot_count)
        raw_scores = jnp.einsum(
            "qhd,khd->hqk", query_block, key_rows, preferred_element_type=jnp.float32
        )
        scores = jnp.where(allowed[None], raw_scores * score_scale, NEGATIVE)
        row_max = jnp.max(scores, axis=2, keepdims=True)
        exponent = jnp.exp(scores - row_max)
        total_sum = jnp.sum(exponent, axis=2, keepdims=True)
        probs = (exponent / total_sum).astype(jnp.bfloat16)
        mixed_block = jnp.einsum(
            "hqk,khd->qhd", probs, value_rows, preferred_element_type=jnp.float32
        )
        return (mixed_block.astype(jnp.bfloat16), row_max + jnp.log(total_sum))

    mixed_blocks, log_totals = lax.map(attend, (in_blocks(queries, block_count),) + block_layout)
    mixed = mixed_blocks.reshape(row_count, width)
    residual = inputs + matmul_low(mixed, output_full)
    hidden_f, second_pull = jax.vjp(
        layer_norm, residual, second_gain.astype(jnp.float32), second_shift.astype(jnp.float32)
    )
    hidden_in = hidden_f.astype(jnp.bfloat16)
    pre_act = matmul_low(hidden_in, up_full) + up_shift.astype(jnp.float32)
    activated_f, gelu_pull = jax.vjp(partial(jax.nn.gelu, approximate=True), pre_act)
    activated = activated_f.astype(jnp.bfloat16)
    result = residual + matmul_low(activated, down_full) + down_shift.astype(jnp.float32)
    output = result.astype(jnp.bfloat16)
    regathered = (
        lax.all_gather(query_weight, "fsdp", axis=0, tiled=True),
        lax.all_gather(key_weight, "fsdp", axis=0, tiled=True),
        lax.all_gather(value_weight, "fsdp", axis=0, tiled=True),
        lax.all_gather(output_weight, "fsdp", axis=0, tiled=True),
        lax.all_gather(up_weight, "fsdp", axis=0, tiled=True),
        lax.all_gather(down_weight, "fsdp", axis=0, tiled=True),
    )
    query_back, key_back, value_back, output_back, up_back, down_back = regathered
    upstream = cotangent.astype(jnp.float32)
    down_bias_grad = jnp.sum(upstream, axis=0)
    down_weight_grad = weight_grad(activated, cotangent)
    act_grad = back_through(cotangent, down_back)
    pre_grad = gelu_pull(act_grad)[0].astype(jnp.bfloat16)
    up_bias_grad = jnp.sum(pre_grad.astype(jnp.float32), axis=0)
    up_weight_grad = weight_grad(hidden_in, pre_grad)
    hidden_grad = back_through(pre_grad, up_back)
    residual_part, norm2_gain_grad, norm2_bias_grad = second_pull(hidden_grad)
    residual_grad = upstream + residual_part
    branch_grad = residual_grad.astype(jnp.bfloat16)
    output_weight_grad = weight_grad(mixed, branch_grad)
    mixed_grad = back_through(branch_grad, output_back).astype(jnp.bfloat16).reshape(heads_split)

    def attend_back(running, block_item):
        key_acc, value_acc = running
        query_block, grad_block, log_total = (block_item[0], block_item[1], block_item[2])
        allowed = allowed_pairs(block_item[3:], layout, BLOCK, slot_count)
        raw_scores = jnp.einsum(
            "qhd,khd->hqk", query_block, key_rows, preferred_element_type=jnp.float32
        )
        scores = jnp.where(allowed[None], raw_scores * score_scale, NEGATIVE)
        probs = jnp.exp(scores - log_total)
        prob_grad = jnp.einsum(
            "qhd,khd->hqk", grad_block, value_rows, preferred_element_type=jnp.float32
        )
        inner_sum = jnp.sum(probs * prob_grad, axis=2, keepdims=True)
        score_grad = (score_scale * (probs * (prob_grad - inner_sum))).astype(jnp.bfloat16)
        query_part = jnp.einsum(
            "hqk,khd->qhd", score_grad, key_rows, preferred_element_type=jnp.float32
        )
        key_acc = key_acc + jnp.einsum(
            "hqk,qhd->khd", score_grad, query_block, preferred_element_type=jnp.float32
        )
        value_acc = value_acc + jnp.einsum(
            "hqk,qhd->khd",
            probs.astype(jnp.bfloat16),
            grad_block,
            preferred_element_type=jnp.float32,
        )
        return ((key_acc, value_acc), query_part)

    zero_heads = jnp.zeros(heads_split, jnp.float32)
    (key_acc, value_acc), query_parts = lax.scan(
        attend_back,
        (zero_heads, zero_heads),
        (in_blocks(queries, block_count), in_blocks(mixed_grad, block_count), log_totals)
        + block_layout,
    )
    query_grad = (
        unrotate(query_parts.reshape(heads_split), cosine, sine)
        .reshape(row_count, width)
        .astype(jnp.bfloat16)
    )
    key_grad = unrotate(key_acc, cosine, sine).reshape(row_count, width).astype(jnp.bfloat16)
    value_grad = value_acc.reshape(row_count, width).astype(jnp.bfloat16)
    query_weight_grad = weight_grad(normed, query_grad)
    key_weight_grad = weight_grad(normed, key_grad)
    value_weight_grad = weight_grad(normed, value_grad)
    normed_grad = (
        back_through(query_grad, query_back)
        + back_through(key_grad, key_back)
        + back_through(value_grad, value_back)
    )
    input_part, norm1_gain_grad, norm1_bias_grad = first_pull(normed_grad)
    input_grad = residual_grad + input_part
    grad_shards = (
        lax.psum_scatter(norm1_gain_grad, "fsdp", scatter_dimension=0, tiled=True),
        lax.psum_scatter(norm1_bias_grad, "fsdp", scatter_dimension=0, tiled=True),
        lax.psum_scatter(query_weight_grad, "fsdp", scatter_dimension=0, tiled=True),
        lax.psum_scatter(key_weight_grad, "fsdp", scatter_dimension=0, tiled=True),
        lax.psum_scatter(value_weight_grad, "fsdp", scatter_dimension=0, tiled=True),
        lax.psum_scatter(output_weight_grad, "fsdp", scatter_dimension=0, tiled=True),
        lax.psum_scatter(norm2_gain_grad, "fsdp", scatter_dimension=0, tiled=True),
        lax.psum_scatter(norm2_bias_grad, "fsdp", scatter_dimension=0, tiled=True),
        lax.psum_scatter(up_weight_grad, "fsdp", scatter_dimension=0, tiled=True),
        lax.psum_scatter(up_bias_grad, "fsdp", scatter_dimension=0, tiled=True),
        lax.psum_scatter(down_weight_grad, "fsdp", scatter_dimension=0, tiled=True),
        lax.psum_scatter(down_bias_grad, "fsdp", scatter_dimension=0, tiled=True),
    )
    final_grads = lax.psum(
        (
            grad_shards[0],
            grad_shards[1],
            grad_shards[2],
            grad_shards[3],
            grad_shards[4],
            grad_shards[5],
            grad_shards[6],
            grad_shards[7],
            grad_shards[8],
            grad_shards[9],
            grad_shards[10],
            grad_shards[11],
        ),
        "dp",
    )
    return (
        output,
        input_grad,
        final_grads[0],
        final_grads[1],
        final_grads[2],
        final_grads[3],
        final_grads[4],
        final_grads[5],
        final_grads[6],
        final_grads[7],
        final_grads[8],
        final_grads[9],
        final_grads[10],
        final_grads[11],
    )


def solution(mesh):
    in_specs = (
        P(("dp", "fsdp"), None),
        P(("dp", "fsdp"), None),
        P("fsdp"),
        P("fsdp"),
        P("fsdp", None),
        P("fsdp", None),
        P("fsdp", None),
        P("fsdp", None),
        P("fsdp"),
        P("fsdp"),
        P("fsdp", None),
        P("fsdp"),
        P("fsdp", None),
        P("fsdp"),
        P(("dp", "fsdp"), None),
    )
    out_specs = (
        P(("dp", "fsdp"), None),
        P(("dp", "fsdp"), None),
        P("fsdp"),
        P("fsdp"),
        P("fsdp", None),
        P("fsdp", None),
        P("fsdp", None),
        P("fsdp", None),
        P("fsdp"),
        P("fsdp"),
        P("fsdp", None),
        P("fsdp"),
        P("fsdp", None),
        P("fsdp"),
    )
    return jax.shard_map(local, mesh=mesh, in_specs=in_specs, out_specs=out_specs, check_vma=False)
```

profile of v0, /device:TPU:0, one launch (start us, length us, event | category | flops | bytes accessed | tf_op | source)
XLA Modules:
  0.0 1065.1 jit_solution(10605085145220299724)
XLA Ops:
  14.1 39.6 %all-reduce.14 = (bf16[768]{0:T(1024)(128)(2,1)S(1)}, bf16[768]{0:T(1024)(128)(2,1)S(1)}, bf16[768]{0:T(1024)(128)(2,1)}, bf16[768]{0:T(1024)(128)(2,1)S(1)}, bf16[768]{0:T(1024)(128)(2,1)S(1)}) all-reduce(bf16[768]{0:T(1024)(128)(2,1)S(1)} %dynamic-update-slice.1, ...), channel_id=1, replica_groups=mesh['dp'=4,'fsdp'=8] {'fsdp'}, use_global_device_ids=true, to_apply=%add.1 | all-reduce | flops 3840 | bytes 15360
  54.9 26.0 %all-gather = bf16[8,1,384]{2,1,0:T(2,128)(2,1)S(1)} all-gather(bf16[1,1,384]{2,1,0:T(2,128)(2,1)S(1)} %reshape.525), channel_id=1, replica_groups=mesh['dp'=4,'fsdp'=8] {'fsdp'}, dimensions={0}, use_global_device_ids=true | all-gather | bytes 6912 | tf_op jit(solution)/shard_map/all_gather | solution.py:138
  83.0 2.3 fusion.62
  85.4 2.2 convolution_convert_fusion.1
  87.9 8.3 all-gather.10.cloned.1.call-done
  96.2 2.3 fusion.102
  98.4 39.8 %all-gather.12.cloned.1.call-done = bf16[768,768]{1,0:T(8,128)(2,1)} async-done(((bf16[96,768]{1,0:T(8,128)(2,1)}), bf16[768,768]{1,0:T(8,128)(2,1)}) %all-gather.12.cloned.1.call-update) | async-done | bytes 1179664 | tf_op jit(solution)/shard_map/all_gather | solution.py:132
  138.2 2.3 fusion.100
  141.0 2.1 fusion.3
  143.2 2.6 fusion.2
  145.8 1.9 copy-done.2
  148.0 4.3 fusion.60
  152.3 27.6 %all-gather.14.cloned.1.call-done = bf16[768,768]{1,0:T(8,128)(2,1)} async-done(((bf16[96,768]{1,0:T(8,128)(2,1)}), bf16[768,768]{1,0:T(8,128)(2,1)}) %all-gather.14.cloned.1.call-update) | async-done | bytes 1179664 | tf_op jit(solution)/shard_map/all_gather | solution.py:134
  179.9 2.4 fusion.111
  184.0 76.0 %all-gather.16.cloned.1.call-done = bf16[768,3072]{1,0:T(8,128)(2,1)} async-done(((bf16[96,3072]{1,0:T(8,128)(2,1)}), bf16[768,3072]{1,0:T(8,128)(2,1)}) %all-gather.16.cloned.1.call-update) | async-done | bytes 4718608 | tf_op jit(solution)/shard_map/all_gather | solution.py:137
  259.9 7.4 fusion.92
  267.4 72.3 %all-gather.18.cloned.1.call-done = bf16[3072,768]{1,0:T(8,128)(2,1)} async-done(((bf16[384,768]{1,0:T(8,128)(2,1)}), bf16[3072,768]{1,0:T(8,128)(2,1)}) %all-gather.18.cloned.1.call-update) | async-done | bytes 4718608 | tf_op jit(solution)/shard_map/all_gather | solution.py:139
  339.7 9.9 convert_reduce_fusion
  349.6 3.5 multiply_reduce_fusion.1
  353.1 2.1 fusion.107
  356.7 2.2 fusion.115
  360.3 3.2 convolution_convert_fusion
  363.5 2.4 copy.61
  365.9 7.8 fusion.57
  374.6 2.5 fusion.94
  377.4 7.5 fusion.112
  384.9 21.1 %fusion.51 = f32[512,12,64]{0,2,1:T(8,128)} fusion(f32[12,512,512]{1,2,0:T(8,128)} %fusion.112, f32[12,512,512]{1,2,0:T(8,128)} %copy-done.2, f32[12,512]{1,0:T(8,128)} %log_add_fusion, pred[512,512]{0,1:T(8,128)(4,1)S(1)} %fusion.62, bf16[512,12,32]{0,2,1:T(8,128)(2,1)} %copy-done.20, bf16[512,12,32]{0,2,1:T(8,128)(2,1)} %copy-done.21), kind=kOutput, calls=%fused_computation.60 | convolution fusion | flops 438835712 | bytes 27811840 | tf_op jit(solution)/shard_map/while/body/eval_jaxpr/hqk,khd->qhd/dot_general | solution.py:234
  406.0 20.8 %fusion.54 = f32[512,12,64]{0,2,1:T(8,128)} fusion(f32[12,512,512]{1,2,0:T(8,128)} %fusion.112, f32[12,512,512]{1,2,0:T(8,128)} %copy-done.2, f32[12,512]{1,0:T(8,128)} %log_add_fusion, pred[512,512]{0,1:T(8,128)(4,1)S(1)} %fusion.62, bf16[512,12,32]{0,2,1:T(8,128)(2,1)S(1)} %copy-done.19, bf16[512,12,32]{0,2,1:T(8,128)(2,1)S(1)} %copy-done.17), kind=kOutput, calls=%fused_computation.61 | convolution fusion | flops 438835712 | bytes 27811840 | tf_op jit(solution)/shard_map/while/body/eval_jaxpr/hqk,qhd->khd/dot_general | solution.py:237
  426.8 2.4 add_convert_fusion.2
  430.1 2.5 fusion.98
  434.0 2.5 fusion.96
  437.7 10.1 fusion.93
  448.4 8.9 fusion.91
  458.8 2.5 fusion.114
  462.8 2.3 fusion.105
  465.1 34.2 %reduce-scatter.11.cloned.1.call-done = f32[96,768]{1,0:T(8,128)} async-done(((f32[768,768]{1,0:T(8,128)}), f32[96,768]{1,0:T(8,128)}) %reduce-scatter.11.cloned.1.call-update) | async-done | bytes 294928 | tf_op jit(solution)/shard_map/reduce_scatter | solution.py:277
  499.4 72.3 %reduce-scatter.7.cloned.1.call-done = f32[96,768]{1,0:T(8,128)} async-done(((f32[768,768]{1,0:T(8,128)}), f32[96,768]{1,0:T(8,128)}) %reduce-scatter.7.cloned.1.call-update) | async-done | bytes 294928 | tf_op jit(solution)/shard_map/reduce_scatter | solution.py:275
  571.7 72.2 %reduce-scatter.9.cloned.1.call-done = f32[96,768]{1,0:T(8,128)} async-done(((f32[768,768]{1,0:T(8,128)}), f32[96,768]{1,0:T(8,128)}) %reduce-scatter.9.cloned.1.call-update) | async-done | bytes 294928 | tf_op jit(solution)/shard_map/reduce_scatter | solution.py:276
  643.9 165.0 %reduce-scatter.17.cloned.1.call-done = f32[384,768]{1,0:T(8,128)} async-done(((f32[3072,768]{1,0:T(8,128)}), f32[384,768]{1,0:T(8,128)}) %reduce-scatter.17.cloned.1.call-update) | async-done | bytes 1179664 | tf_op jit(solution)/shard_map/reduce_scatter | solution.py:283
  808.8 164.7 %reduce-scatter.15.cloned.1.call-done = f32[96,3072]{1,0:T(8,128)} async-done(((f32[768,3072]{1,0:T(8,128)}), f32[96,3072]{1,0:T(8,128)}) %reduce-scatter.15.cloned.1.call-update) | async-done | bytes 1179664 | tf_op jit(solution)/shard_map/reduce_scatter | solution.py:281
  973.6 2.3 fusion.48
  975.9 1.9 convert_reduce_fusion.2
  977.8 35.6 %all-reduce.11 = (f32[768]{0:T(1024)S(1)}, f32[768]{0:T(1024)S(1)}, f32[768]{0:T(1024)S(1)}, f32[768]{0:T(1024)S(1)}, f32[3072]{0:T(1024)S(1)}, /*index=5*/f32[768]{0:T(1024)S(1)}) all-reduce(f32[768]{0:T(1024)S(1)} %get-tuple-element.92, f32[768]{0:T(1024)S(1)} %get-tuple-element.95, ...), channel_id=2, replica_groups=mesh['dp'=4,'fsdp'=8] {'fsdp'}, use_global_device_ids=true, to_apply=%region_16.17.clone | all-reduce | flops 6912 | bytes 55296
  1013.9 6.3 all-reduce.12
  1020.2 9.8 add_convert_fusion
  1030.0 20.4 %all-reduce.17.cloned.1.call-done = (f32[96,768]{1,0:T(8,128)}, f32[96,768]{1,0:T(8,128)}, f32[96,768]{1,0:T(8,128)}, f32[96,768]{1,0:T(8,128)}, f32[96,3072]{1,0:T(8,128)}, /*index=5*/f32[384,768]{1,0:T(8,128)}) async-done(((f32[96,768]{1,0:T(8,128)}, f32[96,768]{1,0:T(8,128)}, f32[96,768]{1,0:T(8,128)}, f32[96,768]{1,0:T(8,128)}, f32[96,3072]{1,0:T(8,128)}, /*index=5*/f32[384,768]{1,0:T(8,128)}), ...) | async-done | bytes 3538960 | tf_op jit(solution)/shard_map/psum | solution.py:286
  1050.4 1.8 copy.82
  1052.2 1.7 copy.83
  (192 shorter events, 26.8 us)
Async XLA Ops:
  7.2 4.5 copy-start.44
  7.2 4.1 copy-start.46
  7.2 4.4 copy-start.45
  7.2 5.7 copy-start.49
  7.2 5.9 copy-start.50
  7.2 6.2 copy-start.51
  7.2 6.4 copy-start.52
  7.3 6.6 copy-start.53
  7.3 74.3 %copy-start = (bf16[512,768]{1,0:T(8,128)(2,1)S(1)}, bf16[512,768]{1,0:T(8,128)(2,1)}, u32[]{:S(2)}) copy-start(bf16[512,768]{1,0:T(8,128)(2,1)} %param.15) | copy-start | bytes 2359300
  7.3 78.1 %all-gather.8.cloned.1.call-start = ((), (), s32[]{:S(2)}) async-start(), calls=%async_computation.6 | async-start | bytes 1327104 | tf_op jit(solution)/shard_map/all_gather | solution.py:133
  8.0 88.2 %all-gather.10.cloned.1.call-start = ((), (), s32[]{:S(2)}) async-start(), calls=%async_computation.7 | async-start | bytes 1327104 | tf_op jit(solution)/shard_map/all_gather | solution.py:131
  8.8 129.4 %all-gather.12.cloned.1.call-start = ((), (), s32[]{:S(2)}) async-start(), calls=%async_computation.8 | async-start | bytes 1327104 | tf_op jit(solution)/shard_map/all_gather | solution.py:132
  9.5 170.4 %all-gather.14.cloned.1.call-start = ((), (), s32[]{:S(2)}) async-start(), calls=%async_computation.9 | async-start | bytes 1327104 | tf_op jit(solution)/shard_map/all_gather | solution.py:134
  10.1 249.9 %all-gather.16.cloned.1.call-start = ((), (), s32[]{:S(2)}) async-start(), calls=%async_computation.10 | async-start | bytes 5308416 | tf_op jit(solution)/shard_map/all_gather | solution.py:137
  10.7 329.0 %all-gather.18.cloned.1.call-start = ((), (), s32[]{:S(2)}) async-start(), calls=%async_computation.11 | async-start | bytes 5308416 | tf_op jit(solution)/shard_map/all_gather | solution.py:139
  11.2 453.9 %reduce-scatter.13.cloned.1.call-start = ((), (), s32[]{:S(2)}) async-start(), calls=%async_computation.15 | async-start | bytes 2654208 | tf_op jit(solution)/shard_map/reduce_scatter | solution.py:278
  53.7 84.4 %copy-start.38 = (f32[768]{0:T(1024)}, f32[768]{0:T(1024)S(1)}, u32[]{:S(2)}) copy-start(f32[768]{0:T(1024)S(1)} %convert_element_type.108) | copy-start | bytes 9220
  141.0 2.2 copy-start.16
  141.0 2.2 copy-start.18
  141.0 2.2 copy-start.20
  141.0 2.2 copy-start.21
  143.2 4.5 copy-start.2
  143.2 4.7 copy-start.23
  145.8 2.2 copy-start.24
  182.3 167.3 %copy-start.3 = (f32[512,768]{1,0:T(8,128)}, f32[512,768]{1,0:T(8,128)S(1)}, u32[]{:S(2)}) copy-start(f32[512,768]{1,0:T(8,128)S(1)} %get-tuple-element.171) | copy-start | bytes 4718596
  339.7 9.9 copy-start.31
  339.7 9.9 copy-start.35
  339.7 9.9 copy-start.47
  349.6 3.5 copy-start.54
  349.6 3.5 copy-start.28
  353.1 2.1 copy-start.4
  358.9 140.5 %reduce-scatter.11.cloned.1.call-start = ((), (), s32[]{:S(2)}) async-start(), calls=%async_computation.14 | async-start | bytes 2654208 | tf_op jit(solution)/shard_map/reduce_scatter | solution.py:277
  365.9 8.7 copy-start.39
  377.2 194.5 %reduce-scatter.7.cloned.1.call-start = ((), (), s32[]{:S(2)}) async-start(), calls=%async_computation.12 | async-start | bytes 2654208 | tf_op jit(solution)/shard_map/reduce_scatter | solution.py:275
  384.9 21.1 %copy-start.17 = (bf16[512,12,32]{0,2,1:T(8,128)(2,1)S(1)}, bf16[512,12,32]{0,2,1:T(8,128)(2,1)}, u32[]{:S(2)}) copy-start(bf16[512,12,32]{0,2,1:T(8,128)(2,1)} %copy-done.16) | copy-start | bytes 1179652
  384.9 21.1 %copy-start.19 = (bf16[512,12,32]{0,2,1:T(8,128)(2,1)S(1)}, bf16[512,12,32]{0,2,1:T(8,128)(2,1)}, u32[]{:S(2)}) copy-start(bf16[512,12,32]{0,2,1:T(8,128)(2,1)} %copy-done.18) | copy-start | bytes 1179652
  432.6 211.3 %reduce-scatter.9.cloned.1.call-start = ((), (), s32[]{:S(2)}) async-start(), calls=%async_computation.13 | async-start | bytes 2654208 | tf_op jit(solution)/shard_map/reduce_scatter | solution.py:276
  436.5 372.3 %reduce-scatter.17.cloned.1.call-start = ((), (), s32[]{:S(2)}) async-start(), calls=%async_computation.17 | async-start | bytes 10616832 | tf_op jit(solution)/shard_map/reduce_scatter | solution.py:283
  447.8 525.8 %reduce-scatter.15.cloned.1.call-start = ((), (), s32[]{:S(2)}) async-start(), calls=%async_computation.16 | async-start | bytes 10616832 | tf_op jit(solution)/shard_map/reduce_scatter | solution.py:281
  457.4 593.0 %all-reduce.17.cloned.1.call-start = ((), (), s32[]{:S(2)}) async-start(), calls=%async_computation.18 | async-start | bytes 7077888 | tf_op jit(solution)/shard_map/psum | solution.py:286
  458.8 2.5 copy-start.11
  458.8 2.5 copy-start.48
  462.8 2.3 copy-start.26
  973.6 2.3 copy-start.1
  973.6 2.3 copy-start.30
  975.9 1.9 copy-start.34
  1050.4 5.2 copy-start.22
  1050.4 5.9 copy-start.8
  (20 other events, 22.0 us)
Sparse Core Ops, SparseCore 0:
  10.3 43.8 all-gather.7
  56.3 39.7 all-gather.9
  98.3 39.7 all-gather.11
  140.2 39.5 all-gather.13
  181.9 78.0 all-gather.15
  262.0 77.6 all-gather.17
  359.0 68.0 reduce-scatter.12
  430.5 68.7 reduce-scatter.10
  502.9 68.7 reduce-scatter.6
  575.0 68.7 reduce-scatter.8
  647.5 161.3 reduce-scatter.16
  812.3 161.2 reduce-scatter.14
  976.3 74.0 all-reduce.16
where the time goes:
time: 1070 us
  waiting for transfers between devices  756 us (71%)
  matrix products  141 us (13%)
  blocking collectives  108 us (10%)
  local copies, waits for them, and re-layouts  22.6 us (2%)
  other arithmetic  19.7 us (2%)
  between operations  16.7 us (2%)
    reduce_scatter x1, waiting for transfers between devices, local(): lax.psum_scatter(down_weight_grad, 'fsdp', scatter_dimension=0, tiled=True)  165 us
    reduce_scatter x1, waiting for transfers between devices, local(): lax.psum_scatter(up_weight_grad, 'fsdp', scatter_dimension=0, tiled=True)  165 us
    all_gather x1, waiting for transfers between devices, local(): lax.all_gather(up_weight, 'fsdp', axis=0, tiled=True)  76 us
    unnamed x2, blocking collectives  75.2 us
    reduce_scatter x1, waiting for transfers between devices, local(): lax.psum_scatter(query_weight_grad, 'fsdp', scatter_dimension=0, tiled=True)  72.3 us
    all_gather x1, waiting for transfers between devices, local(): lax.all_gather(down_weight, 'fsdp', axis=0, tiled=True)  72.3 us
    reduce_scatter x1, waiting for transfers between devices, local(): lax.psum_scatter(key_weight_grad, 'fsdp', scatter_dimension=0, tiled=True)  72.2 us
    all_gather x1, waiting for transfers between devices, local(): lax.all_gather(key_weight, 'fsdp', axis=0, tiled=True)  39.8 us
  transfers between devices with their start and end apart: 13, of which 11 were waited for; matrix products, arithmetic and copies ran while one was open for 14% of the time, Pallas kernels for 0%

commit v1 on v0

v1 whole, which is shorter than its diff:
```python
from functools import partial
import math

import jax
import jax.numpy as jnp
from jax import lax
from jax.experimental import pallas as pl
from jax.experimental.pallas import tpu as pltpu
from jax.sharding import PartitionSpec as P

H = 12
HD = 64
BLOCK = 16
EPSILON = 1e-05
BASE = 10000.0
NEGATIVE = -1e30
BF = jnp.bfloat16
F32 = jnp.float32
SMALL = 16
VMEM_LIMIT = 56 * 1024 * 1024


def row_layout(length_row, row_count, slot_count):
    doubled = 2 * length_row
    ends_at = jnp.cumsum(doubled, dtype=jnp.int32)
    starts_at = ends_at - doubled
    row_index = jnp.arange(row_count, dtype=jnp.int32)
    member = (row_index[:, None] >= starts_at[None, :]) & (row_index[:, None] < ends_at[None, :])
    slot_ids = jnp.arange(slot_count, dtype=jnp.int32)
    slot_index = jnp.sum(jnp.where(member, slot_ids[None, :], 0), axis=1, dtype=jnp.int32)
    start_row = jnp.sum(jnp.where(member, starts_at[None, :], 0), axis=1, dtype=jnp.int32)
    seq_length = jnp.sum(jnp.where(member, length_row[None, :], 0), axis=1, dtype=jnp.int32)
    local_row = row_index - start_row
    clean_flag = (local_row >= seq_length).astype(jnp.int32)
    position = local_row - clean_flag * seq_length
    return (row_index, slot_index, clean_flag, position)


def allowed_pairs(query_side, key_side, block_size, slot_count):
    query_row, query_slot, query_clean, query_pos = query_side
    key_row, key_slot, key_clean, key_pos = key_side
    query_block = query_pos // block_size
    key_block = key_pos // block_size
    same_seq = query_slot[:, None] == key_slot[None, :]
    key_noisy = key_clean[None, :] == 0
    key_plain = key_clean[None, :] == 1
    noisy_rule = key_noisy & (key_block[None, :] == query_block[:, None]) | key_plain & (
        key_block[None, :] < query_block[:, None]
    )
    clean_rule = key_plain & (key_block[None, :] <= query_block[:, None])
    rule_held = jnp.where(query_clean[:, None] == 1, clean_rule, noisy_rule)
    padded = query_slot == slot_count - 1
    real_pairs = same_seq & rule_held & jnp.logical_not(padded)[:, None]
    self_pairs = padded[:, None] & (query_row[:, None] == key_row[None, :])
    return real_pairs | self_pairs


def rotary_tables(position):
    half = HD // 2
    lane = jnp.arange(2 * HD, dtype=jnp.int32)
    freqs = jnp.exp((lane % half).astype(F32) * (-2.0 * math.log(BASE) / HD))
    angles = position.astype(F32)[:, None] * freqs[None, :]
    sign = jnp.where(lane % HD < half, -1.0, 1.0)
    return jnp.cos(angles), jnp.sin(angles) * sign[None, :]


def swap(values, axis, mask, size):
    return lax.ppermute(values, axis, [(i, i ^ mask) for i in range(size)])


def dot(a, b):
    return jnp.dot(a, b, preferred_element_type=F32)


def dot_nt(a, b):
    return lax.dot_general(a, b, (((1,), (1,)), ((), ())), preferred_element_type=F32)


def dot_tn(a, b):
    return lax.dot_general(a, b, (((0,), (0,)), ((), ())), preferred_element_type=F32)


def params(**more):
    return pltpu.CompilerParams(vmem_limit_bytes=VMEM_LIMIT, **more)


def cost(flops, moved):
    return pl.CostEstimate(flops=int(flops), bytes_accessed=int(moved), transcendentals=0)


def norm_parts(values):
    center = values - jnp.mean(values, axis=-1, keepdims=True)
    spread = jnp.mean(center * center, axis=-1, keepdims=True)
    inv = lax.rsqrt(spread + EPSILON)
    return center * inv, inv


def norm_back(grad, unit, inv, gain):
    scaled = grad * gain
    first = jnp.mean(scaled, axis=-1, keepdims=True)
    second = jnp.mean(scaled * unit, axis=-1, keepdims=True)
    return inv * (scaled - first - unit * second)


def turn(values, cosine, sine):
    half = HD // 2
    pair = 2 * HD
    lane = lax.broadcasted_iota(jnp.int32, (1, pair), 1)
    low = (lane % HD) < half
    parts = []
    for at in range(0, values.shape[1], pair):
        part = values[:, at : at + pair]
        other = jnp.where(low, pltpu.roll(part, pair - half, 1), pltpu.roll(part, half, 1))
        parts.append(part * cosine + other * sine)
    return parts[0] if len(parts) == 1 else jnp.concatenate(parts, axis=1)


def bits_of(index, masks):
    total = 0
    for bit, mask in enumerate(masks):
        if (index >> bit) & 1:
            total |= mask
    return total


def assemble_kernel(masks, h, idx_ref, a0, a1, a2, a3, b0, b1, b2, b3, out_ref, sems):
    count = 1 << len(masks)
    half = count // 2
    me_d, me_f = idx_ref[0], idx_ref[1]
    copies = []

    def put(src, r, k, colour):
        d = me_d ^ r
        j = me_f ^ k
        copy = pltpu.make_async_copy(src, out_ref.at[d, j, colour], sems.at[len(copies)])
        copy.start()
        copies.append(copy)

    for ref, r in ((a0, 0), (a1, 2), (a2, 1), (a3, 3)):
        for i in range(count):
            put(ref.at[i], r, bits_of(i, masks), 0)
    for ref, r, y in ((b0, 0, 0), (b1, 0, 1), (b2, 1, 0), (b3, 1, 1)):
        for x in range(2):
            for i in range(half):
                put(ref.at[x * half + i], r | (2 * x), bits_of(i, masks) | y, 1)
    for copy in copies:
        copy.wait()


def assemble(idx, pieces, masks, shards, h, width):
    count = 1 << len(masks)
    out = pl.pallas_call(
        partial(assemble_kernel, masks, h),
        out_shape=jax.ShapeDtypeStruct((4, shards, 2, h, width), BF),
        in_specs=[pl.BlockSpec(memory_space=pltpu.SMEM)]
        + [pl.BlockSpec(memory_space=pl.ANY)] * 8,
        out_specs=pl.BlockSpec(memory_space=pltpu.VMEM),
        scratch_shapes=[pltpu.SemaphoreType.DMA((8 * count,))],
        compiler_params=params(),
        cost_estimate=cost(0, 4 * shards * 2 * h * width * 4),
        name="assemble",
    )(idx, *pieces)
    return out.reshape(4, shards * 2 * h, width)


def qkv_kernel(x_ref, small_ref, cos_ref, sin_ref, w_ref, normed_ref, out_ref, keep):
    g = pl.program_id(0)

    @pl.when(g == 0)
    def _():
        unit, _ = norm_parts(x_ref[...].astype(F32))
        normed = (unit * small_ref[0:1, :] + small_ref[1:2, :]).astype(BF)
        keep[...] = normed
        normed_ref[...] = normed

    product = dot(keep[...], w_ref[0])

    @pl.when(g < 2)
    def _():
        out_ref[0] = turn(product, cos_ref[...], sin_ref[...]).astype(BF)

    @pl.when(g == 2)
    def _():
        out_ref[0] = product.astype(BF)


def qkv(x, small, cosine, sine, weights):
    n, d = x.shape
    return pl.pallas_call(
        qkv_kernel,
        grid=(3,),
        out_shape=(jax.ShapeDtypeStruct((n, d), BF), jax.ShapeDtypeStruct((3, n, d), BF)),
        in_specs=[
            pl.BlockSpec((n, d), lambda g: (0, 0)),
            pl.BlockSpec(small.shape, lambda g: (0, 0)),
            pl.BlockSpec(cosine.shape, lambda g: (0, 0)),
            pl.BlockSpec(sine.shape, lambda g: (0, 0)),
            pl.BlockSpec((1, d, d), lambda g: (g, 0, 0)),
        ],
        out_specs=(
            pl.BlockSpec((n, d), lambda g: (0, 0)),
            pl.BlockSpec((1, n, d), lambda g: (g, 0, 0)),
        ),
        scratch_shapes=[pltpu.VMEM((n, d), BF)],
        compiler_params=params(),
        cost_estimate=cost(6 * n * d * d, 2 * (5 * n * d + 3 * d * d)),
        name="qkv",
    )(x, small, cosine, sine, weights)


def head_mask(which):
    lane = lax.broadcasted_iota(jnp.int32, (1, 2 * HD), 1)
    return (lane < HD) if which == 0 else (lane >= HD)


def attend_kernel(q_ref, k_ref, v_ref, bias_ref, mixed_ref, probs_ref):
    q, k, v = q_ref[0], k_ref[0], v_ref[0]
    zero = jnp.zeros((), BF)
    parts = []
    for h in range(2):
        own = jnp.where(head_mask(h), q, zero)
        scores = dot_nt(own, k) * (HD**-0.5) + bias_ref[...]
        top = jnp.max(scores, axis=1, keepdims=True)
        raised = jnp.exp(scores - top)
        total = jnp.sum(raised, axis=1, keepdims=True)
        probs = (raised * (1.0 / total)).astype(BF)
        probs_ref[h] = probs
        parts.append(dot(probs, v))
    mixed_ref[...] = jnp.where(head_mask(0), parts[0], parts[1]).astype(BF)


def attend(three, bias):
    _, n, d = three.shape
    pair = 2 * HD
    return pl.pallas_call(
        attend_kernel,
        grid=(d // pair,),
        out_shape=(
            jax.ShapeDtypeStruct((n, d), BF),
            jax.ShapeDtypeStruct((d // HD, n, n), BF),
        ),
        in_specs=[
            pl.BlockSpec((1, n, pair), lambda p: (0, 0, p)),
            pl.BlockSpec((1, n, pair), lambda p: (1, 0, p)),
            pl.BlockSpec((1, n, pair), lambda p: (2, 0, p)),
            pl.BlockSpec((n, n), lambda p: (0, 0)),
        ],
        out_specs=(
            pl.BlockSpec((n, pair), lambda p: (0, p)),
            pl.BlockSpec((2, n, n), lambda p: (p, 0, 0)),
        ),
        compiler_params=params(),
        cost_estimate=cost(8 * n * n * d, 2 * n * n * (d // HD) + 8 * n * d),
        name="attend",
    )(three, three, three, bias)


def attend_back_kernel(
    q_ref, k_ref, v_ref, probs_ref, grad_ref, mixed_ref, cos_ref, sin_ref, out_ref
):
    q, k, v, grad = q_ref[0], k_ref[0], v_ref[0], grad_ref[...]
    zero = jnp.zeros((), BF)
    product = grad.astype(F32) * mixed_ref[...].astype(F32)
    dq, dk, dv = [], [], []
    for h in range(2):
        mask = head_mask(h)
        inner = jnp.sum(jnp.where(mask, product, 0.0), axis=1, keepdims=True)
        probs = probs_ref[h]
        prob_grad = dot_nt(jnp.where(mask, grad, zero), v)
        score_grad = (probs.astype(F32) * (prob_grad - inner)).astype(BF)
        dq.append(dot(score_grad, k))
        dk.append(dot_tn(score_grad, q))
        dv.append(dot_tn(probs, grad))
    first = head_mask(0)
    scale = HD**-0.5
    cosine, sine = cos_ref[...], sin_ref[...]
    out_ref[0] = turn(jnp.where(first, dq[0], dq[1]) * scale, cosine, -sine).astype(BF)
    out_ref[1] = turn(jnp.where(first, dk[0], dk[1]) * scale, cosine, -sine).astype(BF)
    out_ref[2] = jnp.where(first, dv[0], dv[1]).astype(BF)


def attend_back(three, probs, grad, mixed, cosine, sine):
    _, n, d = three.shape
    pair = 2 * HD
    return pl.pallas_call(
        attend_back_kernel,
        grid=(d // pair,),
        out_shape=jax.ShapeDtypeStruct((3, n, d), BF),
        in_specs=[
            pl.BlockSpec((1, n, pair), lambda p: (0, 0, p)),
            pl.BlockSpec((1, n, pair), lambda p: (1, 0, p)),
            pl.BlockSpec((1, n, pair), lambda p: (2, 0, p)),
            pl.BlockSpec((2, n, n), lambda p: (p, 0, 0)),
            pl.BlockSpec((n, pair), lambda p: (0, p)),
            pl.BlockSpec((n, pair), lambda p: (0, p)),
            pl.BlockSpec(cosine.shape, lambda p: (0, 0)),
            pl.BlockSpec(sine.shape, lambda p: (0, 0)),
        ],
        out_specs=pl.BlockSpec((3, n, pair), lambda p: (0, 0, p)),
        compiler_params=params(),
        cost_estimate=cost(16 * n * n * d, 2 * n * n * (d // HD) + 16 * n * d),
        name="attend_back",
    )(three, three, three, probs, grad, mixed, cosine, sine)


def branch_kernel(x_ref, mixed_ref, w_ref, small_ref, residual_ref, hidden_ref):
    residual = x_ref[...].astype(F32) + dot(mixed_ref[...], w_ref[0])
    residual_ref[...] = residual
    unit, _ = norm_parts(residual)
    hidden_ref[...] = (unit * small_ref[2:3, :] + small_ref[3:4, :]).astype(BF)


def branch(x, mixed, weights, small):
    n, d = x.shape
    rows = n // 2
    return pl.pallas_call(
        branch_kernel,
        grid=(2,),
        out_shape=(jax.ShapeDtypeStruct((n, d), F32), jax.ShapeDtypeStruct((n, d), BF)),
        in_specs=[
            pl.BlockSpec((rows, d), lambda g: (g, 0)),
            pl.BlockSpec((rows, d), lambda g: (g, 0)),
            pl.BlockSpec((1, d, d), lambda g: (3, 0, 0)),
            pl.BlockSpec(small.shape, lambda g: (0, 0)),
        ],
        out_specs=(
            pl.BlockSpec((rows, d), lambda g: (g, 0)),
            pl.BlockSpec((rows, d), lambda g: (g, 0)),
        ),
        compiler_params=params(),
        cost_estimate=cost(2 * n * d * d, 10 * n * d + 2 * d * d),
        name="branch",
    )(x, mixed, weights, small)


def up_kernel(hidden_ref, w_ref, small_ref, act_ref, slope_ref):
    g = pl.program_id(0)
    bias = small_ref[5:6, :]
    for other in range(1, 4):
        bias = jnp.where(g == other, small_ref[5 + other : 6 + other, :], bias)
    v = dot(hidden_ref[...], w_ref[0]) + bias
    c = math.sqrt(2.0 / math.pi)
    square = v * v
    t = jnp.tanh(v * (c + (c * 0.044715) * square))
    half = 0.5 * (1.0 + t)
    act_ref[0] = (v * half).astype(BF)
    slope = half + (0.5 * v) * (1.0 - t * t) * (c + (3.0 * c * 0.044715) * square)
    slope_ref[0] = slope.astype(BF)


def up(hidden, weights, small):
    n, d = hidden.shape
    return pl.pallas_call(
        up_kernel,
        grid=(4,),
        out_shape=(
            jax.ShapeDtypeStruct((4, n, d), BF),
            jax.ShapeDtypeStruct((4, n, d), BF),
        ),
        in_specs=[
            pl.BlockSpec((n, d), lambda g: (0, 0)),
            pl.BlockSpec((1, d, d), lambda g: (g, 0, 0)),
            pl.BlockSpec(small.shape, lambda g: (0, 0)),
        ],
        out_specs=(
            pl.BlockSpec((1, n, d), lambda g: (g, 0, 0)),
            pl.BlockSpec((1, n, d), lambda g: (g, 0, 0)),
        ),
        compiler_params=params(),
        cost_estimate=cost(8 * n * d * d, 18 * n * d + 8 * d * d),
        name="up",
    )(hidden, weights, small)


def weight_grad_kernel(masks, h, shards, idx_ref, x_ref, y_ref, out_ref, keep):
    keep[...] = dot_tn(x_ref[0], y_ref[0]).astype(BF)
    me_f = idx_ref[1]
    for i in range(shards):
        j = me_f ^ bits_of(i, masks)
        for colour in range(2):
            start = pl.multiple_of(j * (2 * h) + colour * h, h & -h)
            out_ref[0, colour, i] = keep[pl.ds(start, h), :]


def weight_grad(idx, xs, ys, x_of, y_of, distances, masks, shards, h):
    _, n, d = xs.shape
    first, step = distances[0], distances[1] - distances[0]

    def chunk(g, idx_ref):
        return idx_ref[0] ^ (first + step * g)

    return pl.pallas_call(
        partial(weight_grad_kernel, masks, h, shards),
        grid_spec=pltpu.PrefetchScalarGridSpec(
            num_scalar_prefetch=1,
            grid=(len(distances),),
            in_specs=[
                pl.BlockSpec((1, n, d), lambda g, i: (x_of(chunk(g, i)), 0, 0)),
                pl.BlockSpec((1, n, d), lambda g, i: (y_of(chunk(g, i)), 0, 0)),
            ],
            out_specs=pl.BlockSpec(
                (1, 2, shards, h, d), lambda g, i: (g, 0, 0, 0, 0)
            ),
            scratch_shapes=[pltpu.VMEM((d, d), BF)],
        ),
        out_shape=jax.ShapeDtypeStruct((len(distances), 2, shards, h, d), BF),
        compiler_params=params(),
        cost_estimate=cost(
            2 * len(distances) * n * d * d, 2 * len(distances) * (2 * n * d + d * d)
        ),
        name="weight_grad",
    )(idx, xs, ys)


def act_grad_kernel(c_ref, down_ref, up_ref, slope_ref, pre_ref, sums_ref, hidden_ref):
    g = pl.program_id(0)
    c = c_ref[...]

    @pl.when(g == 0)
    def _():
        hidden_ref[...] = jnp.zeros_like(hidden_ref)
        sums_ref[...] = jnp.zeros_like(sums_ref)
        sums_ref[4:5, :] = jnp.sum(c.astype(F32), axis=0, keepdims=True)

    pre = (dot_nt(c, down_ref[0]) * slope_ref[0].astype(F32)).astype(BF)
    pre_ref[0] = pre
    sums = jnp.sum(pre.astype(F32), axis=0, keepdims=True)
    row = lax.broadcasted_iota(jnp.int32, (sums_ref.shape[0], 1), 0)
    sums_ref[...] += jnp.where(row == 5 + g, sums, 0.0)
    hidden_ref[...] += dot_nt(pre, up_ref[0])


def act_grad(c, down, up_weights, slope):
    n, d = c.shape
    return pl.pallas_call(
        act_grad_kernel,
        grid=(4,),
        out_shape=(
            jax.ShapeDtypeStruct((4, n, d), BF),
            jax.ShapeDtypeStruct((SMALL, d), F32),
            jax.ShapeDtypeStruct((n, d), F32),
        ),
        in_specs=[
            pl.BlockSpec((n, d), lambda g: (0, 0)),
            pl.BlockSpec((1, d, d), lambda g: (g, 0, 0)),
            pl.BlockSpec((1, d, d), lambda g: (g, 0, 0)),
            pl.BlockSpec((1, n, d), lambda g: (g, 0, 0)),
        ],
        out_specs=(
            pl.BlockSpec((1, n, d), lambda g: (g, 0, 0)),
            pl.BlockSpec((SMALL, d), lambda g: (0, 0)),
            pl.BlockSpec((n, d), lambda g: (0, 0)),
        ),
        compiler_params=params(),
        cost_estimate=cost(16 * n * d * d, 22 * n * d + 16 * d * d),
        name="act_grad",
    )(c, down, up_weights, slope)


def middle_kernel(
    c_ref, hidden_ref, residual_ref, small_ref, w_ref, grad_ref, low_ref, mixed_ref, sums_ref
):
    @pl.when(pl.program_id(0) == 0)
    def _():
        sums_ref[...] = jnp.zeros_like(sums_ref)

    grad = hidden_ref[...]
    unit, inv = norm_parts(residual_ref[...])
    sums_ref[2:3, :] += jnp.sum(grad * unit, axis=0, keepdims=True)
    sums_ref[3:4, :] += jnp.sum(grad, axis=0, keepdims=True)
    full = c_ref[...].astype(F32) + norm_back(grad, unit, inv, small_ref[2:3, :])
    grad_ref[...] = full
    low = full.astype(BF)
    low_ref[...] = low
    mixed_ref[...] = dot_nt(low, w_ref[0]).astype(BF)


def middle(c, hidden_grad, residual, small, weights):
    n, d = c.shape
    rows = n // 2
    return pl.pallas_call(
        middle_kernel,
        grid=(2,),
        out_shape=(
            jax.ShapeDtypeStruct((n, d), F32),
            jax.ShapeDtypeStruct((n, d), BF),
            jax.ShapeDtypeStruct((n, d), BF),
            jax.ShapeDtypeStruct((SMALL, d), F32),
        ),
        in_specs=[
            pl.BlockSpec((rows, d), lambda g: (g, 0)),
            pl.BlockSpec((rows, d), lambda g: (g, 0)),
            pl.BlockSpec((rows, d), lambda g: (g, 0)),
            pl.BlockSpec(small.shape, lambda g: (0, 0)),
            pl.BlockSpec((1, d, d), lambda g: (3, 0, 0)),
        ],
        out_specs=(
            pl.BlockSpec((rows, d), lambda g: (g, 0)),
            pl.BlockSpec((rows, d), lambda g: (g, 0)),
            pl.BlockSpec((rows, d), lambda g: (g, 0)),
            pl.BlockSpec((SMALL, d), lambda g: (0, 0)),
        ),
        compiler_params=params(),
        cost_estimate=cost(2 * n * d * d, 18 * n * d + 2 * d * d),
        name="middle",
    )(c, hidden_grad, residual, small, weights)


def input_kernel(x_ref, three_ref, w_ref, small_ref, grad_ref, out_ref, sums_ref, total):
    g = pl.program_id(0)
    part = dot_nt(three_ref[0], w_ref[0])

    @pl.when(g == 0)
    def _():
        total[...] = part

    @pl.when(g > 0)
    def _():
        total[...] += part

    @pl.when(g == 2)
    def _():
        grad = total[...]
        unit, inv = norm_parts(x_ref[...].astype(F32))
        sums_ref[...] = jnp.zeros_like(sums_ref)
        sums_ref[0:1, :] = jnp.sum(grad * unit, axis=0, keepdims=True)
        sums_ref[1:2, :] = jnp.sum(grad, axis=0, keepdims=True)
        out_ref[...] = grad_ref[...] + norm_back(grad, unit, inv, small_ref[0:1, :])


def input_grads(x, three_grad, weights, small, residual_grad):
    n, d = x.shape
    return pl.pallas_call(
        input_kernel,
        grid=(3,),
        out_shape=(jax.ShapeDtypeStruct((n, d), F32), jax.ShapeDtypeStruct((SMALL, d), F32)),
        in_specs=[
            pl.BlockSpec((n, d), lambda g: (0, 0)),
            pl.BlockSpec((1, n, d), lambda g: (g, 0, 0)),
            pl.BlockSpec((1, d, d), lambda g: (g, 0, 0)),
            pl.BlockSpec(small.shape, lambda g: (0, 0)),
            pl.BlockSpec((n, d), lambda g: (0, 0)),
        ],
        out_specs=(
            pl.BlockSpec((n, d), lambda g: (0, 0)),
            pl.BlockSpec((SMALL, d), lambda g: (0, 0)),
        ),
        scratch_shapes=[pltpu.VMEM((n, d), F32)],
        compiler_params=params(),
        cost_estimate=cost(6 * n * d * d, 16 * n * d + 6 * d * d),
        name="input_grads",
    )(x, three_grad, weights, small, residual_grad)


def down_kernel(act_ref, w_ref, small_ref, residual_ref, out_ref, total):
    g = pl.program_id(0)
    part = dot(act_ref[0], w_ref[0])

    @pl.when(g == 0)
    def _():
        total[...] = residual_ref[...] + small_ref[4:5, :] + part

    @pl.when(g > 0)
    def _():
        total[...] += part

    @pl.when(g == 3)
    def _():
        out_ref[...] = total[...].astype(BF)


def down_out(act, weights, small, residual):
    n, d = residual.shape
    return pl.pallas_call(
        down_kernel,
        grid=(4,),
        out_shape=jax.ShapeDtypeStruct((n, d), BF),
        in_specs=[
            pl.BlockSpec((1, n, d), lambda g: (g, 0, 0)),
            pl.BlockSpec((1, d, d), lambda g: (g, 0, 0)),
            pl.BlockSpec(small.shape, lambda g: (0, 0)),
            pl.BlockSpec((n, d), lambda g: (0, 0)),
        ],
        out_specs=pl.BlockSpec((n, d), lambda g: (0, 0)),
        scratch_shapes=[pltpu.VMEM((n, d), F32)],
        compiler_params=params(),
        cost_estimate=cost(8 * n * d * d, 14 * n * d + 8 * d * d),
        name="down_out",
    )(act, weights, small, residual)


def local(dp, fsdp, tokens, lengths, *rest):
    (
        norm1_gain,
        norm1_bias,
        query_weight,
        key_weight,
        value_weight,
        output_weight,
        norm2_gain,
        norm2_bias,
        up_weight,
        up_bias,
        down_weight,
        down_bias,
        cotangent,
    ) = rest
    row_count, width = tokens.shape
    slot_count = lengths.shape[1]
    R = width // fsdp
    h = R // 2
    me_dp = lax.axis_index("dp").astype(jnp.int32)
    me_f = lax.axis_index("fsdp").astype(jnp.int32)
    d4 = me_dp % 4
    idx = jnp.stack([d4, me_f])
    masks = []
    mask = fsdp // 2
    while mask >= 1:
        masks.append(mask)
        mask //= 2
    masks = tuple(masks)
    outer = masks[:-1]

    def fswap(v, m):
        return swap(v, "fsdp", m, fsdp)

    def dswap(v, m):
        return swap(v, "dp", m, dp)

    shard4 = (query_weight, key_weight, value_weight, output_weight)
    piece1 = lax.select_n(d4, *shard4)
    piece2 = lax.dynamic_index_in_dim(
        up_weight.reshape(R, fsdp, 4, R), d4, axis=2, keepdims=False
    ).reshape(R, width)
    piece3 = lax.dynamic_slice_in_dim(down_weight, d4 * R, R, axis=0)

    tall = jnp.concatenate(
        [norm1_gain, norm1_bias, norm2_gain, norm2_bias, down_bias, up_bias]
    ).reshape(9, R)
    lane = jnp.arange(width, dtype=jnp.int32) // R
    tall = jnp.where((lane == me_f)[None, :], jnp.tile(tall, (1, fsdp)), jnp.zeros((), BF))
    tall = jnp.pad(tall, ((0, SMALL - 9), (0, 0)))

    def gather(piece, extra):
        size = R
        if extra is not None:
            piece = jnp.concatenate([piece, extra], axis=0)
            size = R + SMALL
        cur = piece[None]
        for m in outer[:-1]:
            cur = jnp.concatenate([cur, fswap(cur, m)], axis=0)
        m = outer[-1]
        other = fswap(cur, m)
        if extra is not None:
            a = jnp.concatenate(
                [
                    jnp.concatenate([t[:, :h], t[:, R:]], axis=1) for t in (cur, other)
                ],
                axis=0,
            )
        else:
            a = jnp.concatenate([cur[:, :h], other[:, :h]], axis=0)
        b = jnp.concatenate([cur[:, h:R], other[:, h:R]], axis=0)
        a_y = fswap(a, masks[-1])
        b_x = dswap(b, 2)
        small = None
        if extra is not None:
            small = jnp.sum(a[:, h:].astype(F32), axis=0) + jnp.sum(
                a_y[:, h:].astype(F32), axis=0
            )
        a1 = jnp.concatenate([a[:, :h], a_y[:, :h]], axis=0)
        b1 = jnp.concatenate([b, b_x], axis=0)
        a_x = dswap(a1, 2)
        b_y = fswap(b1, masks[-1])
        pieces = [a1, a_x, dswap(a1, 1), dswap(a_x, 1), b1, b_y, dswap(b1, 1), dswap(b_y, 1)]
        return assemble(idx, pieces, masks, fsdp, h, width), small

    first4, small = gather(piece1, tall)
    up4, _ = gather(piece2, None)
    down4, _ = gather(piece3, None)

    layout = row_layout(lengths[0], row_count, slot_count)
    cosine, sine = rotary_tables(layout[3])
    bias = jnp.where(allowed_pairs(layout, layout, BLOCK, slot_count), 0.0, NEGATIVE)
    normed, three = qkv(tokens, small, cosine, sine, first4)
    mixed, probs = attend(three, bias)
    residual, hidden_in = branch(tokens, mixed, first4, small)
    act, slope = up(hidden_in, up4, small)

    def both(xs, ys, x_of, y_of):
        args = (masks, fsdp, h)
        send = weight_grad(idx, xs, ys, x_of, y_of, (1, 3), *args)
        keep = weight_grad(idx, xs, ys, x_of, y_of, (0, 2), *args)
        return send, keep

    half = fsdp // 2

    def scatter(send, keep, small_sum=None):
        got = dswap(send, 1)
        a_send = keep[1, 0] + got[1, 0]
        a_keep = keep[0, 0] + got[0, 0]
        b_send = keep[:, 1, half:] + got[:, 1, half:]
        b_keep = keep[:, 1, :half] + got[:, 1, :half]
        extra = small_sum is not None

        def with_small(t, s):
            if not extra:
                return t
            return jnp.concatenate([t.reshape(-1, width), s.astype(BF)], axis=0)

        def parts(t, shape):
            if not extra:
                return t, None
            rows = math.prod(shape[:-1])
            return t[:rows].reshape(shape), t[rows:].astype(F32)

        if extra:
            small_sum = small_sum + dswap(small_sum.astype(BF), 1).astype(F32)
        a_got, s = parts(dswap(with_small(a_send, small_sum), 2), a_send.shape)
        b_got = fswap(b_send, masks[-1])
        if extra:
            small_sum = small_sum + s
        a_send = a_keep[half:] + a_got[half:]
        a_keep = a_keep[:half] + a_got[:half]
        b_send = b_keep[1] + b_got[1]
        b_keep = b_keep[0] + b_got[0]
        a_got, s = parts(fswap(with_small(a_send, small_sum), masks[-1]), a_send.shape)
        b_got = dswap(b_send, 2)
        if extra:
            small_sum = small_sum + s
        cur = jnp.stack([a_keep + a_got, b_keep + b_got], axis=1)
        for m in reversed(outer):
            count = cur.shape[0] // 2
            out = cur[count:]
            got, s = parts(fswap(with_small(out, small_sum), m), out.shape)
            if extra:
                small_sum = small_sum + s
            cur = cur[:count] + got
        total = cur.reshape(R, width)
        m = 4
        while m < dp:
            got, s = parts(dswap(with_small(total, small_sum), m), total.shape)
            total = total + got
            if extra:
                small_sum = small_sum + s
            m *= 2
        total_x = dswap(total, 2)
        four = jnp.stack([total, dswap(total, 1), total_x, dswap(total_x, 1)])
        return four, small_sum

    c1 = cotangent[None]
    send3, keep3 = both(act, c1, lambda d: d, lambda d: 0)
    pre_grad, sums_act, hidden_grad = act_grad(cotangent, down4, up4, slope)
    residual_grad, branch_grad, mixed_grad, sums_mid = middle(
        cotangent, hidden_grad, residual, small, first4
    )
    send2, keep2 = both(hidden_in[None], pre_grad, lambda d: 0, lambda d: d)
    three_grad = attend_back(three, probs, mixed_grad, mixed, cosine, sine)
    lefts = jnp.stack([normed, mixed])
    rights = jnp.concatenate([three_grad, branch_grad[None]], axis=0)
    send1, keep1 = both(lefts, rights, lambda d: d // 3, lambda d: d)
    input_grad, sums_in = input_grads(tokens, three_grad, first4, small, residual_grad)
    output = down_out(act, down4, small, residual)

    four3, _ = scatter(send3, keep3)
    four2, _ = scatter(send2, keep2)
    four1, small_sum = scatter(send1, keep1, sums_act + sums_mid + sums_in)

    def pick(four, d):
        return lax.dynamic_index_in_dim(four, d4 ^ d, axis=0, keepdims=False).astype(F32)

    first_grads = [pick(four1, d) for d in range(4)]
    up_grad = jnp.stack(
        [pick(four2, d).reshape(R, fsdp, R) for d in range(4)], axis=2
    ).reshape(R, 4 * width)
    down_grad = jnp.concatenate([pick(four3, d) for d in range(4)], axis=0)
    own = lax.dynamic_slice_in_dim(small_sum, me_f * R, R, axis=1)
    return (
        output,
        input_grad,
        own[0],
        own[1],
        first_grads[0],
        first_grads[1],
        first_grads[2],
        first_grads[3],
        own[2],
        own[3],
        up_grad,
        own[5:9].reshape(4 * R),
        down_grad,
        own[4],
    )


def solution(mesh):
    rows = P(("dp", "fsdp"), None)
    flat = P("fsdp")
    tall = P("fsdp", None)
    in_specs = (
        rows, rows, flat, flat, tall, tall, tall, tall, flat, flat, tall, flat, tall, flat, rows,
    )
    out_specs = (
        rows, rows, flat, flat, tall, tall, tall, tall, flat, flat, tall, flat, tall, flat,
    )
    return jax.shard_map(
        partial(local, mesh.shape["dp"], mesh.shape["fsdp"]),
        mesh=mesh,
        in_specs=in_specs,
        out_specs=out_specs,
        check_vma=False,
    )
```

time: 1070 us -> 348 us (0.33)
  waiting for transfers between devices: 756 us -> 135 us
  matrix products: 141 us -> 0 us
  Pallas kernels: 0 us -> 121 us
  blocking collectives: 108 us -> 0 us
  starting transfers between devices: 1.13 us -> 52.1 us
  between operations: 16.7 us -> 1.67 us
    reduce_scatter x6 -> x0, waiting for transfers between devices: 508 us -> none  [the longest x1 165 us: local(): lax.psum_scatter(down_weight_grad, 'fsdp', scatter_dimension=0, tiled=True)]
    all_gather x6 -> x0, waiting for transfers between devices: 224 us -> none  [the longest x1 76 us: local(): lax.all_gather(up_weight, 'fsdp', axis=0, tiled=True)]
    dot_general x24 -> x0, matrix products: 141 us -> none  [the longest x6 28.7 us: weight_grad(): jnp.einsum('ri,rj->ij', left, right, preferred_element_type=jnp.float32)]
    ppermute x0 -> x61, waiting for transfers between devices: none -> 135 us  [swap(): return lax.ppermute(values, axis, [(i, i ^ mask) for i in range(size)])]
    pallas_call x0 -> x18, Pallas kernels: none -> 121 us  [the longest x6 29.9 us: weight_grad(): pl.pallas_call(partial(weight_grad_kernel, masks, h, shards), grid_spec=p...]
    unnamed x2 -> x0, blocking collectives: 75.2 us -> none
    ppermute x0 -> x61, starting transfers between devices: none -> 52.1 us  [swap(): return lax.ppermute(values, axis, [(i, i ^ mask) for i in range(size)])]
    all_gather x1 -> x0, blocking collectives: 26 us -> none  [local(): lax.all_gather(up_bias, 'fsdp', axis=0, tiled=True)]
  transfers between devices with their start and end apart: 13 -> 61, of which waited for: 11 -> 21; matrix products, arithmetic and copies ran while one was open for 14% -> 7% of each run, Pallas kernels for 0% -> 15%
where the time goes in v1:
time: 348 us; the launch traced here: 346 us
  waiting for transfers between devices  135 us (39%)
  Pallas kernels  121 us (35%)
  starting transfers between devices  52.1 us (15%)
  other arithmetic  20.4 us (6%)
  local copies, waits for them, and re-layouts  16.8 us (5%)
    ppermute x61, waiting for transfers between devices, swap(): return lax.ppermute(values, axis, [(i, i ^ mask) for i in range(size)])  135 us
    ppermute x61, starting transfers between devices, swap(): return lax.ppermute(values, axis, [(i, i ^ mask) for i in range(size)])  52.1 us
    pallas_call x6, Pallas kernels, weight_grad(): pl.pallas_call(partial(weight_grad_kernel, masks, h, shards), grid_spec=p...  29.9 us
    pallas_call x3, Pallas kernels, assemble(): pl.pallas_call(partial(assemble_kernel, masks, h), out_shape=jax.ShapeDty...  17.3 us
    pallas_call x1, Pallas kernels, attend_back(): pl.pallas_call(attend_back_kernel, grid=(d // pair,), out_shape=jax.Shape...  11.6 us
    pallas_call x1, Pallas kernels, act_grad(): pl.pallas_call(act_grad_kernel, grid=(4,), out_shape=(jax.ShapeDtypeStruc...  10.6 us
    pallas_call x1, Pallas kernels, attend(): pl.pallas_call(attend_kernel, grid=(d // pair,), out_shape=(jax.ShapeDtyp...  10.4 us
    pallas_call x1, Pallas kernels, up(): pl.pallas_call(up_kernel, grid=(4,), out_shape=(jax.ShapeDtypeStruct((4,...  8.81 us
  transfers between devices with their start and end apart: 61, of which 21 were waited for; matrix products, arithmetic and copies ran while one was open for 7% of the time, Pallas kernels for 15%

profile of v1, /device:TPU:0, one launch (start us, length us, event | category | flops | bytes accessed | tf_op | source)
XLA Modules:
  0.0 346.4 jit_solution(936132292250018875)
XLA Ops:
  0.7 4.2 %concatenate.83 = bf16[864]{0:T(1024)(128)(2,1)S(1)} concatenate(bf16[96]{0:T(256)(128)(2,1)} %param.17, bf16[96]{0:T(256)(128)(2,1)} %param.18, bf16[96]{0:T(256)(128)(2,1)} %param.23, bf16[96]{0:T(256)(128)(2,1)} %param.24, bf16[96]{0:T(256)(128)(2,1)} %param.28, bf16[384]{0:T(512)(128)(2,1)} %param.26), dimensions={0} | concatenate | bytes 3456 | tf_op jit(solution)/shard_map/concatenate | solution.py:637
  6.2 4.1 %collective-permute-start = (bf16[1,112,768]{2,1,0:T(8,128)(2,1)S(1)}, bf16[1,112,768]{2,1,0:T(8,128)(2,1)S(1)}, u32[]{:S(2)}, u32[]{:S(2)}) collective-permute-start(bf16[1,112,768]{2,1,0:T(8,128)(2,1)S(1)} %fusion.37), channel_id=1, source_target_pairs={{0,4},{1,5},{2,6},{3,7},{4,0},{5,1},{6,2},{7,3},{8,12},{9,13},{10,... | collective-permute-start | bytes 516104 | tf_op jit(solution)/shard_map/ppermute | solution.py:68
  10.3 2.3 reshape.332
  14.1 2.9 collective-permute-start.20
  17.3 11.4 %collective-permute-done.10 = bf16[1,96,768]{2,1,0:T(8,128)(2,1)S(1)} collective-permute-done((bf16[1,96,768]{2,1,0:T(8,128)(2,1)S(1)}, bf16[1,96,768]{2,1,0:T(8,128)(2,1)S(1)}, u32[]{:S(2)}, u32[]{:S(2)}) %collective-permute-start.10) | collective-permute-done | bytes 147488 | tf_op jit(solution)/shard_map/ppermute | solution.py:68
  28.8 2.3 collective-permute-done.20
  33.4 5.2 %collective-permute-done.11 = bf16[2,96,768]{2,1,0:T(8,128)(2,1)S(1)} collective-permute-done((bf16[2,96,768]{2,1,0:T(8,128)(2,1)S(1)}, bf16[2,96,768]{2,1,0:T(8,128)(2,1)S(1)}, u32[]{:S(2)}, u32[]{:S(2)}) %collective-permute-start.11) | collective-permute-done | bytes 294944 | tf_op jit(solution)/shard_map/ppermute | solution.py:68
  38.7 1.9 collective-permute-start.12
  42.2 2.8 collective-permute-done.21
  45.0 1.9 collective-permute-start.22
  48.5 2.5 collective-permute-done.1
  56.7 16.0 %collective-permute-done.6 = bf16[4,48,768]{2,1,0:T(8,128)(2,1)S(1)} collective-permute-done((bf16[4,48,768]{2,1,0:T(8,128)(2,1)S(1)}, bf16[4,48,768]{2,1,0:T(8,128)(2,1)S(1)}, u32[]{:S(2)}, u32[]{:S(2)}) %collective-permute-start.6) | collective-permute-done | bytes 294944 | tf_op jit(solution)/shard_map/ppermute | solution.py:68
  72.7 4.4 %collective-permute-done.2 = bf16[4,64,768]{2,1,0:T(8,128)(2,1)S(1)} collective-permute-done((bf16[4,64,768]{2,1,0:T(8,128)(2,1)S(1)}, bf16[4,64,768]{2,1,0:T(8,128)(2,1)S(1)}, u32[]{:S(2)}, u32[]{:S(2)}) %collective-permute-start.2) | collective-permute-done | bytes 393248 | tf_op jit(solution)/shard_map/ppermute | solution.py:68
  80.3 11.7 %collective-permute-done.23.a1 = bf16[8,48,768]{2,1,0:T(8,128)(2,1)S(1)} collective-permute-done((bf16[8,48,768]{2,1,0:T(8,128)(2,1)S(1)}, bf16[8,48,768]{2,1,0:T(8,128)(2,1)S(1)}, u32[]{:S(2)}, u32[]{:S(2)}) %collective-permute-start.23) | collective-permute-done | bytes 589856 | tf_op jit(solution)/shard_map/ppermute | solution.py:68
  94.4 1.8 fusion.35
  96.3 9.7 %collective-permute-done.7.b1 = bf16[8,48,768]{2,1,0:T(8,128)(2,1)S(1)} collective-permute-done((bf16[8,48,768]{2,1,0:T(8,128)(2,1)S(1)}, bf16[8,48,768]{2,1,0:T(8,128)(2,1)S(1)}, u32[]{:S(2)}, u32[]{:S(2)}) %collective-permute-start.7) | collective-permute-done | bytes 589856 | tf_op jit(solution)/shard_map/ppermute | solution.py:68
  108.8 1.7 fusion.2.bias_ref
  111.2 5.8 %assemble.4 = bf16[4,8,2,48,768]{4,3,2,1,0:T(8,128)(2,1)} custom-call(s32[2]{0:T(128)} %pad_add_fusion.idx_ref, bf16[8,48,768]{2,1,0:T(8,128)(2,1)} %copy-done.7, bf16[8,48,768]{2,1,0:T(8,128)(2,1)} %copy-done.15, bf16[8,48,768]{2,1,0:T(8,128)(2,1)} %copy-done.16, bf16[8,48,768]{2,1,0:T(8,128)(2,1)} %copy-done.25, bf16[8,48,768]{2,1,0:T(8,128)(2,1)} %copy-done.8, ...), custom_call_target="tpu_custom_call" | custom-call | bytes 9437184 | tf_op jit(solution)/shard_map/assemble/pallas_call | solution.py:152
  117.1 5.8 %assemble.5 = bf16[4,8,2,48,768]{4,3,2,1,0:T(8,128)(2,1)} custom-call(s32[2]{0:T(128)} %pad_add_fusion.idx_ref, bf16[8,48,768]{2,1,0:T(8,128)(2,1)} %copy-done.9, bf16[8,48,768]{2,1,0:T(8,128)(2,1)} %copy-done.18, bf16[8,48,768]{2,1,0:T(8,128)(2,1)} %copy-done.20, bf16[8,48,768]{2,1,0:T(8,128)(2,1)} %copy-done.26, bf16[8,48,768]{2,1,0:T(8,128)(2,1)} %copy-done.10, ...), custom_call_target="tpu_custom_call" | custom-call | bytes 9437184 | tf_op jit(solution)/shard_map/assemble/pallas_call | solution.py:152
  122.9 5.7 %assemble.3 = bf16[4,8,2,48,768]{4,3,2,1,0:T(8,128)(2,1)} custom-call(s32[2]{0:T(128)} %pad_add_fusion.idx_ref, bf16[8,48,768]{2,1,0:T(8,128)(2,1)} %copy-done.12, bf16[8,48,768]{2,1,0:T(8,128)(2,1)} %copy-done.24, bf16[8,48,768]{2,1,0:T(8,128)(2,1)} %collective-permute-done.4.a2, bf16[8,48,768]{2,1,0:T(8,128)(2,1)} %collective-permute-done.5.a3, ...), custom_call_target="tpu_custom_call" | custom-call | bytes 9437184 | tf_op jit(solution)/shard_map/assemble/pallas_call | solution.py:152
  128.7 7.8 %qkv.1 = (bf16[512,768]{1,0:T(8,128)(2,1)}, bf16[3,512,768]{2,1,0:T(8,128)(2,1)}) custom-call(bf16[512,768]{1,0:T(8,128)(2,1)} %x_ref.5, f32[16,768]{1,0:T(8,128)} %add.243.small_ref, f32[512,128]{1,0:T(8,128)} %get-tuple-element.105.cos_ref, f32[512,128]{1,0:T(8,128)} %get-tuple-element.104.sin_ref, bf16[4,768,768]{2,1,0:T(8,128)(2,1)} %bitcast.176), custom_call_target="tpu_custom_call" | custom-call | flops 1811939328 | bytes 7471104 | tf_op jit(solution)/shard_map/qkv/pallas_call | solution.py:189
  136.5 10.4 %attend.1 = (bf16[512,768]{1,0:T(8,128)(2,1)}, bf16[12,512,512]{2,1,0:T(8,128)(2,1)}) custom-call(bf16[3,512,768]{2,1,0:T(8,128)(2,1)} %get-tuple-element.31.q_ref.k_ref.v_ref, bf16[3,512,768]{2,1,0:T(8,128)(2,1)} %get-tuple-element.31.q_ref.k_ref.v_ref, bf16[3,512,768]{2,1,0:T(8,128)(2,1)} %get-tuple-element.31.q_ref.k_ref.v_ref, f32[512,512]{1,0:T(8,128)} %fusion.2.bias_ref), custom_call_target="tpu_custom_call" | custom-call | flops 1610612736 | bytes 9437184 | tf_op jit(solution)/shard_map/attend/pallas_call | solution.py:235
  146.9 3.9 %branch.1 = (f32[512,768]{1,0:T(8,128)}, bf16[512,768]{1,0:T(8,128)(2,1)}) custom-call(bf16[512,768]{1,0:T(8,128)(2,1)} %x_ref.5, bf16[512,768]{1,0:T(8,128)(2,1)} %get-tuple-element.32.mixed_ref, bf16[4,768,768]{2,1,0:T(8,128)(2,1)} %bitcast.177, f32[16,768]{1,0:T(8,128)} %add.243.small_ref), custom_call_target="tpu_custom_call" | custom-call | flops 603979776 | bytes 5111808 | tf_op jit(solution)/shard_map/branch/pallas_call | solution.py:316
  150.9 8.8 %up.1 = (bf16[4,512,768]{2,1,0:T(8,128)(2,1)}, bf16[4,512,768]{2,1,0:T(8,128)(2,1)}) custom-call(bf16[512,768]{1,0:T(8,128)(2,1)} %get-tuple-element.33.hidden_ref, bf16[4,768,768]{2,1,0:T(8,128)(2,1)} %bitcast.185, f32[16,768]{1,0:T(8,128)} %add.243.small_ref), custom_call_target="tpu_custom_call" | custom-call | flops 2415919104 | bytes 11796480 | tf_op jit(solution)/shard_map/up/pallas_call | solution.py:353
  159.7 10.6 %act_grad.1 = (bf16[4,512,768]{2,1,0:T(8,128)(2,1)}, f32[16,768]{1,0:T(8,128)}, f32[512,768]{1,0:T(8,128)}) custom-call(bf16[512,768]{1,0:T(8,128)(2,1)} %c_ref.3, bf16[4,768,768]{2,1,0:T(8,128)(2,1)} %bitcast.180, bf16[4,768,768]{2,1,0:T(8,128)(2,1)} %bitcast.186, bf16[4,512,768]{2,1,0:T(8,128)(2,1)} %get-tuple-element.37.slope_ref), custom_call_target="tpu_custom_call" | custom-call | flops 4831838208 | bytes 18087936 | tf_op jit(solution)/shard_map/act_grad/pallas_call | solution.py:435
  170.2 4.9 %middle.1 = (f32[512,768]{1,0:T(8,128)}, bf16[512,768]{1,0:T(8,128)(2,1)}, bf16[512,768]{1,0:T(8,128)(2,1)}, f32[16,768]{1,0:T(8,128)}) custom-call(bf16[512,768]{1,0:T(8,128)(2,1)} %c_ref.3, f32[512,768]{1,0:T(8,128)} %get-tuple-element.38.hidden_ref, f32[512,768]{1,0:T(8,128)} %get-tuple-element.35.residual_ref, f32[16,768]{1,0:T(8,128)} %add.243.small_ref, ...), custom_call_target="tpu_custom_call" | custom-call | flops 603979776 | bytes 8257536 | tf_op jit(solution)/shard_map/middle/pallas_call | solution.py:481
  175.2 11.6 %attend_back.1.three_ref = bf16[3,512,768]{2,1,0:T(8,128)(2,1)} custom-call(bf16[3,512,768]{2,1,0:T(8,128)(2,1)} %get-tuple-element.31.q_ref.k_ref.v_ref, bf16[3,512,768]{2,1,0:T(8,128)(2,1)} %get-tuple-element.31.q_ref.k_ref.v_ref, bf16[3,512,768]{2,1,0:T(8,128)(2,1)} %get-tuple-element.31.q_ref.k_ref.v_ref, ...), custom_call_target="tpu_custom_call" | custom-call | flops 3221225472 | bytes 12582912 | tf_op jit(solution)/shard_map/attend_back/pallas_call | solution.py:285
  189.2 1.9 pad_maximum_fusion.y_ref
  191.1 4.9 %weight_grad.7 = bf16[2,2,8,48,768]{4,3,2,1,0:T(8,128)(2,1)} custom-call(s32[2]{0:T(128)} %pad_add_fusion.idx_ref, bf16[2,512,768]{2,1,0:T(8,128)(2,1)} %pad_maximum_fusion.1.x_ref, bf16[4,512,768]{2,1,0:T(8,128)(2,1)} %pad_maximum_fusion.y_ref), custom_call_target="tpu_custom_call" | custom-call | flops 1207959552 | bytes 5505024 | tf_op jit(solution)/shard_map/weight_grad/pallas_call | solution.py:392
  196.2 4.9 %weight_grad.9 = bf16[2,2,8,48,768]{4,3,2,1,0:T(8,128)(2,1)} custom-call(s32[2]{0:T(128)} %pad_add_fusion.idx_ref, bf16[1,512,768]{2,1,0:T(8,128)(2,1)} %bitcast.187, bf16[4,512,768]{2,1,0:T(8,128)(2,1)} %get-tuple-element.47.y_ref), custom_call_target="tpu_custom_call" | custom-call | flops 1207959552 | bytes 5505024 | tf_op jit(solution)/shard_map/weight_grad/pallas_call | solution.py:392
  201.5 4.9 %weight_grad.11 = bf16[2,2,8,48,768]{4,3,2,1,0:T(8,128)(2,1)} custom-call(s32[2]{0:T(128)} %pad_add_fusion.idx_ref, bf16[4,512,768]{2,1,0:T(8,128)(2,1)} %get-tuple-element.34.act_ref.x_ref, bf16[1,512,768]{2,1,0:T(8,128)(2,1)} %bitcast.183), custom_call_target="tpu_custom_call" | custom-call | flops 1207959552 | bytes 5505024 | tf_op jit(solution)/shard_map/weight_grad/pallas_call | solution.py:392
  206.6 7.9 %input_grads.1 = (f32[512,768]{1,0:T(8,128)}, f32[16,768]{1,0:T(8,128)}) custom-call(bf16[512,768]{1,0:T(8,128)(2,1)} %x_ref.5, bf16[3,512,768]{2,1,0:T(8,128)(2,1)} %attend_back.1.three_ref, bf16[4,768,768]{2,1,0:T(8,128)(2,1)} %bitcast.179, f32[16,768]{1,0:T(8,128)} %add.243.small_ref, f32[512,768]{1,0:T(8,128)} %get-tuple-element.40.grad_ref), custom_call_target="tpu_custom_call" | custom-call | flops 1811939328 | bytes 9830400 | tf_op jit(solution)/shard_map/input_grads/pallas_call | solution.py:533
  215.8 4.9 %weight_grad.6 = bf16[2,2,8,48,768]{4,3,2,1,0:T(8,128)(2,1)} custom-call(s32[2]{0:T(128)} %pad_add_fusion.idx_ref, bf16[2,512,768]{2,1,0:T(8,128)(2,1)} %pad_maximum_fusion.1.x_ref, bf16[4,512,768]{2,1,0:T(8,128)(2,1)} %pad_maximum_fusion.y_ref), custom_call_target="tpu_custom_call" | custom-call | flops 1207959552 | bytes 5505024 | tf_op jit(solution)/shard_map/weight_grad/pallas_call | solution.py:392
  220.7 5.1 %weight_grad.8 = bf16[2,2,8,48,768]{4,3,2,1,0:T(8,128)(2,1)} custom-call(s32[2]{0:T(128)} %pad_add_fusion.idx_ref, bf16[1,512,768]{2,1,0:T(8,128)(2,1)} %bitcast.188, bf16[4,512,768]{2,1,0:T(8,128)(2,1)} %get-tuple-element.47.y_ref), custom_call_target="tpu_custom_call" | custom-call | flops 1207959552 | bytes 5505024 | tf_op jit(solution)/shard_map/weight_grad/pallas_call | solution.py:392
  225.8 7.5 %down_out.1 = bf16[512,768]{1,0:T(8,128)(2,1)} custom-call(bf16[4,512,768]{2,1,0:T(8,128)(2,1)} %get-tuple-element.34.act_ref.x_ref, bf16[4,768,768]{2,1,0:T(8,128)(2,1)} %bitcast.181, f32[16,768]{1,0:T(8,128)} %add.243.small_ref, f32[512,768]{1,0:T(8,128)} %get-tuple-element.35.residual_ref), custom_call_target="tpu_custom_call" | custom-call | flops 2415919104 | bytes 10223616 | tf_op jit(solution)/shard_map/down_out/pallas_call | solution.py:574
  233.3 5.0 %weight_grad.10 = bf16[2,2,8,48,768]{4,3,2,1,0:T(8,128)(2,1)} custom-call(s32[2]{0:T(128)} %pad_add_fusion.idx_ref, bf16[4,512,768]{2,1,0:T(8,128)(2,1)} %get-tuple-element.34.act_ref.x_ref, bf16[1,512,768]{2,1,0:T(8,128)(2,1)} %bitcast.184), custom_call_target="tpu_custom_call" | custom-call | flops 1207959552 | bytes 5505024 | tf_op jit(solution)/shard_map/weight_grad/pallas_call | solution.py:392
  250.3 8.8 %collective-permute-done.34 = bf16[2,4,48,768]{3,2,1,0:T(8,128)(2,1)S(1)} collective-permute-done((bf16[2,4,48,768]{3,2,1,0:T(8,128)(2,1)S(1)}, bf16[2,4,48,768]{3,2,1,0:T(8,128)(2,1)S(1)}, u32[]{:S(2)}, u32[]{:S(2)}) %collective-permute-start.34) | collective-permute-done | bytes 589856 | tf_op jit(solution)/shard_map/ppermute | solution.py:68
  259.6 12.0 %collective-permute-done.44 = bf16[2,4,48,768]{3,2,1,0:T(8,128)(2,1)S(1)} collective-permute-done((bf16[2,4,48,768]{3,2,1,0:T(8,128)(2,1)S(1)}, bf16[2,4,48,768]{3,2,1,0:T(8,128)(2,1)S(1)}, u32[]{:S(2)}, u32[]{:S(2)}) %collective-permute-start.44) | collective-permute-done | bytes 589856 | tf_op jit(solution)/shard_map/ppermute | solution.py:68
  273.8 9.4 %collective-permute-done.54 = bf16[2,4,48,768]{3,2,1,0:T(8,128)(2,1)S(1)} collective-permute-done((bf16[2,4,48,768]{3,2,1,0:T(8,128)(2,1)S(1)}, bf16[2,4,48,768]{3,2,1,0:T(8,128)(2,1)S(1)}, u32[]{:S(2)}, u32[]{:S(2)}) %collective-permute-start.54) | collective-permute-done | bytes 589856 | tf_op jit(solution)/shard_map/ppermute | solution.py:68
  286.2 8.2 %collective-permute-done.45 = bf16[4,48,768]{2,1,0:T(8,128)(2,1)S(1)} collective-permute-done((bf16[4,48,768]{2,1,0:T(8,128)(2,1)S(1)}, bf16[4,48,768]{2,1,0:T(8,128)(2,1)S(1)}, u32[]{:S(2)}, u32[]{:S(2)}) %collective-permute-start.45) | collective-permute-done | bytes 294944 | tf_op jit(solution)/shard_map/ppermute | solution.py:68
  296.5 3.5 %collective-permute-done.55 = bf16[4,48,768]{2,1,0:T(8,128)(2,1)S(1)} collective-permute-done((bf16[4,48,768]{2,1,0:T(8,128)(2,1)S(1)}, bf16[4,48,768]{2,1,0:T(8,128)(2,1)S(1)}, u32[]{:S(2)}, u32[]{:S(2)}) %collective-permute-start.55) | collective-permute-done | bytes 294944 | tf_op jit(solution)/shard_map/ppermute | solution.py:68
  300.5 3.8 %collective-permute-done.33 = bf16[208,768]{1,0:T(8,128)(2,1)S(1)} collective-permute-done((bf16[208,768]{1,0:T(8,128)(2,1)S(1)}, bf16[208,768]{1,0:T(8,128)(2,1)S(1)}, u32[]{:S(2)}, u32[]{:S(2)}) %collective-permute-start.33) | collective-permute-done | bytes 319520 | tf_op jit(solution)/shard_map/ppermute | solution.py:68
  304.8 3.9 %collective-permute-start.47 = (bf16[1,2,48,768]{3,2,0,1:T(8,128)(2,1)S(1)}, bf16[1,2,48,768]{3,2,0,1:T(8,128)(2,1)S(1)}, u32[]{:S(2)}, u32[]{:S(2)}) collective-permute-start(bf16[1,2,48,768]{3,2,0,1:T(8,128)(2,1)S(1)} %slice.496), channel_id=1, source_target_pairs={{0,4},{1,5},{2,6},{3,7},{4,0},{5,1},{6,2},{7,3},{8,12},{9,13},{10,... | collective-permute-start | bytes 442376 | tf_op jit(solution)/shard_map/ppermute | solution.py:68
  308.7 5.4 %collective-permute-done.56 = bf16[2,2,48,768]{3,2,0,1:T(8,128)(2,1)S(1)} collective-permute-done((bf16[2,2,48,768]{3,2,0,1:T(8,128)(2,1)S(1)}, bf16[2,2,48,768]{3,2,0,1:T(8,128)(2,1)S(1)}, u32[]{:S(2)}, u32[]{:S(2)}) %collective-permute-start.56) | collective-permute-done | bytes 294944 | tf_op jit(solution)/shard_map/ppermute | solution.py:68
  315.8 6.0 %collective-permute-done.36 = bf16[208,768]{1,0:T(8,128)(2,1)S(1)} collective-permute-done((bf16[208,768]{1,0:T(8,128)(2,1)S(1)}, bf16[208,768]{1,0:T(8,128)(2,1)S(1)}, u32[]{:S(2)}, u32[]{:S(2)}) %collective-permute-start.36) | collective-permute-done | bytes 319520 | tf_op jit(solution)/shard_map/ppermute | solution.py:68
  323.7 6.9 %collective-permute-done.57 = bf16[1,2,48,768]{3,2,0,1:T(8,128)(2,1)S(1)} collective-permute-done((bf16[1,2,48,768]{3,2,0,1:T(8,128)(2,1)S(1)}, bf16[1,2,48,768]{3,2,0,1:T(8,128)(2,1)S(1)}, u32[]{:S(2)}, u32[]{:S(2)}) %collective-permute-start.57) | collective-permute-done | bytes 147488 | tf_op jit(solution)/shard_map/ppermute | solution.py:68
  336.6 2.3 collective-permute-done.39
  341.6 2.6 reshape.352
  (271 shorter events, 62.6 us)
Async XLA Ops:
  6.2 25.7 %collective-permute-start = (bf16[1,112,768]{2,1,0:T(8,128)(2,1)S(1)}, bf16[1,112,768]{2,1,0:T(8,128)(2,1)S(1)}, u32[]{:S(2)}, u32[]{:S(2)}) collective-permute-start(bf16[1,112,768]{2,1,0:T(8,128)(2,1)S(1)} %fusion.37), channel_id=1, source_target_pairs={{0,4},{1,5},{2,6},{3,7},{4,0},{5,1},{6,2},{7,3},{8,12},{9,13},{10,... | collective-permute-start | bytes 516104 | tf_op jit(solution)/shard_map/ppermute | solution.py:68
  14.0 14.7 %collective-permute-start.10 = (bf16[1,96,768]{2,1,0:T(8,128)(2,1)S(1)}, bf16[1,96,768]{2,1,0:T(8,128)(2,1)S(1)}, u32[]{:S(2)}, u32[]{:S(2)}) collective-permute-start(bf16[1,96,768]{2,1,0:T(8,128)(2,1)S(1)} %broadcast_in_dim_reshape.3), channel_id=1, source_target_pairs={{0,4},{1,5},{2,6},{3,7},{4,0},{5,1},{6,2},{7,3},{8,12},{9,13},{10,... | collective-permute-start | bytes 442376 | tf_op jit(solution)/shard_map/ppermute | solution.py:68
  14.1 17.0 %collective-permute-start.20 = (bf16[1,96,768]{2,1,0:T(8,128)(2,1)S(1)}, bf16[1,96,768]{2,1,0:T(8,128)(2,1)S(1)}, u32[]{:S(2)}, u32[]{:S(2)}) collective-permute-start(bf16[1,96,768]{2,1,0:T(8,128)(2,1)S(1)} %dynamic-slice_bitcast_fusion.4), channel_id=1, source_target_pairs={{0,4},{1,5},{2,6},{3,7},{4,0},{5,1},{6,2},{7,3},{8,12},{9,13},{10,... | collective-permute-start | bytes 442376 | tf_op jit(solution)/shard_map/ppermute | solution.py:68
  31.1 13.8 %collective-permute-start.21 = (bf16[2,96,768]{2,1,0:T(8,128)(2,1)S(1)}, bf16[2,96,768]{2,1,0:T(8,128)(2,1)S(1)}, u32[]{:S(2)}, u32[]{:S(2)}) collective-permute-start(bf16[2,96,768]{2,1,0:T(8,128)(2,1)S(1)} %pad_maximum_fusion.13), channel_id=1, source_target_pairs={{0,2},{1,3},{2,0},{3,1},{4,6},{5,7},{6,4},{7,5},{8,10},{9,11},{10,... | collective-permute-start | bytes 884744 | tf_op jit(solution)/shard_map/ppermute | solution.py:68
  31.9 19.1 %collective-permute-start.1 = (bf16[2,112,768]{2,1,0:T(8,128)(2,1)S(1)}, bf16[2,112,768]{2,1,0:T(8,128)(2,1)S(1)}, u32[]{:S(2)}, u32[]{:S(2)}) collective-permute-start(bf16[2,112,768]{2,1,0:T(8,128)(2,1)S(1)} %pad_maximum_fusion.12), channel_id=1, source_target_pairs={{0,2},{1,3},{2,0},{3,1},{4,6},{5,7},{6,4},{7,5},{8,10},{9,11},{10,... | collective-permute-start | bytes 1032200 | tf_op jit(solution)/shard_map/ppermute | solution.py:68
  38.7 12.4 %collective-permute-start.12 = (bf16[4,48,768]{2,1,0:T(8,128)(2,1)S(1)}, bf16[4,48,768]{2,1,0:T(8,128)(2,1)S(1)}, u32[]{:S(2)}, u32[]{:S(2)}) collective-permute-start(bf16[4,48,768]{2,1,0:T(8,128)(2,1)S(1)} %pad_maximum_fusion.20), channel_id=1, source_target_pairs={{0,1},{1,0},{2,3},{3,2},{4,5},{5,4},{6,7},{7,6},{8,9},{9,8},{10,11... | collective-permute-start | bytes 884744 | tf_op jit(solution)/shard_map/ppermute | solution.py:68
  40.6 12.2 %collective-permute-start.16 = (bf16[4,48,768]{2,1,0:T(8,128)(2,1)S(1)}, bf16[4,48,768]{2,1,0:T(8,128)(2,1)S(1)}, u32[]{:S(2)}, u32[]{:S(2)}) collective-permute-start(bf16[4,48,768]{2,1,0:T(8,128)(2,1)S(1)} %pad_maximum_fusion.21), channel_id=1, source_target_pairs={{0,16},{8,24},{16,0},{24,8},{1,17},{9,25},{17,1},{25,9},{2,18},{10... | collective-permute-start | bytes 884744 | tf_op jit(solution)/shard_map/ppermute | solution.py:68
  51.2 26.4 %collective-permute-start.13 = (bf16[8,48,768]{2,1,0:T(8,128)(2,1)S(1)}, bf16[8,48,768]{2,1,0:T(8,128)(2,1)S(1)}, u32[]{:S(2)}, u32[]{:S(2)}) collective-permute-start(bf16[8,48,768]{2,1,0:T(8,128)(2,1)S(1)} %pad_maximum_fusion.5.a0), channel_id=1, source_target_pairs={{0,16},{8,24},{16,0},{24,8},{1,17},{9,25},{17,1},{25,9},{2,18},{10... | collective-permute-start | bytes 1769480 | tf_op jit(solution)/shard_map/ppermute | solution.py:68
  52.8 24.8 %collective-permute-start.14 = (bf16[8,48,768]{2,1,0:T(8,128)(2,1)S(1)}, bf16[8,48,768]{2,1,0:T(8,128)(2,1)S(1)}, u32[]{:S(2)}, u32[]{:S(2)}) collective-permute-start(bf16[8,48,768]{2,1,0:T(8,128)(2,1)S(1)} %pad_maximum_fusion.5.a0), channel_id=1, source_target_pairs={{0,8},{8,0},{16,24},{24,16},{1,9},{9,1},{17,25},{25,17},{2,10},{10... | collective-permute-start | bytes 1769480 | tf_op jit(solution)/shard_map/ppermute | solution.py:68
  52.9 26.4 %collective-permute-start.17 = (bf16[8,48,768]{2,1,0:T(8,128)(2,1)S(1)}, bf16[8,48,768]{2,1,0:T(8,128)(2,1)S(1)}, u32[]{:S(2)}, u32[]{:S(2)}) collective-permute-start(bf16[8,48,768]{2,1,0:T(8,128)(2,1)S(1)} %pad_maximum_fusion.6.b0), channel_id=1, source_target_pairs={{0,1},{1,0},{2,3},{3,2},{4,5},{5,4},{6,7},{7,6},{8,9},{9,8},{10,11... | collective-permute-start | bytes 1769480 | tf_op jit(solution)/shard_map/ppermute | solution.py:68
  54.5 22.6 %collective-permute-start.2 = (bf16[4,64,768]{2,1,0:T(8,128)(2,1)S(1)}, bf16[4,64,768]{2,1,0:T(8,128)(2,1)S(1)}, u32[]{:S(2)}, u32[]{:S(2)}) collective-permute-start(bf16[4,64,768]{2,1,0:T(8,128)(2,1)S(1)} %maximum_maximum_fusion), channel_id=1, source_target_pairs={{0,1},{1,0},{2,3},{3,2},{4,5},{5,4},{6,7},{7,6},{8,9},{9,8},{10,11... | collective-permute-start | bytes 1179656 | tf_op jit(solution)/shard_map/ppermute | solution.py:68
  55.1 17.6 %collective-permute-start.6 = (bf16[4,48,768]{2,1,0:T(8,128)(2,1)S(1)}, bf16[4,48,768]{2,1,0:T(8,128)(2,1)S(1)}, u32[]{:S(2)}, u32[]{:S(2)}) collective-permute-start(bf16[4,48,768]{2,1,0:T(8,128)(2,1)S(1)} %pad_maximum_fusion.19), channel_id=1, source_target_pairs={{0,16},{8,24},{16,0},{24,8},{1,17},{9,25},{17,1},{25,9},{2,18},{10... | collective-permute-start | bytes 884744 | tf_op jit(solution)/shard_map/ppermute | solution.py:68
  77.1 14.9 %collective-permute-start.23 = (bf16[8,48,768]{2,1,0:T(8,128)(2,1)S(1)}, bf16[8,48,768]{2,1,0:T(8,128)(2,1)S(1)}, u32[]{:S(2)}, u32[]{:S(2)}) collective-permute-start(bf16[8,48,768]{2,1,0:T(8,128)(2,1)S(1)} %pad_maximum_fusion.7.a0), channel_id=1, source_target_pairs={{0,16},{8,24},{16,0},{24,8},{1,17},{9,25},{17,1},{25,9},{2,18},{10... | collective-permute-start | bytes 1769480 | tf_op jit(solution)/shard_map/ppermute | solution.py:68
  77.6 14.9 %collective-permute-start.24 = (bf16[8,48,768]{2,1,0:T(8,128)(2,1)S(1)}, bf16[8,48,768]{2,1,0:T(8,128)(2,1)S(1)}, u32[]{:S(2)}, u32[]{:S(2)}) collective-permute-start(bf16[8,48,768]{2,1,0:T(8,128)(2,1)S(1)} %pad_maximum_fusion.7.a0), channel_id=1, source_target_pairs={{0,8},{8,0},{16,24},{24,16},{1,9},{9,1},{17,25},{25,17},{2,10},{10... | collective-permute-start | bytes 1769480 | tf_op jit(solution)/shard_map/ppermute | solution.py:68
  77.6 16.3 %collective-permute-start.27 = (bf16[8,48,768]{2,1,0:T(8,128)(2,1)S(1)}, bf16[8,48,768]{2,1,0:T(8,128)(2,1)S(1)}, u32[]{:S(2)}, u32[]{:S(2)}) collective-permute-start(bf16[8,48,768]{2,1,0:T(8,128)(2,1)S(1)} %pad_maximum_fusion.8.b0), channel_id=1, source_target_pairs={{0,1},{1,0},{2,3},{3,2},{4,5},{5,4},{6,7},{7,6},{8,9},{9,8},{10,11... | collective-permute-start | bytes 1769480 | tf_op jit(solution)/shard_map/ppermute | solution.py:68
  79.2 14.6 %collective-permute-start.28 = (bf16[8,48,768]{2,1,0:T(8,128)(2,1)S(1)}, bf16[8,48,768]{2,1,0:T(8,128)(2,1)S(1)}, u32[]{:S(2)}, u32[]{:S(2)}) collective-permute-start(bf16[8,48,768]{2,1,0:T(8,128)(2,1)S(1)} %pad_maximum_fusion.8.b0), channel_id=1, source_target_pairs={{0,8},{8,0},{16,24},{24,16},{1,9},{9,1},{17,25},{25,17},{2,10},{10... | collective-permute-start | bytes 1769480 | tf_op jit(solution)/shard_map/ppermute | solution.py:68
  79.8 26.2 %collective-permute-start.7 = (bf16[8,48,768]{2,1,0:T(8,128)(2,1)S(1)}, bf16[8,48,768]{2,1,0:T(8,128)(2,1)S(1)}, u32[]{:S(2)}, u32[]{:S(2)}) collective-permute-start(bf16[8,48,768]{2,1,0:T(8,128)(2,1)S(1)} %pad_maximum_fusion.4.b0), channel_id=1, source_target_pairs={{0,1},{1,0},{2,3},{3,2},{4,5},{5,4},{6,7},{7,6},{8,9},{9,8},{10,11... | collective-permute-start | bytes 1769480 | tf_op jit(solution)/shard_map/ppermute | solution.py:68
  92.0 14.0 %collective-permute-start.3 = (bf16[8,48,768]{2,1,0:T(8,128)(2,1)S(1)}, bf16[8,48,768]{2,1,0:T(8,128)(2,1)S(1)}, u32[]{:S(2)}, u32[]{:S(2)}) collective-permute-start(bf16[8,48,768]{2,1,0:T(8,128)(2,1)S(1)} %pad_maximum_fusion.3.a0), channel_id=1, source_target_pairs={{0,16},{8,24},{16,0},{24,8},{1,17},{9,25},{17,1},{25,9},{2,18},{10... | collective-permute-start | bytes 1769480 | tf_op jit(solution)/shard_map/ppermute | solution.py:68
  92.5 14.0 %collective-permute-start.15 = (bf16[8,48,768]{2,1,0:T(8,128)(2,1)S(1)}, bf16[8,48,768]{2,1,0:T(8,128)(2,1)S(1)}, u32[]{:S(2)}, u32[]{:S(2)}) collective-permute-start(bf16[8,48,768]{2,1,0:T(8,128)(2,1)S(1)} %collective-permute-done.13.a1), channel_id=1, source_target_pairs={{0,8},{8,0},{16,24},{24,16},{1,9},{9,1},{17,25},{25,17},{2,10},{10... | collective-permute-start | bytes 1769480 | tf_op jit(solution)/shard_map/ppermute | solution.py:68
  93.9 12.7 %collective-permute-start.19 = (bf16[8,48,768]{2,1,0:T(8,128)(2,1)S(1)}, bf16[8,48,768]{2,1,0:T(8,128)(2,1)S(1)}, u32[]{:S(2)}, u32[]{:S(2)}) collective-permute-start(bf16[8,48,768]{2,1,0:T(8,128)(2,1)S(1)} %collective-permute-done.17.b1), channel_id=1, source_target_pairs={{0,8},{8,0},{16,24},{24,16},{1,9},{9,1},{17,25},{25,17},{2,10},{10... | collective-permute-start | bytes 1769480 | tf_op jit(solution)/shard_map/ppermute | solution.py:68
  93.9 13.1 %collective-permute-start.25 = (bf16[8,48,768]{2,1,0:T(8,128)(2,1)S(1)}, bf16[8,48,768]{2,1,0:T(8,128)(2,1)S(1)}, u32[]{:S(2)}, u32[]{:S(2)}) collective-permute-start(bf16[8,48,768]{2,1,0:T(8,128)(2,1)S(1)} %collective-permute-done.23.a1), channel_id=1, source_target_pairs={{0,8},{8,0},{16,24},{24,16},{1,9},{9,1},{17,25},{25,17},{2,10},{10... | collective-permute-start | bytes 1769480 | tf_op jit(solution)/shard_map/ppermute | solution.py:68
  106.0 16.9 %collective-permute-start.8 = (bf16[8,48,768]{2,1,0:T(8,128)(2,1)S(1)}, bf16[8,48,768]{2,1,0:T(8,128)(2,1)}, u32[]{:S(2)}, u32[]{:S(2)}) collective-permute-start(bf16[8,48,768]{2,1,0:T(8,128)(2,1)S(1)} %pad_maximum_fusion.4.b0), channel_id=1, source_target_pairs={{0,8},{8,0},{16,24},{24,16},{1,9},{9,1},{17,25},{25,17},{2,10},{10... | collective-permute-start | bytes 1769480 | tf_op jit(solution)/shard_map/ppermute | solution.py:68
  106.0 16.9 %collective-permute-start.4 = (bf16[8,48,768]{2,1,0:T(8,128)(2,1)S(1)}, bf16[8,48,768]{2,1,0:T(8,128)(2,1)}, u32[]{:S(2)}, u32[]{:S(2)}) collective-permute-start(bf16[8,48,768]{2,1,0:T(8,128)(2,1)S(1)} %pad_maximum_fusion.3.a0), channel_id=1, source_target_pairs={{0,8},{8,0},{16,24},{24,16},{1,9},{9,1},{17,25},{25,17},{2,10},{10... | collective-permute-start | bytes 1769480 | tf_op jit(solution)/shard_map/ppermute | solution.py:68
  106.5 10.6 %collective-permute-start.29 = (bf16[8,48,768]{2,1,0:T(8,128)(2,1)S(1)}, bf16[8,48,768]{2,1,0:T(8,128)(2,1)}, u32[]{:S(2)}, u32[]{:S(2)}) collective-permute-start(bf16[8,48,768]{2,1,0:T(8,128)(2,1)S(1)} %collective-permute-done.27.b1), channel_id=1, source_target_pairs={{0,8},{8,0},{16,24},{24,16},{1,9},{9,1},{17,25},{25,17},{2,10},{10... | collective-permute-start | bytes 1769480 | tf_op jit(solution)/shard_map/ppermute | solution.py:68
  106.6 16.3 %collective-permute-start.9 = (bf16[8,48,768]{2,1,0:T(8,128)(2,1)S(1)}, bf16[8,48,768]{2,1,0:T(8,128)(2,1)}, u32[]{:S(2)}, u32[]{:S(2)}) collective-permute-start(bf16[8,48,768]{2,1,0:T(8,128)(2,1)S(1)} %collective-permute-done.7.b1), channel_id=1, source_target_pairs={{0,8},{8,0},{16,24},{24,16},{1,9},{9,1},{17,25},{25,17},{2,10},{10... | collective-permute-start | bytes 1769480 | tf_op jit(solution)/shard_map/ppermute | solution.py:68
  107.3 15.6 %collective-permute-start.5 = (bf16[8,48,768]{2,1,0:T(8,128)(2,1)S(1)}, bf16[8,48,768]{2,1,0:T(8,128)(2,1)}, u32[]{:S(2)}, u32[]{:S(2)}) collective-permute-start(bf16[8,48,768]{2,1,0:T(8,128)(2,1)S(1)} %collective-permute-done.3.a1), channel_id=1, source_target_pairs={{0,8},{8,0},{16,24},{24,16},{1,9},{9,1},{17,25},{25,17},{2,10},{10... | collective-permute-start | bytes 1769480 | tf_op jit(solution)/shard_map/ppermute | solution.py:68
  196.1 42.2 %collective-permute-start.31 = (bf16[2,2,8,48,768]{4,3,2,1,0:T(8,128)(2,1)}, bf16[2,2,8,48,768]{4,3,2,1,0:T(8,128)(2,1)}, u32[]{:S(2)}, u32[]{:S(2)}) collective-permute-start(bf16[2,2,8,48,768]{4,3,2,1,0:T(8,128)(2,1)} %weight_grad.7), channel_id=1, source_target_pairs={{0,8},{8,0},{16,24},{24,16},{1,9},{9,1},{17,25},{25,17},{2,10},{10... | collective-permute-start | bytes 7077896 | tf_op jit(solution)/shard_map/ppermute | solution.py:68
  201.2 43.2 %collective-permute-start.41 = (bf16[2,2,8,48,768]{4,3,2,1,0:T(8,128)(2,1)}, bf16[2,2,8,48,768]{4,3,2,1,0:T(8,128)(2,1)S(1)}, u32[]{:S(2)}, u32[]{:S(2)}) collective-permute-start(bf16[2,2,8,48,768]{4,3,2,1,0:T(8,128)(2,1)} %weight_grad.9), channel_id=1, source_target_pairs={{0,8},{8,0},{16,24},{24,16},{1,9},{9,1},{17,25},{25,17},{2,10},{10... | collective-permute-start | bytes 7077896 | tf_op jit(solution)/shard_map/ppermute | solution.py:68
  206.4 39.4 %collective-permute-start.51 = (bf16[2,2,8,48,768]{4,3,2,1,0:T(8,128)(2,1)}, bf16[2,2,8,48,768]{4,3,2,1,0:T(8,128)(2,1)}, u32[]{:S(2)}, u32[]{:S(2)}) collective-permute-start(bf16[2,2,8,48,768]{4,3,2,1,0:T(8,128)(2,1)} %weight_grad.11), channel_id=1, source_target_pairs={{0,8},{8,0},{16,24},{24,16},{1,9},{9,1},{17,25},{25,17},{2,10},{10... | collective-permute-start | bytes 7077896 | tf_op jit(solution)/shard_map/ppermute | solution.py:68
  215.3 23.0 %collective-permute-start.30 = (bf16[16,768]{1,0:T(8,128)(2,1)S(1)}, bf16[16,768]{1,0:T(8,128)(2,1)S(1)}, u32[]{:S(2)}, u32[]{:S(2)}) collective-permute-start(bf16[16,768]{1,0:T(8,128)(2,1)S(1)} %get-tuple-element.53), channel_id=1, source_target_pairs={{0,8},{8,0},{16,24},{24,16},{1,9},{9,1},{17,25},{25,17},{2,10},{10... | collective-permute-start | bytes 73736 | tf_op jit(solution)/shard_map/ppermute | solution.py:68
  239.8 45.8 %collective-permute-start.32 = (bf16[400,768]{1,0:T(8,128)(2,1)S(1)}, bf16[400,768]{1,0:T(8,128)(2,1)S(1)}, u32[]{:S(2)}, u32[]{:S(2)}) collective-permute-start(bf16[400,768]{1,0:T(8,128)(2,1)S(1)} %pad_maximum_fusion.2), channel_id=1, source_target_pairs={{0,16},{8,24},{16,0},{24,8},{1,17},{9,25},{17,1},{25,9},{2,18},{10... | collective-permute-start | bytes 1843208 | tf_op jit(solution)/shard_map/ppermute | solution.py:68
  242.8 16.3 %collective-permute-start.34 = (bf16[2,4,48,768]{3,2,1,0:T(8,128)(2,1)S(1)}, bf16[2,4,48,768]{3,2,1,0:T(8,128)(2,1)S(1)}, u32[]{:S(2)}, u32[]{:S(2)}) collective-permute-start(bf16[2,4,48,768]{3,2,1,0:T(8,128)(2,1)S(1)} %get-tuple-element.68), channel_id=1, source_target_pairs={{0,1},{1,0},{2,3},{3,2},{4,5},{5,4},{6,7},{7,6},{8,9},{9,8},{10,11... | collective-permute-start | bytes 1769480 | tf_op jit(solution)/shard_map/ppermute | solution.py:68
  244.5 27.2 %collective-permute-start.44 = (bf16[2,4,48,768]{3,2,1,0:T(8,128)(2,1)S(1)}, bf16[2,4,48,768]{3,2,1,0:T(8,128)(2,1)S(1)}, u32[]{:S(2)}, u32[]{:S(2)}) collective-permute-start(bf16[2,4,48,768]{3,2,1,0:T(8,128)(2,1)S(1)} %get-tuple-element.66), channel_id=1, source_target_pairs={{0,1},{1,0},{2,3},{3,2},{4,5},{5,4},{6,7},{7,6},{8,9},{9,8},{10,11... | collective-permute-start | bytes 1769480 | tf_op jit(solution)/shard_map/ppermute | solution.py:68
  245.2 27.1 %collective-permute-start.42 = (bf16[8,48,768]{2,1,0:T(8,128)(2,1)S(1)}, bf16[8,48,768]{2,1,0:T(8,128)(2,1)S(1)}, u32[]{:S(2)}, u32[]{:S(2)}) collective-permute-start(bf16[8,48,768]{2,1,0:T(8,128)(2,1)S(1)} %get-tuple-element.64), channel_id=1, source_target_pairs={{0,16},{8,24},{16,0},{24,8},{1,17},{9,25},{17,1},{25,9},{2,18},{10... | collective-permute-start | bytes 1769480 | tf_op jit(solution)/shard_map/ppermute | solution.py:68
  247.6 35.6 %collective-permute-start.54 = (bf16[2,4,48,768]{3,2,1,0:T(8,128)(2,1)S(1)}, bf16[2,4,48,768]{3,2,1,0:T(8,128)(2,1)S(1)}, u32[]{:S(2)}, u32[]{:S(2)}) collective-permute-start(bf16[2,4,48,768]{3,2,1,0:T(8,128)(2,1)S(1)} %get-tuple-element.62), channel_id=1, source_target_pairs={{0,1},{1,0},{2,3},{3,2},{4,5},{5,4},{6,7},{7,6},{8,9},{9,8},{10,11... | collective-permute-start | bytes 1769480 | tf_op jit(solution)/shard_map/ppermute | solution.py:68
  259.0 25.7 %collective-permute-start.52 = (bf16[8,48,768]{2,1,0:T(8,128)(2,1)S(1)}, bf16[8,48,768]{2,1,0:T(8,128)(2,1)S(1)}, u32[]{:S(2)}, u32[]{:S(2)}) collective-permute-start(bf16[8,48,768]{2,1,0:T(8,128)(2,1)S(1)} %get-tuple-element.60), channel_id=1, source_target_pairs={{0,16},{8,24},{16,0},{24,8},{1,17},{9,25},{17,1},{25,9},{2,18},{10... | collective-permute-start | bytes 1769480 | tf_op jit(solution)/shard_map/ppermute | solution.py:68
  271.7 28.8 %collective-permute-start.35 = (bf16[4,48,768]{2,1,0:T(8,128)(2,1)S(1)}, bf16[4,48,768]{2,1,0:T(8,128)(2,1)S(1)}, u32[]{:S(2)}, u32[]{:S(2)}) collective-permute-start(bf16[4,48,768]{2,1,0:T(8,128)(2,1)S(1)} %fusion.27), channel_id=1, source_target_pairs={{0,16},{8,24},{16,0},{24,8},{1,17},{9,25},{17,1},{25,9},{2,18},{10... | collective-permute-start | bytes 884744 | tf_op jit(solution)/shard_map/ppermute | solution.py:68
  272.3 22.2 %collective-permute-start.45 = (bf16[4,48,768]{2,1,0:T(8,128)(2,1)S(1)}, bf16[4,48,768]{2,1,0:T(8,128)(2,1)S(1)}, u32[]{:S(2)}, u32[]{:S(2)}) collective-permute-start(bf16[4,48,768]{2,1,0:T(8,128)(2,1)S(1)} %fusion.20), channel_id=1, source_target_pairs={{0,16},{8,24},{16,0},{24,8},{1,17},{9,25},{17,1},{25,9},{2,18},{10... | collective-permute-start | bytes 884744 | tf_op jit(solution)/shard_map/ppermute | solution.py:68
  283.2 12.9 %collective-permute-start.43 = (bf16[4,48,768]{2,1,0:T(8,128)(2,1)S(1)}, bf16[4,48,768]{2,1,0:T(8,128)(2,1)S(1)}, u32[]{:S(2)}, u32[]{:S(2)}) collective-permute-start(bf16[4,48,768]{2,1,0:T(8,128)(2,1)S(1)} %slice_add_fusion.18), channel_id=1, source_target_pairs={{0,1},{1,0},{2,3},{3,2},{4,5},{5,4},{6,7},{7,6},{8,9},{9,8},{10,11... | collective-permute-start | bytes 884744 | tf_op jit(solution)/shard_map/ppermute | solution.py:68
  284.8 15.2 %collective-permute-start.55 = (bf16[4,48,768]{2,1,0:T(8,128)(2,1)S(1)}, bf16[4,48,768]{2,1,0:T(8,128)(2,1)S(1)}, u32[]{:S(2)}, u32[]{:S(2)}) collective-permute-start(bf16[4,48,768]{2,1,0:T(8,128)(2,1)S(1)} %fusion.14), channel_id=1, source_target_pairs={{0,16},{8,24},{16,0},{24,8},{1,17},{9,25},{17,1},{25,9},{2,18},{10... | collective-permute-start | bytes 884744 | tf_op jit(solution)/shard_map/ppermute | solution.py:68
  285.6 14.4 %collective-permute-start.53 = (bf16[4,48,768]{2,1,0:T(8,128)(2,1)S(1)}, bf16[4,48,768]{2,1,0:T(8,128)(2,1)S(1)}, u32[]{:S(2)}, u32[]{:S(2)}) collective-permute-start(bf16[4,48,768]{2,1,0:T(8,128)(2,1)S(1)} %slice_add_fusion.14), channel_id=1, source_target_pairs={{0,1},{1,0},{2,3},{3,2},{4,5},{5,4},{6,7},{7,6},{8,9},{9,8},{10,11... | collective-permute-start | bytes 884744 | tf_op jit(solution)/shard_map/ppermute | solution.py:68
  300.2 14.0 %collective-permute-start.56 = (bf16[2,2,48,768]{3,2,0,1:T(8,128)(2,1)S(1)}, bf16[2,2,48,768]{3,2,0,1:T(8,128)(2,1)S(1)}, u32[]{:S(2)}, u32[]{:S(2)}) collective-permute-start(bf16[2,2,48,768]{3,2,0,1:T(8,128)(2,1)S(1)} %pad_maximum_fusion.16), channel_id=1, source_target_pairs={{0,2},{1,3},{2,0},{3,1},{4,6},{5,7},{6,4},{7,5},{8,10},{9,11},{10,... | collective-permute-start | bytes 884744 | tf_op jit(solution)/shard_map/ppermute | solution.py:68
  304.5 17.3 %collective-permute-start.36 = (bf16[208,768]{1,0:T(8,128)(2,1)S(1)}, bf16[208,768]{1,0:T(8,128)(2,1)S(1)}, u32[]{:S(2)}, u32[]{:S(2)}) collective-permute-start(bf16[208,768]{1,0:T(8,128)(2,1)S(1)} %pad_maximum_fusion.15), channel_id=1, source_target_pairs={{0,2},{1,3},{2,0},{3,1},{4,6},{5,7},{6,4},{7,5},{8,10},{9,11},{10,... | collective-permute-start | bytes 958472 | tf_op jit(solution)/shard_map/ppermute | solution.py:68
  304.8 17.3 %collective-permute-start.47 = (bf16[1,2,48,768]{3,2,0,1:T(8,128)(2,1)S(1)}, bf16[1,2,48,768]{3,2,0,1:T(8,128)(2,1)S(1)}, u32[]{:S(2)}, u32[]{:S(2)}) collective-permute-start(bf16[1,2,48,768]{3,2,0,1:T(8,128)(2,1)S(1)} %slice.496), channel_id=1, source_target_pairs={{0,4},{1,5},{2,6},{3,7},{4,0},{5,1},{6,2},{7,3},{8,12},{9,13},{10,... | collective-permute-start | bytes 442376 | tf_op jit(solution)/shard_map/ppermute | solution.py:68
  314.2 16.3 %collective-permute-start.57 = (bf16[1,2,48,768]{3,2,0,1:T(8,128)(2,1)S(1)}, bf16[1,2,48,768]{3,2,0,1:T(8,128)(2,1)S(1)}, u32[]{:S(2)}, u32[]{:S(2)}) collective-permute-start(bf16[1,2,48,768]{3,2,0,1:T(8,128)(2,1)S(1)} %slice.517), channel_id=1, source_target_pairs={{0,4},{1,5},{2,6},{3,7},{4,0},{5,1},{6,2},{7,3},{8,12},{9,13},{10,... | collective-permute-start | bytes 442376 | tf_op jit(solution)/shard_map/ppermute | solution.py:68
  322.0 11.2 %collective-permute-start.37 = (bf16[112,768]{1,0:T(8,128)(2,1)S(1)}, bf16[112,768]{1,0:T(8,128)(2,1)S(1)}, u32[]{:S(2)}, u32[]{:S(2)}) collective-permute-start(bf16[112,768]{1,0:T(8,128)(2,1)S(1)} %pad_maximum_fusion.24), channel_id=1, source_target_pairs={{0,4},{1,5},{2,6},{3,7},{4,0},{5,1},{6,2},{7,3},{8,12},{9,13},{10,... | collective-permute-start | bytes 516104 | tf_op jit(solution)/shard_map/ppermute | solution.py:68
  322.2 13.3 %collective-permute-start.49 = (bf16[96,768]{1,0:T(8,128)(2,1)S(1)}, bf16[96,768]{1,0:T(8,128)(2,1)S(1)}, u32[]{:S(2)}, u32[]{:S(2)}) collective-permute-start(bf16[96,768]{1,0:T(8,128)(2,1)S(1)} %bitcast.204), channel_id=1, source_target_pairs={{0,16},{8,24},{16,0},{24,8},{1,17},{9,25},{17,1},{25,9},{2,18},{10... | collective-permute-start | bytes 442376 | tf_op jit(solution)/shard_map/ppermute | solution.py:68
  323.7 12.3 %collective-permute-start.48 = (bf16[96,768]{1,0:T(8,128)(2,1)S(1)}, bf16[96,768]{1,0:T(8,128)(2,1)S(1)}, u32[]{:S(2)}, u32[]{:S(2)}) collective-permute-start(bf16[96,768]{1,0:T(8,128)(2,1)S(1)} %bitcast.205), channel_id=1, source_target_pairs={{0,8},{8,0},{16,24},{24,16},{1,9},{9,1},{17,25},{25,17},{2,10},{10... | collective-permute-start | bytes 442376 | tf_op jit(solution)/shard_map/ppermute | solution.py:68
  (44 other events, 639.8 us)

commit v2 on v1

--- a/solution.py
+++ b/solution.py
@@ -17,6 +17,7 @@
 BF = jnp.bfloat16
 F32 = jnp.float32
 SMALL = 16
+LONG = 160
 VMEM_LIMIT = 56 * 1024 * 1024
 
 
@@ -123,57 +124,62 @@
     return total
 
 
-def assemble_kernel(masks, h, idx_ref, a0, a1, a2, a3, b0, b1, b2, b3, out_ref, sems):
+def piece_map(which, masks):
     count = 1 << len(masks)
     half = count // 2
-    me_d, me_f = idx_ref[0], idx_ref[1]
-    copies = []
-
-    def put(src, r, k, colour):
-        d = me_d ^ r
-        j = me_f ^ k
-        copy = pltpu.make_async_copy(src, out_ref.at[d, j, colour], sems.at[len(copies)])
-        copy.start()
-        copies.append(copy)
-
-    for ref, r in ((a0, 0), (a1, 2), (a2, 1), (a3, 3)):
-        for i in range(count):
-            put(ref.at[i], r, bits_of(i, masks), 0)
-    for ref, r, y in ((b0, 0, 0), (b1, 0, 1), (b2, 1, 0), (b3, 1, 1)):
-        for x in range(2):
-            for i in range(half):
-                put(ref.at[x * half + i], r | (2 * x), bits_of(i, masks) | y, 1)
-    for copy in copies:
-        copy.wait()
-
-
-def assemble(idx, pieces, masks, shards, h, width):
-    count = 1 << len(masks)
-    out = pl.pallas_call(
-        partial(assemble_kernel, masks, h),
-        out_shape=jax.ShapeDtypeStruct((4, shards, 2, h, width), BF),
-        in_specs=[pl.BlockSpec(memory_space=pltpu.SMEM)]
-        + [pl.BlockSpec(memory_space=pl.ANY)] * 8,
-        out_specs=pl.BlockSpec(memory_space=pltpu.VMEM),
-        scratch_shapes=[pltpu.SemaphoreType.DMA((8 * count,))],
-        compiler_params=params(),
-        cost_estimate=cost(0, 4 * shards * 2 * h * width * 4),
-        name="assemble",
-    )(idx, *pieces)
-    return out.reshape(4, shards * 2 * h, width)
-
-
-def qkv_kernel(x_ref, small_ref, cos_ref, sin_ref, w_ref, normed_ref, out_ref, keep):
+    kind, r, y = which
+    if kind == "a":
+        return [((i,), r, bits_of(i, masks), 0) for i in range(count)]
+    return [
+        ((x * half + i,), r | (2 * x), bits_of(i, masks) | y, 1)
+        for x in range(2)
+        for i in range(half)
+    ]
+
+
+def fetch(pieces, maps, me_f, h, w_ref, slot_of, sems):
+    for ref, entries in zip(pieces, maps):
+        for at, r, k, colour in entries:
+            slot = slot_of(r)
+            pltpu.make_async_copy(
+                ref.at[at],
+                w_ref.at[slot, me_f ^ k, pl.ds(colour * h, h)],
+                sems.at[slot],
+            ).start()
+
+
+def fetched(w_ref, slot, sems):
+    pltpu.make_async_copy(w_ref.at[slot], w_ref.at[slot], sems.at[slot]).wait()
+
+
+def qkv_kernel(
+    maps, h, idx_ref, x_ref, small_ref, cos_ref, sin_ref, p0, p1, p2, p3, p4, p5, p6, p7,
+    normed_ref, out_ref, w_out, keep, w_ref, sems, out_sems,
+):
     g = pl.program_id(0)
+    d4, me_f = idx_ref[0], idx_ref[1]
+    d = keep.shape[1]
+
+    def send(slot):
+        return pltpu.make_async_copy(w_ref.at[slot], w_out.at[slot], out_sems.at[slot])
 
     @pl.when(g == 0)
     def _():
+        fetch((p0, p1, p2, p3, p4, p5, p6, p7), maps, me_f, h, w_ref, lambda r: d4 ^ r, sems)
         unit, _ = norm_parts(x_ref[...].astype(F32))
         normed = (unit * small_ref[0:1, :] + small_ref[1:2, :]).astype(BF)
         keep[...] = normed
         normed_ref[...] = normed
 
-    product = dot(keep[...], w_ref[0])
+    fetched(w_ref, g, sems)
+    send(g).start()
+
+    @pl.when(g == 2)
+    def _():
+        fetched(w_ref, 3, sems)
+        send(3).start()
+
+    product = dot(keep[...], w_ref[g].reshape(d, d))
 
     @pl.when(g < 2)
     def _():
@@ -182,30 +188,43 @@
     @pl.when(g == 2)
     def _():
         out_ref[0] = product.astype(BF)
-
-
-def qkv(x, small, cosine, sine, weights):
+        for slot in range(4):
+            send(slot).wait()
+
+
+def qkv(idx, x, small, cosine, sine, pieces, maps, shards, h):
     n, d = x.shape
     return pl.pallas_call(
-        qkv_kernel,
+        partial(qkv_kernel, maps, h),
         grid=(3,),
-        out_shape=(jax.ShapeDtypeStruct((n, d), BF), jax.ShapeDtypeStruct((3, n, d), BF)),
+        out_shape=(
+            jax.ShapeDtypeStruct((n, d), BF),
+            jax.ShapeDtypeStruct((3, n, d), BF),
+            jax.ShapeDtypeStruct((4, shards, 2 * h, d), BF),
+        ),
         in_specs=[
+            pl.BlockSpec(memory_space=pltpu.SMEM),
             pl.BlockSpec((n, d), lambda g: (0, 0)),
             pl.BlockSpec(small.shape, lambda g: (0, 0)),
             pl.BlockSpec(cosine.shape, lambda g: (0, 0)),
             pl.BlockSpec(sine.shape, lambda g: (0, 0)),
-            pl.BlockSpec((1, d, d), lambda g: (g, 0, 0)),
-        ],
+        ]
+        + [pl.BlockSpec(memory_space=pl.ANY)] * 8,
         out_specs=(
             pl.BlockSpec((n, d), lambda g: (0, 0)),
             pl.BlockSpec((1, n, d), lambda g: (g, 0, 0)),
-        ),
-        scratch_shapes=[pltpu.VMEM((n, d), BF)],
+            pl.BlockSpec(memory_space=pl.ANY),
+        ),
+        scratch_shapes=[
+            pltpu.VMEM((n, d), BF),
+            pltpu.VMEM((4, shards, 2 * h, d), BF),
+            pltpu.SemaphoreType.DMA((4,)),
+            pltpu.SemaphoreType.DMA((4,)),
+        ],
         compiler_params=params(),
-        cost_estimate=cost(6 * n * d * d, 2 * (5 * n * d + 3 * d * d)),
+        cost_estimate=cost(6 * n * d * d, 2 * (5 * n * d + 8 * d * d)),
         name="qkv",
-    )(x, small, cosine, sine, weights)
+    )(idx, x, small, cosine, sine, *pieces)
 
 
 def head_mask(which):
@@ -333,48 +352,8 @@
     )(x, mixed, weights, small)
 
 
-def up_kernel(hidden_ref, w_ref, small_ref, act_ref, slope_ref):
-    g = pl.program_id(0)
-    bias = small_ref[5:6, :]
-    for other in range(1, 4):
-        bias = jnp.where(g == other, small_ref[5 + other : 6 + other, :], bias)
-    v = dot(hidden_ref[...], w_ref[0]) + bias
-    c = math.sqrt(2.0 / math.pi)
-    square = v * v
-    t = jnp.tanh(v * (c + (c * 0.044715) * square))
-    half = 0.5 * (1.0 + t)
-    act_ref[0] = (v * half).astype(BF)
-    slope = half + (0.5 * v) * (1.0 - t * t) * (c + (3.0 * c * 0.044715) * square)
-    slope_ref[0] = slope.astype(BF)
-
-
-def up(hidden, weights, small):
-    n, d = hidden.shape
-    return pl.pallas_call(
-        up_kernel,
-        grid=(4,),
-        out_shape=(
-            jax.ShapeDtypeStruct((4, n, d), BF),
-            jax.ShapeDtypeStruct((4, n, d), BF),
-        ),
-        in_specs=[
-            pl.BlockSpec((n, d), lambda g: (0, 0)),
-            pl.BlockSpec((1, d, d), lambda g: (g, 0, 0)),
-            pl.BlockSpec(small.shape, lambda g: (0, 0)),
-        ],
-        out_specs=(
-            pl.BlockSpec((1, n, d), lambda g: (g, 0, 0)),
-            pl.BlockSpec((1, n, d), lambda g: (g, 0, 0)),
-        ),
-        compiler_params=params(),
-        cost_estimate=cost(8 * n * d * d, 18 * n * d + 8 * d * d),
-        name="up",
-    )(hidden, weights, small)
-
-
-def weight_grad_kernel(masks, h, shards, idx_ref, x_ref, y_ref, out_ref, keep):
-    keep[...] = dot_tn(x_ref[0], y_ref[0]).astype(BF)
-    me_f = idx_ref[1]
+def spread(out_ref, keep, product, me_f, masks, h, shards):
+    keep[...] = product.astype(BF)
     for i in range(shards):
         j = me_f ^ bits_of(i, masks)
         for colour in range(2):
@@ -382,79 +361,201 @@
             out_ref[0, colour, i] = keep[pl.ds(start, h), :]
 
 
-def weight_grad(idx, xs, ys, x_of, y_of, distances, masks, shards, h):
-    _, n, d = xs.shape
-    first, step = distances[0], distances[1] - distances[0]
-
-    def chunk(g, idx_ref):
-        return idx_ref[0] ^ (first + step * g)
-
+def up_kernel(
+    masks, maps, rs, h, shards, idx_ref, hidden_ref, c_ref, small_ref, p0, p1, p2, p3,
+    act_ref, slope_ref, grad_ref, w_out, w_ref, keep, sems, out_sems,
+):
+    g = pl.program_id(0)
+    d4, me_f = idx_ref[0], idx_ref[1]
+    d = hidden_ref.shape[1]
+
+    def send(slot):
+        return pltpu.make_async_copy(w_ref.at[slot], w_out.at[slot], out_sems.at[slot])
+
+    @pl.when(g == 0)
+    def _():
+        fetch((p0, p1, p2, p3), maps, me_f, h, w_ref, rs.index, sems)
+
+    fetched(w_ref, g, sems)
+    send(g).start()
+    chunk = d4 ^ jnp.where(g == 0, rs[0], rs[1])
+    bias = small_ref[5:6, :]
+    for other in range(1, 4):
+        bias = jnp.where(chunk == other, small_ref[5 + other : 6 + other, :], bias)
+    v = dot(hidden_ref[...], w_ref[g].reshape(d, d)) + bias
+    c = math.sqrt(2.0 / math.pi)
+    square = v * v
+    t = jnp.tanh(v * (c + (c * 0.044715) * square))
+    half = 0.5 * (1.0 + t)
+    act = (v * half).astype(BF)
+    act_ref[0] = act
+    slope = half + (0.5 * v) * (1.0 - t * t) * (c + (3.0 * c * 0.044715) * square)
+    slope_ref[0] = slope.astype(BF)
+    spread(grad_ref, keep, dot_tn(act, c_ref[...]), me_f, masks, h, shards)
+
+    @pl.when(g == 1)
+    def _():
+        send(0).wait()
+        send(1).wait()
+
+
+def up(idx, hidden, c, small, pieces, maps, rs, masks, shards, h):
+    n, d = hidden.shape
     return pl.pallas_call(
-        partial(weight_grad_kernel, masks, h, shards),
+        partial(up_kernel, masks, maps, rs, h, shards),
+        grid=(2,),
+        out_shape=(
+            jax.ShapeDtypeStruct((2, n, d), BF),
+            jax.ShapeDtypeStruct((2, n, d), BF),
+            jax.ShapeDtypeStruct((2, 2, shards, h, d), BF),
+            jax.ShapeDtypeStruct((2, shards, 2 * h, d), BF),
+        ),
+        in_specs=[
+            pl.BlockSpec(memory_space=pltpu.SMEM),
+            pl.BlockSpec((n, d), lambda g: (0, 0)),
+            pl.BlockSpec((n, d), lambda g: (0, 0)),
+            pl.BlockSpec(small.shape, lambda g: (0, 0)),
+        ]
+        + [pl.BlockSpec(memory_space=pl.ANY)] * 4,
+        out_specs=(
+            pl.BlockSpec((1, n, d), lambda g: (g, 0, 0)),
+            pl.BlockSpec((1, n, d), lambda g: (g, 0, 0)),
+            pl.BlockSpec((1, 2, shards, h, d), lambda g: (g, 0, 0, 0, 0)),
+            pl.BlockSpec(memory_space=pl.ANY),
+        ),
+        scratch_shapes=[
+            pltpu.VMEM((2, shards, 2 * h, d), BF),
+            pltpu.VMEM((d, d), BF),
+            pltpu.SemaphoreType.DMA((2,)),
+            pltpu.SemaphoreType.DMA((2,)),
+        ],
+        compiler_params=params(),
+        cost_estimate=cost((LONG if rs[0] == 0 else 8) * n * d * d, 2 * (6 * n * d + 6 * d * d)),
+        name="up",
+    )(idx, hidden, c, small, *pieces)
+
+
+def act_grad_kernel(
+    masks, maps, rs, h, shards, first, idx_ref, c_ref, x_ref, up_ref, slope_ref, p0, p1, p2, p3,
+    *more,
+):
+    if first:
+        (hidden_ref, sums_ref, grad_ref, w_out, w_ref, keep, sems, out_sems) = more
+    else:
+        (
+            hidden_in, sums_in, hidden_ref, sums_ref, grad_ref, w_out, w_ref, keep, sems, out_sems,
+        ) = more
+    g = pl.program_id(0)
+    d4, me_f = idx_ref[0], idx_ref[1]
+    d = x_ref.shape[1]
+    c = c_ref[...]
+
+    def send(slot):
+        return pltpu.make_async_copy(w_ref.at[slot], w_out.at[slot], out_sems.at[slot])
+
+    @pl.when(g == 0)
+    def _():
+        fetch((p0, p1, p2, p3), maps, me_f, h, w_ref, rs.index, sems)
+        if first:
+            hidden_ref[...] = jnp.zeros_like(hidden_ref)
+            sums_ref[...] = jnp.zeros_like(sums_ref)
+            sums_ref[4:5, :] = jnp.sum(c.astype(F32), axis=0, keepdims=True)
+        else:
+            hidden_ref[...] = hidden_in[...]
+            sums_ref[...] = sums_in[...]
+
+    fetched(w_ref, g, sems)
+    send(g).start()
+    chunk = d4 ^ jnp.where(g == 0, rs[0], rs[1])
+    pre = (dot_nt(c, w_ref[g].reshape(d, d)) * slope_ref[0].astype(F32)).astype(BF)
+    sums = jnp.sum(pre.astype(F32), axis=0, keepdims=True)
+    row = lax.broadcasted_iota(jnp.int32, (sums_ref.shape[0], 1), 0)
+    sums_ref[...] += jnp.where(row == 5 + chunk, sums, 0.0)
+    hidden_ref[...] += dot_nt(pre, up_ref[0])
+    spread(grad_ref, keep, dot_tn(x_ref[...], pre), me_f, masks, h, shards)
+
+    @pl.when(g == 1)
+    def _():
+        send(0).wait()
+        send(1).wait()
+
+
+def act_grad(idx, c, hidden, up_half, slope, pieces, maps, rs, masks, shards, h, before=None):
+    n, d = c.shape
+    whole = pl.BlockSpec((n, d), lambda g: (0, 0))
+    sums = pl.BlockSpec((SMALL, d), lambda g: (0, 0))
+    return pl.pallas_call(
+        partial(act_grad_kernel, masks, maps, rs, h, shards, before is None),
+        grid=(2,),
+        out_shape=(
+            jax.ShapeDtypeStruct((n, d), F32),
+            jax.ShapeDtypeStruct((SMALL, d), F32),
+            jax.ShapeDtypeStruct((2, 2, shards, h, d), BF),
+            jax.ShapeDtypeStruct((2, shards, 2 * h, d), BF),
+        ),
+        in_specs=[
+            pl.BlockSpec(memory_space=pltpu.SMEM),
+            whole,
+            whole,
+            pl.BlockSpec((1, d, d), lambda g: (g, 0, 0)),
+            pl.BlockSpec((1, n, d), lambda g: (g, 0, 0)),
+        ]
+        + [pl.BlockSpec(memory_space=pl.ANY)] * 4
+        + ([] if before is None else [whole, sums]),
+        out_specs=(
+            whole,
+            sums,
+            pl.BlockSpec((1, 2, shards, h, d), lambda g: (g, 0, 0, 0, 0)),
+            pl.BlockSpec(memory_space=pl.ANY),
+        ),
+        scratch_shapes=[
+            pltpu.VMEM((2, shards, 2 * h, d), BF),
+            pltpu.VMEM((d, d), BF),
+            pltpu.SemaphoreType.DMA((2,)),
+            pltpu.SemaphoreType.DMA((2,)),
+        ],
+        compiler_params=params(),
+        cost_estimate=cost((LONG if rs[0] == 0 else 12) * n * d * d, 2 * (8 * n * d + 8 * d * d)),
+        name="act_grad",
+    )(idx, c, hidden, up_half.reshape(2, d, d), slope, *pieces, *(before or ()))
+
+
+def first_grad_kernel(
+    masks, h, shards, rs, idx_ref, normed_ref, mixed_ref, three_ref, branch_ref, out_ref, keep
+):
+    g = pl.program_id(0)
+    last = (idx_ref[0] ^ jnp.where(g == 0, rs[0], rs[1])) == 3
+    x = jnp.where(last, mixed_ref[...], normed_ref[...])
+    y = jnp.where(last, branch_ref[...], three_ref[0])
+    spread(out_ref, keep, dot_tn(x, y), idx_ref[1], masks, h, shards)
+
+
+def first_grad(idx, normed, mixed, three_grad, branch_grad, rs, masks, shards, h):
+    n, d = normed.shape
+
+    def which(g, idx_ref):
+        return jnp.minimum(idx_ref[0] ^ jnp.where(g == 0, rs[0], rs[1]), 2)
+
+    whole = pl.BlockSpec((n, d), lambda g, i: (0, 0))
+    return pl.pallas_call(
+        partial(first_grad_kernel, masks, h, shards, rs),
         grid_spec=pltpu.PrefetchScalarGridSpec(
             num_scalar_prefetch=1,
-            grid=(len(distances),),
+            grid=(2,),
             in_specs=[
-                pl.BlockSpec((1, n, d), lambda g, i: (x_of(chunk(g, i)), 0, 0)),
-                pl.BlockSpec((1, n, d), lambda g, i: (y_of(chunk(g, i)), 0, 0)),
+                whole,
+                whole,
+                pl.BlockSpec((1, n, d), lambda g, i: (which(g, i), 0, 0)),
+                whole,
             ],
-            out_specs=pl.BlockSpec(
-                (1, 2, shards, h, d), lambda g, i: (g, 0, 0, 0, 0)
-            ),
+            out_specs=pl.BlockSpec((1, 2, shards, h, d), lambda g, i: (g, 0, 0, 0, 0)),
             scratch_shapes=[pltpu.VMEM((d, d), BF)],
         ),
-        out_shape=jax.ShapeDtypeStruct((len(distances), 2, shards, h, d), BF),
+        out_shape=jax.ShapeDtypeStruct((2, 2, shards, h, d), BF),
         compiler_params=params(),
-        cost_estimate=cost(
-            2 * len(distances) * n * d * d, 2 * len(distances) * (2 * n * d + d * d)
-        ),
-        name="weight_grad",
-    )(idx, xs, ys)
-
-
-def act_grad_kernel(c_ref, down_ref, up_ref, slope_ref, pre_ref, sums_ref, hidden_ref):
-    g = pl.program_id(0)
-    c = c_ref[...]
-
-    @pl.when(g == 0)
-    def _():
-        hidden_ref[...] = jnp.zeros_like(hidden_ref)
-        sums_ref[...] = jnp.zeros_like(sums_ref)
-        sums_ref[4:5, :] = jnp.sum(c.astype(F32), axis=0, keepdims=True)
-
-    pre = (dot_nt(c, down_ref[0]) * slope_ref[0].astype(F32)).astype(BF)
-    pre_ref[0] = pre
-    sums = jnp.sum(pre.astype(F32), axis=0, keepdims=True)
-    row = lax.broadcasted_iota(jnp.int32, (sums_ref.shape[0], 1), 0)
-    sums_ref[...] += jnp.where(row == 5 + g, sums, 0.0)
-    hidden_ref[...] += dot_nt(pre, up_ref[0])
-
-
-def act_grad(c, down, up_weights, slope):
-    n, d = c.shape
-    return pl.pallas_call(
-        act_grad_kernel,
-        grid=(4,),
-        out_shape=(
-            jax.ShapeDtypeStruct((4, n, d), BF),
-            jax.ShapeDtypeStruct((SMALL, d), F32),
-            jax.ShapeDtypeStruct((n, d), F32),
-        ),
-        in_specs=[
-            pl.BlockSpec((n, d), lambda g: (0, 0)),
-            pl.BlockSpec((1, d, d), lambda g: (g, 0, 0)),
-            pl.BlockSpec((1, d, d), lambda g: (g, 0, 0)),
-            pl.BlockSpec((1, n, d), lambda g: (g, 0, 0)),
-        ],
-        out_specs=(
-            pl.BlockSpec((1, n, d), lambda g: (g, 0, 0)),
-            pl.BlockSpec((SMALL, d), lambda g: (0, 0)),
-            pl.BlockSpec((n, d), lambda g: (0, 0)),
-        ),
-        compiler_params=params(),
-        cost_estimate=cost(16 * n * d * d, 22 * n * d + 16 * d * d),
-        name="act_grad",
-    )(c, down, up_weights, slope)
+        cost_estimate=cost((LONG if rs[0] == 0 else 4) * n * d * d, 2 * (5 * n * d + 2 * d * d)),
+        name="first_grad",
+    )(idx, normed, mixed, three_grad, branch_grad)
 
 
 def middle_kernel(
@@ -552,31 +653,29 @@
     )(x, three_grad, weights, small, residual_grad)
 
 
-def down_kernel(act_ref, w_ref, small_ref, residual_ref, out_ref, total):
+def down_kernel(a0_ref, a1_ref, w0_ref, w1_ref, small_ref, residual_ref, out_ref, total):
     g = pl.program_id(0)
-    part = dot(act_ref[0], w_ref[0])
+    part = dot(a0_ref[0], w0_ref[0]) + dot(a1_ref[0], w1_ref[0])
 
     @pl.when(g == 0)
     def _():
         total[...] = residual_ref[...] + small_ref[4:5, :] + part
 
-    @pl.when(g > 0)
-    def _():
-        total[...] += part
-
-    @pl.when(g == 3)
-    def _():
-        out_ref[...] = total[...].astype(BF)
-
-
-def down_out(act, weights, small, residual):
+    @pl.when(g == 1)
+    def _():
+        out_ref[...] = (total[...] + part).astype(BF)
+
+
+def down_out(acts, weights, small, residual):
     n, d = residual.shape
     return pl.pallas_call(
         down_kernel,
-        grid=(4,),
+        grid=(2,),
         out_shape=jax.ShapeDtypeStruct((n, d), BF),
         in_specs=[
             pl.BlockSpec((1, n, d), lambda g: (g, 0, 0)),
+            pl.BlockSpec((1, n, d), lambda g: (g, 0, 0)),
+            pl.BlockSpec((1, d, d), lambda g: (g, 0, 0)),
             pl.BlockSpec((1, d, d), lambda g: (g, 0, 0)),
             pl.BlockSpec(small.shape, lambda g: (0, 0)),
             pl.BlockSpec((n, d), lambda g: (0, 0)),
@@ -586,7 +685,7 @@
         compiler_params=params(),
         cost_estimate=cost(8 * n * d * d, 14 * n * d + 8 * d * d),
         name="down_out",
-    )(act, weights, small, residual)
+    )(*acts, *(w.reshape(2, d, d) for w in weights), small, residual)
 
 
 def local(dp, fsdp, tokens, lengths, *rest):
@@ -627,153 +726,250 @@
     def dswap(v, m):
         return swap(v, "dp", m, dp)
 
-    shard4 = (query_weight, key_weight, value_weight, output_weight)
-    piece1 = lax.select_n(d4, *shard4)
-    piece2 = lax.dynamic_index_in_dim(
-        up_weight.reshape(R, fsdp, 4, R), d4, axis=2, keepdims=False
-    ).reshape(R, width)
-    piece3 = lax.dynamic_slice_in_dim(down_weight, d4 * R, R, axis=0)
-
-    tall = jnp.concatenate(
-        [norm1_gain, norm1_bias, norm2_gain, norm2_bias, down_bias, up_bias]
-    ).reshape(9, R)
+    def after(value, *tokens):
+        return lax.optimization_barrier((value,) + tokens)[0]
+
+    def after_all(values, *tokens):
+        values = tuple(values)
+        return list(lax.optimization_barrier(values + tokens)[: len(values)])
+
+    half = fsdp // 2
+    maps_own = [
+        piece_map(w, masks) for w in (("a", 0, 0), ("a", 2, 0), ("b", 0, 0), ("b", 0, 1))
+    ]
+    maps_core = [
+        piece_map(w, masks) for w in (("a", 1, 0), ("a", 3, 0), ("b", 1, 0), ("b", 1, 1))
+    ]
+
+    class Gather:
+        def __init__(self, piece):
+            self.cur = piece[None]
+
+        def far(self, m):
+            self.got = fswap(self.cur, m)
+
+        def join(self):
+            self.cur = jnp.concatenate([self.cur, self.got], axis=0)
+
+        def near(self):
+            self.got = fswap(self.cur, outer[-1])
+
+        def sides(self):
+            a = jnp.concatenate([self.cur[:, :h], self.got[:, :h]], axis=0)
+            b = jnp.concatenate([self.cur[:, h:R], self.got[:, h:R]], axis=0)
+            self.ab = (a, b)
+            self.got_ab = (fswap(a, masks[-1]), dswap(b, 2))
+            if self.cur.shape[1] > R:
+                rest = [jnp.sum(t[:, R:].astype(F32), axis=0) for t in (self.cur, self.got)]
+                self.small = rest[0] + rest[1]
+
+        def cross(self):
+            a1 = jnp.concatenate([self.ab[0], self.got_ab[0]], axis=0)
+            b1 = jnp.concatenate([self.ab[1], self.got_ab[1]], axis=0)
+            self.ab1 = (a1, b1)
+            self.got_ab1 = (dswap(a1, 2), fswap(b1, masks[-1]))
+            self.core = [dswap(a1, 1), dswap(b1, 1)]
+
+        def finish(self):
+            a_x, b_y = self.got_ab1
+            a1, b1 = self.ab1
+            self.own = [a1, a_x, b1, b_y]
+            self.other = [self.core[0], dswap(a_x, 1), self.core[1], dswap(b_y, 1)]
+
+    class Inner:
+        def __init__(self, cur):
+            self.cur = cur
+            self.left = list(reversed(outer))
+
+        def send(self):
+            m = self.left.pop(0)
+            count = self.cur.shape[0] // 2
+            self.got = fswap(self.cur[count:], m)
+            self.cur = self.cur[:count]
+
+        def add(self, *tokens):
+            self.cur = self.cur + after(self.got, *tokens)
+
+        def sums(self):
+            while self.left:
+                self.send()
+                self.add()
+
+        def spread(self):
+            total = self.cur[0]
+            m = 4
+            while m < dp:
+                total = total + dswap(total, m)
+                m *= 2
+            self.total = total
+            self.pair = dswap(total, 2)
+
+        def four(self, *tokens):
+            pair = after(self.pair, *tokens)
+            return jnp.stack([self.total, dswap(self.total, 1), pair, dswap(pair, 1)])
+
+    piece1 = lax.select_n(d4, query_weight, key_weight, value_weight, output_weight)
+    g1 = Gather(piece1)
+    for m in outer[:-1]:
+        g1.far(m)
+        g1.join()
+    g1.near()
+    vectors = after_all(
+        (norm1_gain, norm1_bias, norm2_gain, norm2_bias, down_bias, up_bias, up_weight), piece1
+    )
+    tall = jnp.concatenate(vectors[:6]).reshape(9, R)
     lane = jnp.arange(width, dtype=jnp.int32) // R
     tall = jnp.where((lane == me_f)[None, :], jnp.tile(tall, (1, fsdp)), jnp.zeros((), BF))
     tall = jnp.pad(tall, ((0, SMALL - 9), (0, 0)))
-
-    def gather(piece, extra):
-        size = R
-        if extra is not None:
-            piece = jnp.concatenate([piece, extra], axis=0)
-            size = R + SMALL
-        cur = piece[None]
-        for m in outer[:-1]:
-            cur = jnp.concatenate([cur, fswap(cur, m)], axis=0)
-        m = outer[-1]
-        other = fswap(cur, m)
-        if extra is not None:
-            a = jnp.concatenate(
-                [
-                    jnp.concatenate([t[:, :h], t[:, R:]], axis=1) for t in (cur, other)
-                ],
-                axis=0,
-            )
-        else:
-            a = jnp.concatenate([cur[:, :h], other[:, :h]], axis=0)
-        b = jnp.concatenate([cur[:, h:R], other[:, h:R]], axis=0)
-        a_y = fswap(a, masks[-1])
-        b_x = dswap(b, 2)
-        small = None
-        if extra is not None:
-            small = jnp.sum(a[:, h:].astype(F32), axis=0) + jnp.sum(
-                a_y[:, h:].astype(F32), axis=0
-            )
-        a1 = jnp.concatenate([a[:, :h], a_y[:, :h]], axis=0)
-        b1 = jnp.concatenate([b, b_x], axis=0)
-        a_x = dswap(a1, 2)
-        b_y = fswap(b1, masks[-1])
-        pieces = [a1, a_x, dswap(a1, 1), dswap(a_x, 1), b1, b_y, dswap(b1, 1), dswap(b_y, 1)]
-        return assemble(idx, pieces, masks, fsdp, h, width), small
-
-    first4, small = gather(piece1, tall)
-    up4, _ = gather(piece2, None)
-    down4, _ = gather(piece3, None)
+    up_part = lax.dynamic_index_in_dim(
+        vectors[6].reshape(R, fsdp, 4, R), d4, axis=2, keepdims=False
+    ).reshape(R, width)
+    piece2 = jnp.concatenate([up_part, tall], axis=0)
+    g2 = Gather(after(piece2, g1.cur))
+    for m in outer[:-1]:
+        g2.far(m)
+        g2.join()
+    g1.sides()
+    g2.cur, g2.got = after_all((g2.cur, g2.got), *g1.ab)
+    g2.near()
+    g1.cross()
+    g3 = Gather(
+        lax.dynamic_slice_in_dim(after(down_weight, *g1.ab1), d4 * R, R, axis=0)
+    )
+    for m in outer[:-1]:
+        g3.far(m)
+    g1.finish()
+    g2.cur, g2.got = after_all((g2.cur, g2.got), *g1.got_ab1)
+    g2.sides()
+    small = g2.small + fswap(g2.small.astype(BF), masks[-1]).astype(F32)
 
     layout = row_layout(lengths[0], row_count, slot_count)
     cosine, sine = rotary_tables(layout[3])
     bias = jnp.where(allowed_pairs(layout, layout, BLOCK, slot_count), 0.0, NEGATIVE)
-    normed, three = qkv(tokens, small, cosine, sine, first4)
-    mixed, probs = attend(three, bias)
-    residual, hidden_in = branch(tokens, mixed, first4, small)
-    act, slope = up(hidden_in, up4, small)
-
-    def both(xs, ys, x_of, y_of):
-        args = (masks, fsdp, h)
-        send = weight_grad(idx, xs, ys, x_of, y_of, (1, 3), *args)
-        keep = weight_grad(idx, xs, ys, x_of, y_of, (0, 2), *args)
-        return send, keep
-
-    half = fsdp // 2
-
-    def scatter(send, keep, small_sum=None):
-        got = dswap(send, 1)
-        a_send = keep[1, 0] + got[1, 0]
-        a_keep = keep[0, 0] + got[0, 0]
-        b_send = keep[:, 1, half:] + got[:, 1, half:]
-        b_keep = keep[:, 1, :half] + got[:, 1, :half]
-        extra = small_sum is not None
-
-        def with_small(t, s):
-            if not extra:
-                return t
-            return jnp.concatenate([t.reshape(-1, width), s.astype(BF)], axis=0)
-
-        def parts(t, shape):
-            if not extra:
-                return t, None
-            rows = math.prod(shape[:-1])
-            return t[:rows].reshape(shape), t[rows:].astype(F32)
-
-        if extra:
-            small_sum = small_sum + dswap(small_sum.astype(BF), 1).astype(F32)
-        a_got, s = parts(dswap(with_small(a_send, small_sum), 2), a_send.shape)
-        b_got = fswap(b_send, masks[-1])
-        if extra:
-            small_sum = small_sum + s
-        a_send = a_keep[half:] + a_got[half:]
-        a_keep = a_keep[:half] + a_got[:half]
-        b_send = b_keep[1] + b_got[1]
-        b_keep = b_keep[0] + b_got[0]
-        a_got, s = parts(fswap(with_small(a_send, small_sum), masks[-1]), a_send.shape)
-        b_got = dswap(b_send, 2)
-        if extra:
-            small_sum = small_sum + s
-        cur = jnp.stack([a_keep + a_got, b_keep + b_got], axis=1)
-        for m in reversed(outer):
-            count = cur.shape[0] // 2
-            out = cur[count:]
-            got, s = parts(fswap(with_small(out, small_sum), m), out.shape)
-            if extra:
-                small_sum = small_sum + s
-            cur = cur[:count] + got
-        total = cur.reshape(R, width)
-        m = 4
-        while m < dp:
-            got, s = parts(dswap(with_small(total, small_sum), m), total.shape)
-            total = total + got
-            if extra:
-                small_sum = small_sum + s
-            m *= 2
-        total_x = dswap(total, 2)
-        four = jnp.stack([total, dswap(total, 1), total_x, dswap(total_x, 1)])
-        return four, small_sum
-
-    c1 = cotangent[None]
-    send3, keep3 = both(act, c1, lambda d: d, lambda d: 0)
-    pre_grad, sums_act, hidden_grad = act_grad(cotangent, down4, up4, slope)
+    normed, three, first4 = qkv(
+        idx, after(tokens, *g2.ab), small, cosine, sine, g1.own + g1.other,
+        maps_own + maps_core, fsdp, h,
+    )
+    first4 = first4.reshape(4, width, width)
+    *g2.got_ab, g3.cur, g3.got = after_all((*g2.got_ab, g3.cur, g3.got), three)
+    g2.cross()
+    for m in outer[:-1]:
+        g3.join()
+    g3.near()
+    mixed, probs = attend(after(three, *g2.ab1, g3.cur), bias)
+    *g2.got_ab1, g3.got = after_all((*g2.got_ab1, g3.got), mixed)
+    g2.finish()
+    g3.sides()
+    residual, hidden_in = branch(tokens, after(mixed, *g3.ab), first4, small)
+    send_rs, keep_rs = (1, 3), (0, 2)
+    act_s, slope_s, send3, up_s = up(
+        idx, hidden_in, cotangent, small, g2.other, maps_core, send_rs, masks, fsdp, h
+    )
+    g3.got_ab = after_all(g3.got_ab, send3)
+    g3.cross()
+    act_k, slope_k, keep3, up_k = up(
+        idx, after(hidden_in, *g3.ab1), cotangent, small, g2.own, maps_own, keep_rs, masks,
+        fsdp, h,
+    )
+    g3.got_ab1 = after_all(g3.got_ab1, keep3)
+    g3.finish()
+
+    class Scatter:
+        def __init__(self, send):
+            self.got = dswap(send, 1)
+
+        def sides(self, keep):
+            got = self.got
+            a = keep[1, 0] + got[1, 0]
+            b = keep[:, 1, half:] + got[:, 1, half:]
+            self.keep = (keep[0, 0] + got[0, 0], keep[:, 1, :half] + got[:, 1, :half])
+            self.mid = [dswap(a, 2), fswap(b, masks[-1])]
+            self.done = (a, b) + self.keep
+
+        def cross(self):
+            (a, b), (x, y) = self.keep, self.mid
+            self.last = (a[:half] + x[:half], b[0] + y[0])
+            out = (a[half:] + x[half:], b[1] + y[1])
+            self.got_last = [fswap(out[0], masks[-1]), dswap(out[1], 2)]
+            self.done = out + self.last
+
+        def rows(self):
+            (a, b), (x, y) = self.last, self.got_last
+            return jnp.stack([a + x, b + y], axis=1)
+
+    s3 = Scatter(send3)
+    s3.sides(keep3)
+    hidden_s, sums_s, send2, down_s = act_grad(
+        idx, after(cotangent, *s3.done), hidden_in, up_s, slope_s, g3.other, maps_core, send_rs,
+        masks, fsdp, h,
+    )
+    s2 = Scatter(send2)
+    hidden_grad, sums_act, keep2, down_k = act_grad(
+        idx, after(cotangent, send2), hidden_in, up_k, slope_k, g3.own, maps_own, keep_rs, masks,
+        fsdp, h, (hidden_s, sums_s),
+    )
+    s2.sides(keep2)
+    s3.mid = after_all(s3.mid, keep2)
+    s3.cross()
     residual_grad, branch_grad, mixed_grad, sums_mid = middle(
-        cotangent, hidden_grad, residual, small, first4
-    )
-    send2, keep2 = both(hidden_in[None], pre_grad, lambda d: 0, lambda d: d)
+        cotangent, after(hidden_grad, *s2.done, *s3.done), residual, small, first4
+    )
     three_grad = attend_back(three, probs, mixed_grad, mixed, cosine, sine)
-    lefts = jnp.stack([normed, mixed])
-    rights = jnp.concatenate([three_grad, branch_grad[None]], axis=0)
-    send1, keep1 = both(lefts, rights, lambda d: d // 3, lambda d: d)
-    input_grad, sums_in = input_grads(tokens, three_grad, first4, small, residual_grad)
-    output = down_out(act, down4, small, residual)
-
-    four3, _ = scatter(send3, keep3)
-    four2, _ = scatter(send2, keep2)
-    four1, small_sum = scatter(send1, keep1, sums_act + sums_mid + sums_in)
+    s2.mid = after_all(s2.mid, three_grad)
+    s2.cross()
+    send1 = first_grad(
+        idx, after(normed, *s2.done), mixed, three_grad, branch_grad, send_rs, masks, fsdp, h
+    )
+    s1 = Scatter(send1)
+    s2.got_last = after_all(s2.got_last, send1)
+    s3.got_last = after_all(s3.got_last, send1)
+    rows23 = Inner(jnp.stack([s2.rows(), s3.rows()], axis=1))
+    front = rows23.cur
+    rows23.send()
+    keep1 = first_grad(
+        idx, after(normed, front), mixed, three_grad, branch_grad, keep_rs, masks, fsdp, h
+    )
+    s1.sides(keep1)
+    rows23.add(*s1.done)
+    rows23.sums()
+    input_grad, sums_in = input_grads(
+        after(tokens, *s1.done, rows23.cur if not rows23.left else front), three_grad, first4,
+        small, residual_grad,
+    )
+    small_sum = sums_act + sums_mid + sums_in
+    small_sum = small_sum + dswap(small_sum.astype(BF), 1).astype(F32)
+    s1.mid = after_all(s1.mid, input_grad)
+    s1.cross()
+    rows23.cur = after(rows23.cur, *s1.done)
+    rows23.spread()
+    output = down_out(
+        (act_s, act_k), (down_s, down_k), small, after(residual, rows23.total)
+    )
+    s1.got_last = after_all(s1.got_last, output)
+    rows1 = Inner(s1.rows())
+    m = 2
+    while m < dp:
+        small_sum = small_sum + dswap(small_sum.astype(BF), m).astype(F32)
+        m *= 2
+    for m in masks:
+        small_sum = small_sum + fswap(small_sum.astype(BF), m).astype(F32)
+    four23 = rows23.four(rows1.cur)
+    rows1.sums()
+    rows1.spread()
+    four1 = rows1.four()
 
     def pick(four, d):
-        return lax.dynamic_index_in_dim(four, d4 ^ d, axis=0, keepdims=False).astype(F32)
+        return (
+            lax.dynamic_index_in_dim(four, d4 ^ d, axis=0, keepdims=False)
+            .reshape(R, width)
+            .astype(F32)
+        )
 
     first_grads = [pick(four1, d) for d in range(4)]
     up_grad = jnp.stack(
-        [pick(four2, d).reshape(R, fsdp, R) for d in range(4)], axis=2
+        [pick(four23[:, 0], d).reshape(R, fsdp, R) for d in range(4)], axis=2
     ).reshape(R, 4 * width)
-    down_grad = jnp.concatenate([pick(four3, d) for d in range(4)], axis=0)
+    down_grad = jnp.concatenate([pick(four23[:, 1], d) for d in range(4)], axis=0)
     own = lax.dynamic_slice_in_dim(small_sum, me_f * R, R, axis=1)
     return (
         output,

time: 348 us -> 285 us (0.82)
  waiting for transfers between devices: 135 us -> 79.4 us
  Pallas kernels: 121 us -> 104 us
    ppermute x61, waiting for transfers between devices: 135 us -> 79.4 us  [swap(): return lax.ppermute(values, axis, [(i, i ^ mask) for i in range(size)])]
    pallas_call x13 -> x8, Pallas kernels: 81.9 us -> 65.5 us  [the longest x2 20.1 us: act_grad(): pl.pallas_call(partial(act_grad_kernel, masks, maps, rs, h, shards, befor...]
    add x20 -> x18, other arithmetic: 6.92 us -> 8.26 us  [the longest x5 4.75 us: sides(): self.keep = (keep[0, 0] + got[0, 0], keep[:, 1, :half] + got[:, 1, :half])]
  transfers between devices with their start and end apart: 61 -> 61, of which waited for: 21 -> 20; matrix products, arithmetic and copies ran while one was open for 7% -> 11% of each run, Pallas kernels for 15% -> 31%
where the time goes in v2:
time: 285 us; the launch traced here: 281 us
  Pallas kernels  104 us (36%)
  waiting for transfers between devices  79.4 us (28%)
  starting transfers between devices  53.9 us (19%)
  other arithmetic  23.4 us (8%)
  local copies, waits for them, and re-layouts  17.6 us (6%)
    ppermute x61, waiting for transfers between devices, swap(): return lax.ppermute(values, axis, [(i, i ^ mask) for i in range(size)])  79.4 us
    ppermute x61, starting transfers between devices, swap(): return lax.ppermute(values, axis, [(i, i ^ mask) for i in range(size)])  53.9 us
    pallas_call x2, Pallas kernels, act_grad(): pl.pallas_call(partial(act_grad_kernel, masks, maps, rs, h, shards, befor...  20.1 us
    pallas_call x2, Pallas kernels, up(): pl.pallas_call(partial(up_kernel, masks, maps, rs, h, shards), grid=(2,),...  18.3 us
    pallas_call x1, Pallas kernels, attend_back(): pl.pallas_call(attend_back_kernel, grid=(d // pair,), out_shape=jax.Shape...  11.6 us
    pallas_call x2, Pallas kernels, first_grad(): pl.pallas_call(partial(first_grad_kernel, masks, h, shards, rs), grid_spe...  10.8 us
    pallas_call x1, Pallas kernels, attend(): pl.pallas_call(attend_kernel, grid=(d // pair,), out_shape=(jax.ShapeDtyp...  10.4 us
    pallas_call x1, Pallas kernels, qkv(): pl.pallas_call(partial(qkv_kernel, maps, h), grid=(3,), out_shape=(jax.Sh...  9.39 us
  transfers between devices with their start and end apart: 61, of which 20 were waited for; matrix products, arithmetic and copies ran while one was open for 11% of the time, Pallas kernels for 31%

profile of v2, /device:TPU:0, one launch (start us, length us, event | category | flops | bytes accessed | tf_op | source)
XLA Modules:
  0.0 280.7 jit_solution(3193196176375800684)
XLA Ops:
  1.8 4.1 %collective-permute-start = (bf16[1,96,768]{2,1,0:T(8,128)(2,1)S(1)}, bf16[1,96,768]{2,1,0:T(8,128)(2,1)S(1)}, u32[]{:S(2)}, u32[]{:S(2)}) collective-permute-start(bf16[1,96,768]{2,1,0:T(8,128)(2,1)S(1)} %bitcast.186), channel_id=1, source_target_pairs={{0,4},{1,5},{2,6},{3,7},{4,0},{5,1},{6,2},{7,3},{8,12},{9,13},{10,... | collective-permute-start | bytes 442376 | tf_op jit(solution)/shard_map/ppermute | solution.py:69
  5.9 4.1 %concatenate.63 = bf16[864]{0:T(1024)(128)(2,1)S(1)} concatenate(bf16[96]{0:T(256)(128)(2,1)} %param.17, bf16[96]{0:T(256)(128)(2,1)} %param.18, bf16[96]{0:T(256)(128)(2,1)} %param.23, bf16[96]{0:T(256)(128)(2,1)} %param.24, bf16[96]{0:T(256)(128)(2,1)} %param.28, bf16[384]{0:T(512)(128)(2,1)} %param.26), dimensions={0} | concatenate | bytes 3456 | tf_op jit(solution)/shard_map/concatenate | solution.py:820
  14.3 6.9 %collective-permute-done.2 = bf16[2,96,768]{2,1,0:T(8,128)(2,1)S(1)} collective-permute-done((bf16[2,96,768]{2,1,0:T(8,128)(2,1)S(1)}, bf16[2,96,768]{2,1,0:T(8,128)(2,1)S(1)}, u32[]{:S(2)}, u32[]{:S(2)}) %collective-permute-start.2) | collective-permute-done | bytes 294944 | tf_op jit(solution)/shard_map/ppermute | solution.py:69
  21.2 1.5 collective-permute-start.4
  22.8 1.6 collective-permute-start.6
  26.6 3.3 %collective-permute-start.1 = (bf16[1,112,768]{2,1,0:T(8,128)(2,1)S(1)}, bf16[1,112,768]{2,1,0:T(8,128)(2,1)S(1)}, u32[]{:S(2)}, u32[]{:S(2)}) collective-permute-start(bf16[1,112,768]{2,1,0:T(8,128)(2,1)S(1)} %bitcast.191), channel_id=1, source_target_pairs={{0,4},{1,5},{2,6},{3,7},{4,0},{5,1},{6,2},{7,3},{8,12},{9,13},{10,... | collective-permute-start | bytes 516104 | tf_op jit(solution)/shard_map/ppermute | solution.py:69
  32.8 2.0 fusion.34
  34.7 2.2 collective-permute-done.1
  38.9 7.2 %collective-permute-done.3 = bf16[2,112,768]{2,1,0:T(8,128)(2,1)S(1)} collective-permute-done((bf16[2,112,768]{2,1,0:T(8,128)(2,1)S(1)}, bf16[2,112,768]{2,1,0:T(8,128)(2,1)S(1)}, u32[]{:S(2)}, u32[]{:S(2)}) %collective-permute-start.3) | collective-permute-done | bytes 344096 | tf_op jit(solution)/shard_map/ppermute | solution.py:69
  47.5 1.6 collective-permute-start.13
  49.1 1.9 collective-permute-done.8
  52.2 2.8 collective-permute-start.15
  56.0 9.4 %qkv.1 = (bf16[512,768]{1,0:T(8,128)(2,1)}, bf16[3,512,768]{2,1,0:T(8,128)(2,1)}, bf16[4,8,96,768]{3,2,1,0:T(8,128)(2,1)}) custom-call(s32[2]{0:T(128)} %pad_add_fusion.idx_ref, bf16[512,768]{1,0:T(8,128)(2,1)} %x_ref.3, f32[16,768]{1,0:T(8,128)} %convert_add_fusion.4.small_ref, f32[512,128]{1,0:T(8,128)} %get-tuple-element.241.cos_ref, ...), custom_call_target="tpu_custom_call" | custom-call | flops 1811939328 | bytes 13369344 | tf_op jit(solution)/shard_map/qkv/pallas_call | solution.py:197
  65.6 1.7 collective-permute-start.16
  67.3 1.8 collective-permute-start.17
  70.3 1.7 fusion.2.bias_ref
  72.5 10.4 %attend.1 = (bf16[512,768]{1,0:T(8,128)(2,1)}, bf16[12,512,512]{2,1,0:T(8,128)(2,1)}) custom-call(bf16[3,512,768]{2,1,0:T(8,128)(2,1)} %get-tuple-element.110.q_ref.k_ref.v_ref, bf16[3,512,768]{2,1,0:T(8,128)(2,1)} %get-tuple-element.110.q_ref.k_ref.v_ref, bf16[3,512,768]{2,1,0:T(8,128)(2,1)} %get-tuple-element.110.q_ref.k_ref.v_ref, f32[512,512]{1,0:T(8,128)} %fusion.2.bias_ref), custom_call_target="tpu_custom_call" | custom-call | flops 1610612736 | bytes 9437184 | tf_op jit(solution)/shard_map/attend/pallas_call | solution.py:254
  85.3 3.7 %branch.1 = (f32[512,768]{1,0:T(8,128)}, bf16[512,768]{1,0:T(8,128)(2,1)}) custom-call(bf16[512,768]{1,0:T(8,128)(2,1)} %x_ref.3, bf16[512,768]{1,0:T(8,128)(2,1)} %get-tuple-element.113.mixed_ref, bf16[4,768,768]{2,1,0:T(8,128)(2,1)} %bitcast.181, f32[16,768]{1,0:T(8,128)} %convert_add_fusion.4.small_ref), custom_call_target="tpu_custom_call" | custom-call | flops 603979776 | bytes 5111808 | tf_op jit(solution)/shard_map/branch/pallas_call | solution.py:335
  90.3 9.0 %up.2 = (bf16[2,512,768]{2,1,0:T(8,128)(2,1)}, bf16[2,512,768]{2,1,0:T(8,128)(2,1)}, bf16[2,2,8,48,768]{4,3,2,1,0:T(8,128)(2,1)}, bf16[2,8,96,768]{3,2,1,0:T(8,128)(2,1)}) custom-call(s32[2]{0:T(128)} %pad_add_fusion.idx_ref, bf16[512,768]{1,0:T(8,128)(2,1)} %get-tuple-element.122.hidden_ref.x_ref, bf16[512,768]{1,0:T(8,128)(2,1)} %c_ref.7, ...), custom_call_target="tpu_custom_call" | custom-call | flops 2415919104 | bytes 11796480 | tf_op jit(solution)/shard_map/up/pallas_call | solution.py:404
  100.1 1.6 collective-permute-start.27
  102.7 9.2 %up.3 = (bf16[2,512,768]{2,1,0:T(8,128)(2,1)}, bf16[2,512,768]{2,1,0:T(8,128)(2,1)}, bf16[2,2,8,48,768]{4,3,2,1,0:T(8,128)(2,1)}, bf16[2,8,96,768]{3,2,1,0:T(8,128)(2,1)}) custom-call(s32[2]{0:T(128)} %pad_add_fusion.idx_ref, bf16[512,768]{1,0:T(8,128)(2,1)} %get-tuple-element.122.hidden_ref.x_ref, bf16[512,768]{1,0:T(8,128)(2,1)} %c_ref.7, ...), custom_call_target="tpu_custom_call" | custom-call | flops 48318382080 | bytes 11796480 | tf_op jit(solution)/shard_map/up/pallas_call | solution.py:404
  112.0 3.4 %collective-permute-done.27.p1 = bf16[8,48,768]{2,1,0:T(8,128)(2,1)S(1)} collective-permute-done((bf16[8,48,768]{2,1,0:T(8,128)(2,1)S(1)}, bf16[8,48,768]{2,1,0:T(8,128)(2,1)S(1)}, u32[]{:S(2)}, u32[]{:S(2)}) %collective-permute-start.27) | collective-permute-done | bytes 589856 | tf_op jit(solution)/shard_map/ppermute | solution.py:69
  115.4 1.4 collective-permute-done.28.p3
  117.3 1.5 slice_add_fusion.6
  121.4 9.8 %act_grad.2 = (f32[512,768]{1,0:T(8,128)}, f32[16,768]{1,0:T(8,128)}, bf16[2,2,8,48,768]{4,3,2,1,0:T(8,128)(2,1)}, bf16[2,8,96,768]{3,2,1,0:T(8,128)(2,1)}) custom-call(s32[2]{0:T(128)} %pad_add_fusion.idx_ref, bf16[512,768]{1,0:T(8,128)(2,1)} %c_ref.7, bf16[512,768]{1,0:T(8,128)(2,1)} %get-tuple-element.122.hidden_ref.x_ref, ...), custom_call_target="tpu_custom_call" | custom-call | flops 3623878656 | bytes 15728640 | tf_op jit(solution)/shard_map/act_grad/pallas_call | solution.py:487
  132.7 10.3 %act_grad.3 = (f32[512,768]{1,0:T(8,128)}, f32[16,768]{1,0:T(8,128)}, bf16[2,2,8,48,768]{4,3,2,1,0:T(8,128)(2,1)}, bf16[2,8,96,768]{3,2,1,0:T(8,128)(2,1)}) custom-call(s32[2]{0:T(128)} %pad_add_fusion.idx_ref, bf16[512,768]{1,0:T(8,128)(2,1)} %c_ref.7, bf16[512,768]{1,0:T(8,128)(2,1)} %get-tuple-element.122.hidden_ref.x_ref, ...), custom_call_target="tpu_custom_call" | custom-call | flops 48318382080 | bytes 15728640 | tf_op jit(solution)/shard_map/act_grad/pallas_call | solution.py:487
  143.0 3.9 %collective-permute-done.35 = bf16[8,48,768]{2,1,0:T(8,128)(2,1)S(1)} collective-permute-done((bf16[8,48,768]{2,1,0:T(8,128)(2,1)S(1)}, bf16[8,48,768]{2,1,0:T(8,128)(2,1)S(1)}, u32[]{:S(2)}, u32[]{:S(2)}) %collective-permute-start.35) | collective-permute-done | bytes 589856 | tf_op jit(solution)/shard_map/ppermute | solution.py:69
  149.6 1.6 collective-permute-start.33
  153.1 4.9 %middle.1 = (f32[512,768]{1,0:T(8,128)}, bf16[512,768]{1,0:T(8,128)(2,1)}, bf16[512,768]{1,0:T(8,128)(2,1)}, f32[16,768]{1,0:T(8,128)}) custom-call(bf16[512,768]{1,0:T(8,128)(2,1)} %c_ref.7, f32[512,768]{1,0:T(8,128)} %get-tuple-element.144.hidden_ref, f32[512,768]{1,0:T(8,128)} %get-tuple-element.163.residual_ref, f32[16,768]{1,0:T(8,128)} %convert_add_fusion.4.small_ref, ...), custom_call_target="tpu_custom_call" | custom-call | flops 603979776 | bytes 8257536 | tf_op jit(solution)/shard_map/middle/pallas_call | solution.py:582
  158.1 11.6 %attend_back.1.three_ref = bf16[3,512,768]{2,1,0:T(8,128)(2,1)} custom-call(bf16[3,512,768]{2,1,0:T(8,128)(2,1)} %get-tuple-element.110.q_ref.k_ref.v_ref, bf16[3,512,768]{2,1,0:T(8,128)(2,1)} %get-tuple-element.110.q_ref.k_ref.v_ref, bf16[3,512,768]{2,1,0:T(8,128)(2,1)} %get-tuple-element.110.q_ref.k_ref.v_ref, ...), custom_call_target="tpu_custom_call" | custom-call | flops 3221225472 | bytes 12582912 | tf_op jit(solution)/shard_map/attend_back/pallas_call | solution.py:304
  170.9 1.6 collective-permute-start.38
  172.5 5.4 %first_grad.2 = bf16[2,2,8,48,768]{4,3,2,1,0:T(8,128)(2,1)} custom-call(s32[2]{0:T(128)} %pad_add_fusion.idx_ref, bf16[512,768]{1,0:T(8,128)(2,1)} %get-tuple-element.155.normed_ref, bf16[512,768]{1,0:T(8,128)(2,1)} %get-tuple-element.113.mixed_ref, bf16[3,512,768]{2,1,0:T(8,128)(2,1)} %attend_back.1.three_ref, bf16[512,768]{1,0:T(8,128)(2,1)} %get-tuple-element.150.branch_ref), custom_call_target="tpu_custom_call" | custom-call | flops 1207959552 | bytes 6291456 | tf_op jit(solution)/shard_map/first_grad/pallas_call | solution.py:540
  179.3 5.4 %first_grad.3 = bf16[2,2,8,48,768]{4,3,2,1,0:T(8,128)(2,1)} custom-call(s32[2]{0:T(128)} %pad_add_fusion.idx_ref, bf16[512,768]{1,0:T(8,128)(2,1)} %get-tuple-element.155.normed_ref, bf16[512,768]{1,0:T(8,128)(2,1)} %get-tuple-element.113.mixed_ref, bf16[3,512,768]{2,1,0:T(8,128)(2,1)} %attend_back.1.three_ref, bf16[512,768]{1,0:T(8,128)(2,1)} %get-tuple-element.150.branch_ref), custom_call_target="tpu_custom_call" | custom-call | flops 48318382080 | bytes 6291456 | tf_op jit(solution)/shard_map/first_grad/pallas_call | solution.py:540
  184.7 1.5 slice_add_fusion.1
  186.9 7.2 %collective-permute-done.41 = bf16[2,2,2,48,768]{4,3,0,2,1:T(8,128)(2,1)S(1)} collective-permute-done((bf16[2,2,2,48,768]{4,3,0,2,1:T(8,128)(2,1)S(1)}, bf16[2,2,2,48,768]{4,3,0,2,1:T(8,128)(2,1)S(1)}, u32[]{:S(2)}, u32[]{:S(2)}) %collective-permute-start.41) | collective-permute-done | bytes 589856 | tf_op jit(solution)/shard_map/ppermute | solution.py:69
  194.5 15.6 %collective-permute-done.43 = bf16[1,2,2,48,768]{4,3,0,2,1:T(8,128)(2,1)S(1)} collective-permute-done((bf16[1,2,2,48,768]{4,3,0,2,1:T(8,128)(2,1)S(1)}, bf16[1,2,2,48,768]{4,3,0,2,1:T(8,128)(2,1)S(1)}, u32[]{:S(2)}, u32[]{:S(2)}) %collective-permute-start.43) | collective-permute-done | bytes 294944 | tf_op jit(solution)/shard_map/ppermute | solution.py:69
  210.1 8.1 %input_grads.1 = (f32[512,768]{1,0:T(8,128)}, f32[16,768]{1,0:T(8,128)}) custom-call(bf16[512,768]{1,0:T(8,128)(2,1)} %x_ref.3, bf16[3,512,768]{2,1,0:T(8,128)(2,1)} %attend_back.1.three_ref, bf16[4,768,768]{2,1,0:T(8,128)(2,1)} %bitcast.183, f32[16,768]{1,0:T(8,128)} %convert_add_fusion.4.small_ref, f32[512,768]{1,0:T(8,128)} %get-tuple-element.158.grad_ref), custom_call_target="tpu_custom_call" | custom-call | flops 1811939328 | bytes 9830400 | tf_op jit(solution)/shard_map/input_grads/pallas_call | solution.py:634
  220.4 1.8 collective-permute-start.47
  222.2 13.3 %collective-permute-done.47 = bf16[16,768]{1,0:T(8,128)(2,1)S(1)} collective-permute-done((bf16[16,768]{1,0:T(8,128)(2,1)S(1)}, bf16[16,768]{1,0:T(8,128)(2,1)S(1)}, u32[]{:S(2)}, u32[]{:S(2)}) %collective-permute-start.47) | collective-permute-done | bytes 24608 | tf_op jit(solution)/shard_map/ppermute | solution.py:69
  235.5 4.7 %collective-permute-done.48 = bf16[16,768]{1,0:T(8,128)(2,1)S(1)} collective-permute-done((bf16[16,768]{1,0:T(8,128)(2,1)S(1)}, bf16[16,768]{1,0:T(8,128)(2,1)S(1)}, u32[]{:S(2)}, u32[]{:S(2)}) %collective-permute-start.48) | collective-permute-done | bytes 24608 | tf_op jit(solution)/shard_map/ppermute | solution.py:69
  245.1 1.7 collective-permute-start.59
  246.8 6.8 %down_out.1 = bf16[512,768]{1,0:T(8,128)(2,1)} custom-call(bf16[2,512,768]{2,1,0:T(8,128)(2,1)} %get-tuple-element.118.a0_ref, bf16[2,512,768]{2,1,0:T(8,128)(2,1)} %get-tuple-element.123.a1_ref, bf16[2,768,768]{2,1,0:T(8,128)(2,1)} %bitcast.184, bf16[2,768,768]{2,1,0:T(8,128)(2,1)} %bitcast.185, f32[16,768]{1,0:T(8,128)} %convert_add_fusion.4.small_ref, ...), custom_call_target="tpu_custom_call" | custom-call | flops 2415919104 | bytes 10223616 | tf_op jit(solution)/shard_map/down_out/pallas_call | solution.py:671
  253.8 2.1 collective-permute-start.53
  258.2 2.6 collective-permute-done.53
  263.1 3.9 %collective-permute-done.54 = bf16[1,2,48,768]{3,2,0,1:T(8,128)(2,1)S(1)} collective-permute-done((bf16[1,2,48,768]{3,2,0,1:T(8,128)(2,1)S(1)}, bf16[1,2,48,768]{3,2,0,1:T(8,128)(2,1)S(1)}, u32[]{:S(2)}, u32[]{:S(2)}) %collective-permute-start.54) | collective-permute-done | bytes 147488 | tf_op jit(solution)/shard_map/ppermute | solution.py:69
  267.0 2.2 collective-permute-start.56
  269.6 2.8 collective-permute-done.56
  273.4 2.6 reshape.362
  (249 shorter events, 52.9 us)
Async XLA Ops:
  1.8 11.1 %collective-permute-start = (bf16[1,96,768]{2,1,0:T(8,128)(2,1)S(1)}, bf16[1,96,768]{2,1,0:T(8,128)(2,1)S(1)}, u32[]{:S(2)}, u32[]{:S(2)}) collective-permute-start(bf16[1,96,768]{2,1,0:T(8,128)(2,1)S(1)} %bitcast.186), channel_id=1, source_target_pairs={{0,4},{1,5},{2,6},{3,7},{4,0},{5,1},{6,2},{7,3},{8,12},{9,13},{10,... | collective-permute-start | bytes 442376 | tf_op jit(solution)/shard_map/ppermute | solution.py:69
  12.9 8.2 %collective-permute-start.2 = (bf16[2,96,768]{2,1,0:T(8,128)(2,1)S(1)}, bf16[2,96,768]{2,1,0:T(8,128)(2,1)S(1)}, u32[]{:S(2)}, u32[]{:S(2)}) collective-permute-start(bf16[2,96,768]{2,1,0:T(8,128)(2,1)S(1)} %pad_maximum_fusion.10), channel_id=1, source_target_pairs={{0,2},{1,3},{2,0},{3,1},{4,6},{5,7},{6,4},{7,5},{8,10},{9,11},{10,... | collective-permute-start | bytes 884744 | tf_op jit(solution)/shard_map/ppermute | solution.py:69
  21.2 8.6 %collective-permute-start.4 = (bf16[4,48,768]{2,1,0:T(8,128)(2,1)S(1)}, bf16[4,48,768]{2,1,0:T(8,128)(2,1)}, u32[]{:S(2)}, u32[]{:S(2)}) collective-permute-start(bf16[4,48,768]{2,1,0:T(8,128)(2,1)S(1)} %pad_maximum_fusion.12), channel_id=1, source_target_pairs={{0,1},{1,0},{2,3},{3,2},{4,5},{5,4},{6,7},{7,6},{8,9},{9,8},{10,11... | collective-permute-start | bytes 884744 | tf_op jit(solution)/shard_map/ppermute | solution.py:69
  22.8 8.7 %collective-permute-start.6 = (bf16[4,48,768]{2,1,0:T(8,128)(2,1)S(1)}, bf16[4,48,768]{2,1,0:T(8,128)(2,1)S(1)}, u32[]{:S(2)}, u32[]{:S(2)}) collective-permute-start(bf16[4,48,768]{2,1,0:T(8,128)(2,1)S(1)} %pad_maximum_fusion.13), channel_id=1, source_target_pairs={{0,16},{8,24},{16,0},{24,8},{1,17},{9,25},{17,1},{25,9},{2,18},{10... | collective-permute-start | bytes 884744 | tf_op jit(solution)/shard_map/ppermute | solution.py:69
  26.6 10.4 %collective-permute-start.1 = (bf16[1,112,768]{2,1,0:T(8,128)(2,1)S(1)}, bf16[1,112,768]{2,1,0:T(8,128)(2,1)S(1)}, u32[]{:S(2)}, u32[]{:S(2)}) collective-permute-start(bf16[1,112,768]{2,1,0:T(8,128)(2,1)S(1)} %bitcast.191), channel_id=1, source_target_pairs={{0,4},{1,5},{2,6},{3,7},{4,0},{5,1},{6,2},{7,3},{8,12},{9,13},{10,... | collective-permute-start | bytes 516104 | tf_op jit(solution)/shard_map/ppermute | solution.py:69
  30.9 15.3 %collective-permute-start.5 = (bf16[8,48,768]{2,1,0:T(8,128)(2,1)S(1)}, bf16[8,48,768]{2,1,0:T(8,128)(2,1)}, u32[]{:S(2)}, u32[]{:S(2)}) collective-permute-start(bf16[8,48,768]{2,1,0:T(8,128)(2,1)S(1)} %pad_maximum_fusion.3.p0), channel_id=1, source_target_pairs={{0,16},{8,24},{16,0},{24,8},{1,17},{9,25},{17,1},{25,9},{2,18},{10... | collective-permute-start | bytes 1769480 | tf_op jit(solution)/shard_map/ppermute | solution.py:69
  31.6 14.6 %collective-permute-start.7 = (bf16[8,48,768]{2,1,0:T(8,128)(2,1)S(1)}, bf16[8,48,768]{2,1,0:T(8,128)(2,1)}, u32[]{:S(2)}, u32[]{:S(2)}) collective-permute-start(bf16[8,48,768]{2,1,0:T(8,128)(2,1)S(1)} %pad_maximum_fusion.4.p2), channel_id=1, source_target_pairs={{0,1},{1,0},{2,3},{3,2},{4,5},{5,4},{6,7},{7,6},{8,9},{9,8},{10,11... | collective-permute-start | bytes 1769480 | tf_op jit(solution)/shard_map/ppermute | solution.py:69
  37.0 9.1 %collective-permute-start.3 = (bf16[2,112,768]{2,1,0:T(8,128)(2,1)S(1)}, bf16[2,112,768]{2,1,0:T(8,128)(2,1)S(1)}, u32[]{:S(2)}, u32[]{:S(2)}) collective-permute-start(bf16[2,112,768]{2,1,0:T(8,128)(2,1)S(1)} %pad_maximum_fusion.11), channel_id=1, source_target_pairs={{0,2},{1,3},{2,0},{3,1},{4,6},{5,7},{6,4},{7,5},{8,10},{9,11},{10,... | collective-permute-start | bytes 1032200 | tf_op jit(solution)/shard_map/ppermute | solution.py:69
  38.4 9.1 %collective-permute-start.9 = (bf16[8,48,768]{2,1,0:T(8,128)(2,1)S(1)}, bf16[8,48,768]{2,1,0:T(8,128)(2,1)S(1)}, u32[]{:S(2)}, u32[]{:S(2)}) collective-permute-start(bf16[8,48,768]{2,1,0:T(8,128)(2,1)S(1)} %pad_maximum_fusion.3.p0), channel_id=1, source_target_pairs={{0,8},{8,0},{16,24},{24,16},{1,9},{9,1},{17,25},{25,17},{2,10},{10... | collective-permute-start | bytes 1769480 | tf_op jit(solution)/shard_map/ppermute | solution.py:69
  38.4 13.9 %collective-permute-start.11 = (bf16[8,48,768]{2,1,0:T(8,128)(2,1)S(1)}, bf16[8,48,768]{2,1,0:T(8,128)(2,1)S(1)}, u32[]{:S(2)}, u32[]{:S(2)}) collective-permute-start(bf16[8,48,768]{2,1,0:T(8,128)(2,1)S(1)} %pad_maximum_fusion.4.p2), channel_id=1, source_target_pairs={{0,8},{8,0},{16,24},{24,16},{1,9},{9,1},{17,25},{25,17},{2,10},{10... | collective-permute-start | bytes 1769480 | tf_op jit(solution)/shard_map/ppermute | solution.py:69
  46.2 8.8 %collective-permute-start.10 = (bf16[8,48,768]{2,1,0:T(8,128)(2,1)}, bf16[8,48,768]{2,1,0:T(8,128)(2,1)S(1)}, u32[]{:S(2)}, u32[]{:S(2)}) collective-permute-start(bf16[8,48,768]{2,1,0:T(8,128)(2,1)} %collective-permute-done.5.p1), channel_id=1, source_target_pairs={{0,8},{8,0},{16,24},{24,16},{1,9},{9,1},{17,25},{25,17},{2,10},{10... | collective-permute-start | bytes 1769480 | tf_op jit(solution)/shard_map/ppermute | solution.py:69
  46.3 8.7 %collective-permute-start.12 = (bf16[8,48,768]{2,1,0:T(8,128)(2,1)}, bf16[8,48,768]{2,1,0:T(8,128)(2,1)S(1)}, u32[]{:S(2)}, u32[]{:S(2)}) collective-permute-start(bf16[8,48,768]{2,1,0:T(8,128)(2,1)} %collective-permute-done.7.p3), channel_id=1, source_target_pairs={{0,8},{8,0},{16,24},{24,16},{1,9},{9,1},{17,25},{25,17},{2,10},{10... | collective-permute-start | bytes 1769480 | tf_op jit(solution)/shard_map/ppermute | solution.py:69
  47.5 18.0 %collective-permute-start.13 = (bf16[4,48,768]{2,1,0:T(8,128)(2,1)S(1)}, bf16[4,48,768]{2,1,0:T(8,128)(2,1)S(1)}, u32[]{:S(2)}, u32[]{:S(2)}) collective-permute-start(bf16[4,48,768]{2,1,0:T(8,128)(2,1)S(1)} %pad_maximum_fusion.14), channel_id=1, source_target_pairs={{0,1},{1,0},{2,3},{3,2},{4,5},{5,4},{6,7},{7,6},{8,9},{9,8},{10,11... | collective-permute-start | bytes 884744 | tf_op jit(solution)/shard_map/ppermute | solution.py:69
  51.0 14.5 %collective-permute-start.14 = (bf16[4,48,768]{2,1,0:T(8,128)(2,1)S(1)}, bf16[4,48,768]{2,1,0:T(8,128)(2,1)S(1)}, u32[]{:S(2)}, u32[]{:S(2)}) collective-permute-start(bf16[4,48,768]{2,1,0:T(8,128)(2,1)S(1)} %pad_maximum_fusion.15), channel_id=1, source_target_pairs={{0,16},{8,24},{16,0},{24,8},{1,17},{9,25},{17,1},{25,9},{2,18},{10... | collective-permute-start | bytes 884744 | tf_op jit(solution)/shard_map/ppermute | solution.py:69
  52.2 13.2 %collective-permute-start.15 = (bf16[1,96,768]{2,1,0:T(8,128)(2,1)S(1)}, bf16[1,96,768]{2,1,0:T(8,128)(2,1)S(1)}, u32[]{:S(2)}, u32[]{:S(2)}) collective-permute-start(bf16[1,96,768]{2,1,0:T(8,128)(2,1)S(1)} %dynamic-slice_bitcast_fusion), channel_id=1, source_target_pairs={{0,4},{1,5},{2,6},{3,7},{4,0},{5,1},{6,2},{7,3},{8,12},{9,13},{10,... | collective-permute-start | bytes 442376 | tf_op jit(solution)/shard_map/ppermute | solution.py:69
  65.6 17.3 %collective-permute-start.16 = (bf16[8,48,768]{2,1,0:T(8,128)(2,1)S(1)}, bf16[8,48,768]{2,1,0:T(8,128)(2,1)S(1)}, u32[]{:S(2)}, u32[]{:S(2)}) collective-permute-start(bf16[8,48,768]{2,1,0:T(8,128)(2,1)S(1)} %pad_maximum_fusion.5.p0), channel_id=1, source_target_pairs={{0,16},{8,24},{16,0},{24,8},{1,17},{9,25},{17,1},{25,9},{2,18},{10... | collective-permute-start | bytes 1769480 | tf_op jit(solution)/shard_map/ppermute | solution.py:69
  67.3 15.7 %collective-permute-start.17 = (bf16[8,48,768]{2,1,0:T(8,128)(2,1)S(1)}, bf16[8,48,768]{2,1,0:T(8,128)(2,1)S(1)}, u32[]{:S(2)}, u32[]{:S(2)}) collective-permute-start(bf16[8,48,768]{2,1,0:T(8,128)(2,1)S(1)} %pad_maximum_fusion.6.p2), channel_id=1, source_target_pairs={{0,1},{1,0},{2,3},{3,2},{4,5},{5,4},{6,7},{7,6},{8,9},{9,8},{10,11... | collective-permute-start | bytes 1769480 | tf_op jit(solution)/shard_map/ppermute | solution.py:69
  69.1 13.8 %collective-permute-start.18 = (bf16[2,96,768]{2,1,0:T(8,128)(2,1)S(1)}, bf16[2,96,768]{2,1,0:T(8,128)(2,1)S(1)}, u32[]{:S(2)}, u32[]{:S(2)}) collective-permute-start(bf16[2,96,768]{2,1,0:T(8,128)(2,1)S(1)} %constant_dynamic-update-slice_fusion), channel_id=1, source_target_pairs={{0,2},{1,3},{2,0},{3,1},{4,6},{5,7},{6,4},{7,5},{8,10},{9,11},{10,... | collective-permute-start | bytes 884744 | tf_op jit(solution)/shard_map/ppermute | solution.py:69
  72.0 12.8 %collective-permute-start.19 = (bf16[8,48,768]{2,1,0:T(8,128)(2,1)S(1)}, bf16[8,48,768]{2,1,0:T(8,128)(2,1)S(1)}, u32[]{:S(2)}, u32[]{:S(2)}) collective-permute-start(bf16[8,48,768]{2,1,0:T(8,128)(2,1)S(1)} %pad_maximum_fusion.5.p0), channel_id=1, source_target_pairs={{0,8},{8,0},{16,24},{24,16},{1,9},{9,1},{17,25},{25,17},{2,10},{10... | collective-permute-start | bytes 1769480 | tf_op jit(solution)/shard_map/ppermute | solution.py:69
  72.0 17.1 %collective-permute-start.21 = (bf16[8,48,768]{2,1,0:T(8,128)(2,1)S(1)}, bf16[8,48,768]{2,1,0:T(8,128)(2,1)S(1)}, u32[]{:S(2)}, u32[]{:S(2)}) collective-permute-start(bf16[8,48,768]{2,1,0:T(8,128)(2,1)S(1)} %pad_maximum_fusion.6.p2), channel_id=1, source_target_pairs={{0,8},{8,0},{16,24},{24,16},{1,9},{9,1},{17,25},{25,17},{2,10},{10... | collective-permute-start | bytes 1769480 | tf_op jit(solution)/shard_map/ppermute | solution.py:69
  83.7 15.8 %collective-permute-start.23 = (bf16[4,48,768]{2,1,0:T(8,128)(2,1)S(1)}, bf16[4,48,768]{2,1,0:T(8,128)(2,1)S(1)}, u32[]{:S(2)}, u32[]{:S(2)}) collective-permute-start(bf16[4,48,768]{2,1,0:T(8,128)(2,1)S(1)} %pad_maximum_fusion.16), channel_id=1, source_target_pairs={{0,1},{1,0},{2,3},{3,2},{4,5},{5,4},{6,7},{7,6},{8,9},{9,8},{10,11... | collective-permute-start | bytes 884744 | tf_op jit(solution)/shard_map/ppermute | solution.py:69
  84.8 14.6 %collective-permute-start.24 = (bf16[4,48,768]{2,1,0:T(8,128)(2,1)S(1)}, bf16[4,48,768]{2,1,0:T(8,128)(2,1)S(1)}, u32[]{:S(2)}, u32[]{:S(2)}) collective-permute-start(bf16[4,48,768]{2,1,0:T(8,128)(2,1)S(1)} %pad_maximum_fusion.17), channel_id=1, source_target_pairs={{0,16},{8,24},{16,0},{24,8},{1,17},{9,25},{17,1},{25,9},{2,18},{10... | collective-permute-start | bytes 884744 | tf_op jit(solution)/shard_map/ppermute | solution.py:69
  99.3 18.0 %collective-permute-start.25 = (bf16[2,2,8,48,768]{4,3,2,1,0:T(8,128)(2,1)}, bf16[2,2,8,48,768]{4,3,2,1,0:T(8,128)(2,1)S(1)}, u32[]{:S(2)}, u32[]{:S(2)}) collective-permute-start(bf16[2,2,8,48,768]{4,3,2,1,0:T(8,128)(2,1)} %get-tuple-element.119), channel_id=1, source_target_pairs={{0,8},{8,0},{16,24},{24,16},{1,9},{9,1},{17,25},{25,17},{2,10},{10... | collective-permute-start | bytes 7077896 | tf_op jit(solution)/shard_map/ppermute | solution.py:69
  99.5 20.0 %collective-permute-start.26 = (bf16[8,48,768]{2,1,0:T(8,128)(2,1)S(1)}, bf16[8,48,768]{2,1,0:T(8,128)(2,1)S(1)}, u32[]{:S(2)}, u32[]{:S(2)}) collective-permute-start(bf16[8,48,768]{2,1,0:T(8,128)(2,1)S(1)} %pad_maximum_fusion.7.p0), channel_id=1, source_target_pairs={{0,8},{8,0},{16,24},{24,16},{1,9},{9,1},{17,25},{25,17},{2,10},{10... | collective-permute-start | bytes 1769480 | tf_op jit(solution)/shard_map/ppermute | solution.py:69
  100.1 15.3 %collective-permute-start.27 = (bf16[8,48,768]{2,1,0:T(8,128)(2,1)S(1)}, bf16[8,48,768]{2,1,0:T(8,128)(2,1)S(1)}, u32[]{:S(2)}, u32[]{:S(2)}) collective-permute-start(bf16[8,48,768]{2,1,0:T(8,128)(2,1)S(1)} %pad_maximum_fusion.7.p0), channel_id=1, source_target_pairs={{0,16},{8,24},{16,0},{24,8},{1,17},{9,25},{17,1},{25,9},{2,18},{10... | collective-permute-start | bytes 1769480 | tf_op jit(solution)/shard_map/ppermute | solution.py:69
  101.7 15.1 %collective-permute-start.28 = (bf16[8,48,768]{2,1,0:T(8,128)(2,1)S(1)}, bf16[8,48,768]{2,1,0:T(8,128)(2,1)S(1)}, u32[]{:S(2)}, u32[]{:S(2)}) collective-permute-start(bf16[8,48,768]{2,1,0:T(8,128)(2,1)S(1)} %pad_maximum_fusion.8.p2), channel_id=1, source_target_pairs={{0,1},{1,0},{2,3},{3,2},{4,5},{5,4},{6,7},{7,6},{8,9},{9,8},{10,11... | collective-permute-start | bytes 1769480 | tf_op jit(solution)/shard_map/ppermute | solution.py:69
  102.7 16.8 %collective-permute-start.30 = (bf16[8,48,768]{2,1,0:T(8,128)(2,1)S(1)}, bf16[8,48,768]{2,1,0:T(8,128)(2,1)S(1)}, u32[]{:S(2)}, u32[]{:S(2)}) collective-permute-start(bf16[8,48,768]{2,1,0:T(8,128)(2,1)S(1)} %pad_maximum_fusion.8.p2), channel_id=1, source_target_pairs={{0,8},{8,0},{16,24},{24,16},{1,9},{9,1},{17,25},{25,17},{2,10},{10... | collective-permute-start | bytes 1769480 | tf_op jit(solution)/shard_map/ppermute | solution.py:69
  131.2 17.1 %collective-permute-start.32 = (bf16[2,2,8,48,768]{4,3,2,1,0:T(8,128)(2,1)}, bf16[2,2,8,48,768]{4,3,2,1,0:T(8,128)(2,1)S(1)}, u32[]{:S(2)}, u32[]{:S(2)}) collective-permute-start(bf16[2,2,8,48,768]{4,3,2,1,0:T(8,128)(2,1)} %get-tuple-element.131), channel_id=1, source_target_pairs={{0,8},{8,0},{16,24},{24,16},{1,9},{9,1},{17,25},{25,17},{2,10},{10... | collective-permute-start | bytes 7077896 | tf_op jit(solution)/shard_map/ppermute | solution.py:69
  131.3 15.7 %collective-permute-start.35 = (bf16[8,48,768]{2,1,0:T(8,128)(2,1)S(1)}, bf16[8,48,768]{2,1,0:T(8,128)(2,1)S(1)}, u32[]{:S(2)}, u32[]{:S(2)}) collective-permute-start(bf16[8,48,768]{2,1,0:T(8,128)(2,1)S(1)} %get-tuple-element.192), channel_id=1, source_target_pairs={{0,16},{8,24},{16,0},{24,8},{1,17},{9,25},{17,1},{25,9},{2,18},{10... | collective-permute-start | bytes 1769480 | tf_op jit(solution)/shard_map/ppermute | solution.py:69
  131.8 15.4 %collective-permute-start.36 = (bf16[2,4,48,768]{3,2,1,0:T(8,128)(2,1)S(1)}, bf16[2,4,48,768]{3,2,1,0:T(8,128)(2,1)S(1)}, u32[]{:S(2)}, u32[]{:S(2)}) collective-permute-start(bf16[2,4,48,768]{3,2,1,0:T(8,128)(2,1)S(1)} %get-tuple-element.190), channel_id=1, source_target_pairs={{0,1},{1,0},{2,3},{3,2},{4,5},{5,4},{6,7},{7,6},{8,9},{9,8},{10,11... | collective-permute-start | bytes 1769480 | tf_op jit(solution)/shard_map/ppermute | solution.py:69
  147.2 30.7 %collective-permute-start.39 = (bf16[4,48,768]{2,1,0:T(8,128)(2,1)S(1)}, bf16[4,48,768]{2,1,0:T(8,128)(2,1)S(1)}, u32[]{:S(2)}, u32[]{:S(2)}) collective-permute-start(bf16[4,48,768]{2,1,0:T(8,128)(2,1)S(1)} %get-tuple-element.208), channel_id=1, source_target_pairs={{0,1},{1,0},{2,3},{3,2},{4,5},{5,4},{6,7},{7,6},{8,9},{9,8},{10,11... | collective-permute-start | bytes 884744 | tf_op jit(solution)/shard_map/ppermute | solution.py:69
  149.6 20.1 %collective-permute-start.33 = (bf16[8,48,768]{2,1,0:T(8,128)(2,1)S(1)}, bf16[8,48,768]{2,1,0:T(8,128)(2,1)S(1)}, u32[]{:S(2)}, u32[]{:S(2)}) collective-permute-start(bf16[8,48,768]{2,1,0:T(8,128)(2,1)S(1)} %get-tuple-element.188), channel_id=1, source_target_pairs={{0,16},{8,24},{16,0},{24,8},{1,17},{9,25},{17,1},{25,9},{2,18},{10... | collective-permute-start | bytes 1769480 | tf_op jit(solution)/shard_map/ppermute | solution.py:69
  151.4 18.3 %collective-permute-start.34 = (bf16[2,4,48,768]{3,2,1,0:T(8,128)(2,1)S(1)}, bf16[2,4,48,768]{3,2,1,0:T(8,128)(2,1)S(1)}, u32[]{:S(2)}, u32[]{:S(2)}) collective-permute-start(bf16[2,4,48,768]{3,2,1,0:T(8,128)(2,1)S(1)} %get-tuple-element.193), channel_id=1, source_target_pairs={{0,1},{1,0},{2,3},{3,2},{4,5},{5,4},{6,7},{7,6},{8,9},{9,8},{10,11... | collective-permute-start | bytes 1769480 | tf_op jit(solution)/shard_map/ppermute | solution.py:69
  152.6 25.3 %collective-permute-start.40 = (bf16[4,48,768]{2,1,0:T(8,128)(2,1)S(1)}, bf16[4,48,768]{2,1,0:T(8,128)(2,1)S(1)}, u32[]{:S(2)}, u32[]{:S(2)}) collective-permute-start(bf16[4,48,768]{2,1,0:T(8,128)(2,1)S(1)} %get-tuple-element.206), channel_id=1, source_target_pairs={{0,16},{8,24},{16,0},{24,8},{1,17},{9,25},{17,1},{25,9},{2,18},{10... | collective-permute-start | bytes 884744 | tf_op jit(solution)/shard_map/ppermute | solution.py:69
  169.8 8.3 %collective-permute-start.37 = (bf16[4,48,768]{2,1,0:T(8,128)(2,1)S(1)}, bf16[4,48,768]{2,1,0:T(8,128)(2,1)S(1)}, u32[]{:S(2)}, u32[]{:S(2)}) collective-permute-start(bf16[4,48,768]{2,1,0:T(8,128)(2,1)S(1)} %get-tuple-element.202), channel_id=1, source_target_pairs={{0,1},{1,0},{2,3},{3,2},{4,5},{5,4},{6,7},{7,6},{8,9},{9,8},{10,11... | collective-permute-start | bytes 884744 | tf_op jit(solution)/shard_map/ppermute | solution.py:69
  170.9 7.3 %collective-permute-start.38 = (bf16[4,48,768]{2,1,0:T(8,128)(2,1)S(1)}, bf16[4,48,768]{2,1,0:T(8,128)(2,1)S(1)}, u32[]{:S(2)}, u32[]{:S(2)}) collective-permute-start(bf16[4,48,768]{2,1,0:T(8,128)(2,1)S(1)} %get-tuple-element.203), channel_id=1, source_target_pairs={{0,16},{8,24},{16,0},{24,8},{1,17},{9,25},{17,1},{25,9},{2,18},{10... | collective-permute-start | bytes 884744 | tf_op jit(solution)/shard_map/ppermute | solution.py:69
  177.9 6.8 %collective-permute-start.42 = (bf16[2,2,8,48,768]{4,3,2,1,0:T(8,128)(2,1)}, bf16[2,2,8,48,768]{4,3,2,1,0:T(8,128)(2,1)S(1)}, u32[]{:S(2)}, u32[]{:S(2)}) collective-permute-start(bf16[2,2,8,48,768]{4,3,2,1,0:T(8,128)(2,1)} %first_grad.2), channel_id=1, source_target_pairs={{0,8},{8,0},{16,24},{24,16},{1,9},{9,1},{17,25},{25,17},{2,10},{10... | collective-permute-start | bytes 7077896 | tf_op jit(solution)/shard_map/ppermute | solution.py:69
  178.3 15.8 %collective-permute-start.41 = (bf16[2,2,2,48,768]{4,3,0,2,1:T(8,128)(2,1)S(1)}, bf16[2,2,2,48,768]{4,3,0,2,1:T(8,128)(2,1)S(1)}, u32[]{:S(2)}, u32[]{:S(2)}) collective-permute-start(bf16[2,2,2,48,768]{4,3,0,2,1:T(8,128)(2,1)S(1)} %fusion.5), channel_id=1, source_target_pairs={{0,2},{1,3},{2,0},{3,1},{4,6},{5,7},{6,4},{7,5},{8,10},{9,11},{10,... | collective-permute-start | bytes 1769480 | tf_op jit(solution)/shard_map/ppermute | solution.py:69
  194.2 15.8 %collective-permute-start.43 = (bf16[1,2,2,48,768]{4,3,0,2,1:T(8,128)(2,1)S(1)}, bf16[1,2,2,48,768]{4,3,0,2,1:T(8,128)(2,1)S(1)}, u32[]{:S(2)}, u32[]{:S(2)}) collective-permute-start(bf16[1,2,2,48,768]{4,3,0,2,1:T(8,128)(2,1)S(1)} %slice.403), channel_id=1, source_target_pairs={{0,4},{1,5},{2,6},{3,7},{4,0},{5,1},{6,2},{7,3},{8,12},{9,13},{10,... | collective-permute-start | bytes 884744 | tf_op jit(solution)/shard_map/ppermute | solution.py:69
  219.2 21.2 %collective-permute-start.44 = (bf16[8,48,768]{2,1,0:T(8,128)(2,1)S(1)}, bf16[8,48,768]{2,1,0:T(8,128)(2,1)}, u32[]{:S(2)}, u32[]{:S(2)}) collective-permute-start(bf16[8,48,768]{2,1,0:T(8,128)(2,1)S(1)} %get-tuple-element.186), channel_id=1, source_target_pairs={{0,16},{8,24},{16,0},{24,8},{1,17},{9,25},{17,1},{25,9},{2,18},{10... | collective-permute-start | bytes 1769480 | tf_op jit(solution)/shard_map/ppermute | solution.py:69
  219.2 21.1 %collective-permute-start.45 = (bf16[2,4,48,768]{3,2,1,0:T(8,128)(2,1)S(1)}, bf16[2,4,48,768]{3,2,1,0:T(8,128)(2,1)}, u32[]{:S(2)}, u32[]{:S(2)}) collective-permute-start(bf16[2,4,48,768]{3,2,1,0:T(8,128)(2,1)S(1)} %get-tuple-element.184), channel_id=1, source_target_pairs={{0,1},{1,0},{2,3},{3,2},{4,5},{5,4},{6,7},{7,6},{8,9},{9,8},{10,11... | collective-permute-start | bytes 1769480 | tf_op jit(solution)/shard_map/ppermute | solution.py:69
  220.4 15.1 %collective-permute-start.47 = (bf16[16,768]{1,0:T(8,128)(2,1)S(1)}, bf16[16,768]{1,0:T(8,128)(2,1)S(1)}, u32[]{:S(2)}, u32[]{:S(2)}) collective-permute-start(bf16[16,768]{1,0:T(8,128)(2,1)S(1)} %fusion.38), channel_id=1, source_target_pairs={{0,16},{8,24},{16,0},{24,8},{1,17},{9,25},{17,1},{25,9},{2,18},{10... | collective-permute-start | bytes 73736 | tf_op jit(solution)/shard_map/ppermute | solution.py:69
  242.6 11.1 %collective-permute-start.51 = (bf16[4,48,768]{2,1,0:T(8,128)(2,1)S(1)}, bf16[4,48,768]{2,1,0:T(8,128)(2,1)S(1)}, u32[]{:S(2)}, u32[]{:S(2)}) collective-permute-start(bf16[4,48,768]{2,1,0:T(8,128)(2,1)S(1)} %get-tuple-element.200), channel_id=1, source_target_pairs={{0,1},{1,0},{2,3},{3,2},{4,5},{5,4},{6,7},{7,6},{8,9},{9,8},{10,11... | collective-permute-start | bytes 884744 | tf_op jit(solution)/shard_map/ppermute | solution.py:69
  243.5 10.2 %collective-permute-start.52 = (bf16[4,48,768]{2,1,0:T(8,128)(2,1)S(1)}, bf16[4,48,768]{2,1,0:T(8,128)(2,1)S(1)}, u32[]{:S(2)}, u32[]{:S(2)}) collective-permute-start(bf16[4,48,768]{2,1,0:T(8,128)(2,1)S(1)} %get-tuple-element.198), channel_id=1, source_target_pairs={{0,16},{8,24},{16,0},{24,8},{1,17},{9,25},{17,1},{25,9},{2,18},{10... | collective-permute-start | bytes 884744 | tf_op jit(solution)/shard_map/ppermute | solution.py:69
  244.2 11.7 %collective-permute-start.50 = (bf16[16,768]{1,0:T(8,128)(2,1)S(1)}, bf16[16,768]{1,0:T(8,128)(2,1)S(1)}, u32[]{:S(2)}, u32[]{:S(2)}) collective-permute-start(bf16[16,768]{1,0:T(8,128)(2,1)S(1)} %get-tuple-element.173), channel_id=1, source_target_pairs={{0,1},{1,0},{2,3},{3,2},{4,5},{5,4},{6,7},{7,6},{8,9},{9,8},{10,11... | collective-permute-start | bytes 73736 | tf_op jit(solution)/shard_map/ppermute | solution.py:69
  245.1 11.9 %collective-permute-start.59 = (bf16[2,2,48,768]{3,2,1,0:T(8,128)(2,1)S(1)}, bf16[2,2,48,768]{3,2,1,0:T(8,128)(2,1)S(1)}, u32[]{:S(2)}, u32[]{:S(2)}) collective-permute-start(bf16[2,2,48,768]{3,2,1,0:T(8,128)(2,1)S(1)} %bitcast.189), channel_id=1, source_target_pairs={{0,16},{8,24},{16,0},{24,8},{1,17},{9,25},{17,1},{25,9},{2,18},{10... | collective-permute-start | bytes 884744 | tf_op jit(solution)/shard_map/ppermute | solution.py:69
  253.8 6.9 %collective-permute-start.53 = (bf16[2,2,48,768]{3,2,0,1:T(8,128)(2,1)S(1)}, bf16[2,2,48,768]{3,2,0,1:T(8,128)(2,1)S(1)}, u32[]{:S(2)}, u32[]{:S(2)}) collective-permute-start(bf16[2,2,48,768]{3,2,0,1:T(8,128)(2,1)S(1)} %fusion.15), channel_id=1, source_target_pairs={{0,2},{1,3},{2,0},{3,1},{4,6},{5,7},{6,4},{7,5},{8,10},{9,11},{10,... | collective-permute-start | bytes 884744 | tf_op jit(solution)/shard_map/ppermute | solution.py:69
  269.5 7.7 %collective-permute-start.55 = (bf16[2,48,768]{2,1,0:T(8,128)(2,1)S(1)}, bf16[2,48,768]{2,1,0:T(8,128)(2,1)S(1)}, u32[]{:S(2)}, u32[]{:S(2)}) collective-permute-start(bf16[2,48,768]{2,1,0:T(8,128)(2,1)S(1)} %bitcast.198), channel_id=1, source_target_pairs={{0,8},{8,0},{16,24},{24,16},{1,9},{9,1},{17,25},{25,17},{2,10},{10... | collective-permute-start | bytes 442376 | tf_op jit(solution)/shard_map/ppermute | solution.py:69
  (43 other events, 278.7 us)
